TPU v7x, 32 devices: a 4x4x1 block of a 4x4x8 slice. The times are simulated.
32 devices in a mesh: part: 1 (over z), row: 4 (over y), col: 4 (over x), dep: 2 (over core).
Axes of the slice: x: 4, y: 4, z: 1, core: 2. Of those that a mesh axis runs over, the one named last changes fastest.
The devices are a block of a 4x4x8 slice.
Arguments:
- x_in: bfloat16 [8192, 4096], P(('part', 'row', 'col'), 'dep')
- ln_scale: float32 [4096], P('dep')
- ln_shift: float32 [4096], P('dep')
- w_up: bfloat16 [4096, 16384], P(('dep', 'row'), 'col')
- b_up: bfloat16 [16384], P('col')
- w_down: bfloat16 [16384, 4096], P(('col', 'row'), 'dep')
- b_down: bfloat16 [4096], P('dep')
- y_grad: bfloat16 [8192, 4096], P(('part', 'row', 'col'), 'dep')
Outputs:
- output 1: bfloat16 [8192, 4096], P(('part', 'row', 'col'), 'dep')
- output 2: bfloat16 [8192, 4096], P(('part', 'row', 'col'), 'dep')
- output 3: bfloat16 [4096, 16384], P(('part', 'dep', 'row'), 'col')
- output 4: float32 [16384], P(('part', 'col'))
- output 5: bfloat16 [16384, 4096], P(('part', 'col', 'row'), 'dep')
- output 6: float32 [4096], P(('part', 'dep'))
- output 7: float32 [4096], P(('part', 'dep'))
- output 8: float32 [4096], P(('part', 'dep'))
All inputs are finite; a program needn't handle non-finite values.
Results may differ from a plain program's by a relative error of at most 0.00166166.
Values are sent between devices in bfloat16 or wider.
A program may use at most 768 MiB of HBM per device.

v0:
```python
import jax
import jax.numpy as jnp
from jax import lax
from jax.sharding import PartitionSpec as P

LN_EPS = 1e-5
GELU_K = 0.7978845608028654
GELU_C = 0.044715


def gelu_tanh(pre_act):
    inner_arg = GELU_K * (pre_act + GELU_C * pre_act * (pre_act * pre_act))
    return 0.5 * pre_act * (1.0 + jnp.tanh(inner_arg))


def gelu_slope(pre_act):
    squared = pre_act * pre_act
    tanh_val = jnp.tanh(GELU_K * (pre_act + GELU_C * pre_act * squared))
    return 0.5 * (1.0 + tanh_val) + 0.5 * pre_act * (1.0 - tanh_val * tanh_val) * GELU_K * (1.0 + 3.0 * GELU_C * squared)


def solution(mesh):
    dep_size = mesh.shape["dep"]
    tok_spec = P(("part", "row", "col"), "dep")
    vec_dep = P("dep")
    part_dep = P(("part", "dep"))
    in_specs = (tok_spec, vec_dep, vec_dep, P(("dep", "row"), "col"), P("col"), P(("col", "row"), "dep"), vec_dep, tok_spec)
    out_specs = (tok_spec, tok_spec, P(("part", "dep", "row"), "col"), P(("part", "col")), P(("part", "col", "row"), "dep"), part_dep, part_dep, part_dep)

    def local_step(x_in, ln_scale, ln_shift, w_up, b_up, w_down, b_down, y_grad):
        row_width = x_in.shape[1] * dep_size
        x_float = x_in.astype(jnp.float32)
        row_stats = jnp.stack([jnp.sum(x_float, axis=1), jnp.sum(x_float * x_float, axis=1)], axis=1)
        row_stats = lax.psum(row_stats, "dep")
        mean_row = row_stats[:, 0:1] / row_width
        var_row = row_stats[:, 1:2] / row_width - mean_row * mean_row
        inv_std = lax.rsqrt(var_row + LN_EPS)
        x_hat = (x_float - mean_row) * inv_std
        normed = (x_hat * ln_scale + ln_shift).astype(jnp.bfloat16)
        normed_full = lax.all_gather(normed, "col", axis=0, tiled=True)
        w_up_full = lax.all_gather(w_up, "row", axis=0, tiled=True)
        pre_part = jnp.dot(normed_full, w_up_full, preferred_element_type=jnp.float32)
        pre_act = lax.psum_scatter(pre_part, "dep", scatter_dimension=0, tiled=True) + b_up.astype(jnp.float32)
        hidden = gelu_tanh(pre_act).astype(jnp.bfloat16)
        hidden_full = lax.all_gather(hidden, "dep", axis=0, tiled=True)
        w_down_full = lax.all_gather(w_down, "row", axis=0, tiled=True)
        out_part = jnp.dot(hidden_full, w_down_full, preferred_element_type=jnp.float32)
        out_sum = lax.psum_scatter(out_part, "col", scatter_dimension=0, tiled=True)
        y_out = (x_float + out_sum + b_down.astype(jnp.float32)).astype(jnp.bfloat16)

        g_float = y_grad.astype(jnp.float32)
        grad_full = lax.all_gather(y_grad, "col", axis=0, tiled=True)
        b_down_grad = lax.psum(jnp.sum(g_float, axis=0), ("row", "col"))
        w_down_part = jnp.einsum("tf,td->fd", hidden_full, grad_full, preferred_element_type=jnp.float32)
        w_down_grad = lax.psum_scatter(w_down_part, "row", scatter_dimension=0, tiled=True).astype(jnp.bfloat16)
        hid_part = jnp.einsum("td,fd->tf", grad_full, w_down_full, preferred_element_type=jnp.float32)
        hid_grad = lax.psum_scatter(hid_part, "dep", scatter_dimension=0, tiled=True)
        pre_grad = hid_grad * gelu_slope(pre_act)
        b_up_grad = lax.psum(jnp.sum(pre_grad, axis=0), ("row", "dep"))
        pre_lowp = pre_grad.astype(jnp.bfloat16)
        pre_full = lax.all_gather(pre_lowp, "dep", axis=0, tiled=True)
        w_up_part = jnp.einsum("td,tf->df", normed_full, pre_full, preferred_element_type=jnp.float32)
        w_up_grad = lax.psum_scatter(w_up_part, "row", scatter_dimension=0, tiled=True).astype(jnp.bfloat16)
        norm_part = jnp.einsum("tf,df->td", pre_full, w_up_full, preferred_element_type=jnp.float32)
        norm_grad = lax.psum_scatter(norm_part, "col", scatter_dimension=0, tiled=True)
        value_a9 = norm_grad * ln_scale
        grad_stats = jnp.stack([jnp.sum(value_a9, axis=1), jnp.sum(value_a9 * x_hat, axis=1)], axis=1)
        grad_stats = lax.psum(grad_stats, "dep")
        x_grad = (g_float + inv_std * (value_a9 - grad_stats[:, 0:1] / row_width - x_hat * (grad_stats[:, 1:2] / row_width))).astype(jnp.bfloat16)
        gain_sums = lax.psum(jnp.stack([jnp.sum(norm_grad * x_hat, axis=0), jnp.sum(norm_grad, axis=0)]), ("row", "col"))
        return (y_out, x_grad, w_up_grad, b_up_grad, w_down_grad, b_down_grad, gain_sums[0], gain_sums[1])

    return jax.shard_map(local_step, mesh=mesh, in_specs=in_specs, out_specs=out_specs, check_vma=False)
```

profile of v0, /device:TPU:97, one launch (start us, length us, event | category | flops | bytes accessed | tf_op | source)
XLA Modules:
  0.0 1555.1 jit_solution(15612823690881889490)
XLA Ops:
  7.2 2.3 convert_reduce_fusion
  9.6 4.2 psum.35
  14.4 3.8 fusion.8
  18.3 0.7 all-gather.9.cloned.1.call-update
  19.1 0.7 all-gather.15.cloned.1.call-update
  20.5 80.6 %all-gather.7.cloned.1.call-done = bf16[2048,2048]{1,0:T(8,128)(2,1)} async-done(((bf16[512,2048]{1,0:T(8,128)(2,1)}), bf16[2048,2048]{1,0:T(8,128)(2,1)}) %all-gather.7.cloned.1.call-update) | async-done | bytes 8388624 | tf_op jit(solution)/shard_map/all_gather | solution.py:40
  101.1 154.9 %all-gather.9.cloned.1.call-done = bf16[2048,4096]{1,0:T(8,128)(2,1)} async-done(((bf16[512,4096]{1,0:T(8,128)(2,1)}), bf16[2048,4096]{1,0:T(8,128)(2,1)}) %all-gather.9.cloned.1.call-update) | async-done | bytes 16777232 | tf_op jit(solution)/shard_map/all_gather | solution.py:41
  256.0 43.5 %fusion.18 = f32[2048,4096]{1,0:T(8,128)} fusion(bf16[2048,2048]{1,0:T(8,128)(2,1)} %all-gather.7.cloned.1.call-done, bf16[2048,4096]{1,0:T(8,128)(2,1)} %all-gather.9.cloned.1.call-done), kind=kOutput, calls=%fused_computation.36 | convolution fusion | flops 34359738368 | bytes 58720256 | tf_op jit(solution)/shard_map/dot_general | solution.py:42
  299.8 39.5 %all-gather.15.cloned.1.call-done = bf16[2048,2048]{1,0:T(8,128)(2,1)} async-done(((bf16[512,2048]{1,0:T(8,128)(2,1)}), bf16[2048,2048]{1,0:T(8,128)(2,1)}) %all-gather.15.cloned.1.call-update) | async-done | bytes 8388624 | tf_op jit(solution)/shard_map/all_gather | solution.py:52
  339.3 154.7 %all-gather.13.cloned.1.call-done = bf16[4096,2048]{1,0:T(8,128)(2,1)} async-done(((bf16[1024,2048]{1,0:T(8,128)(2,1)}), bf16[4096,2048]{1,0:T(8,128)(2,1)}) %all-gather.13.cloned.1.call-update) | async-done | bytes 16777232 | tf_op jit(solution)/shard_map/all_gather | solution.py:46
  494.0 43.6 %fusion.20 = f32[2048,4096]{1,0:T(8,128)} fusion(bf16[2048,2048]{1,0:T(8,128)(2,1)} %all-gather.15.cloned.1.call-done, bf16[4096,2048]{1,0:T(8,128)(2,1)} %all-gather.13.cloned.1.call-done), kind=kOutput, calls=%fused_computation.38 | convolution fusion | flops 34359738368 | bytes 58720256 | tf_op jit(solution)/shard_map/td,fd->tf/dot_general | solution.py:56
  538.3 1.4 reduce-scatter.7.cloned.1.call-done
  539.8 45.6 %reduce-scatter.11.cloned.1.call-done = f32[1024,4096]{1,0:T(8,128)} async-done(((f32[2048,4096]{1,0:T(8,128)}), f32[1024,4096]{1,0:T(8,128)}) %reduce-scatter.11.cloned.1.call-update) | async-done | bytes 16777232 | tf_op jit(solution)/shard_map/reduce_scatter | solution.py:57
  585.4 21.7 %fusion.16 = (f32[4096]{0:T(1024)}, bf16[1024,4096]{1,0:T(8,128)(2,1)}, bf16[1024,4096]{1,0:T(8,128)(2,1)}) fusion(f32[1024,4096]{1,0:T(8,128)} %reduce-scatter.11.cloned.1.call-done, f32[1024,4096]{1,0:T(8,128)} %reduce-scatter.7.cloned.1.call-done, f32[4096]{0:T(1024)S(1)} %convert_element_type.35), kind=kLoop, calls=%fused_computation.34 | loop fusion | flops 92270592 | bytes 50364416 | tf_op jit(solution)/shard_map/reduce_sum | solution.py:59
  607.3 0.7 all-gather.11.cloned.1.call-update
  608.3 31.1 %all-gather.17.cloned.1.call-done = bf16[2048,4096]{1,0:T(8,128)(2,1)} async-done(((bf16[1024,4096]{1,0:T(8,128)(2,1)}), bf16[2048,4096]{1,0:T(8,128)(2,1)}) %all-gather.17.cloned.1.call-update) | async-done | bytes 16777232 | tf_op jit(solution)/shard_map/all_gather | solution.py:61
  639.4 43.1 %fusion.21 = f32[2048,2048]{1,0:T(8,128)} fusion(bf16[2048,4096]{1,0:T(8,128)(2,1)} %all-gather.17.cloned.1.call-done, bf16[2048,4096]{1,0:T(8,128)(2,1)} %all-gather.9.cloned.1.call-done), kind=kOutput, calls=%fused_computation.39 | convolution fusion | flops 34359738368 | bytes 50331648 | tf_op jit(solution)/shard_map/tf,df->td/dot_general | solution.py:64
  682.7 43.0 %fusion.19 = f32[2048,2048]{1,0:T(8,128)} fusion(bf16[2048,4096]{1,0:T(8,128)(2,1)} %all-gather.11.cloned.1.call-done, bf16[4096,2048]{1,0:T(8,128)(2,1)} %all-gather.13.cloned.1.call-done), kind=kOutput, calls=%fused_computation.37 | convolution fusion | flops 34359738368 | bytes 50331648 | tf_op jit(solution)/shard_map/dot_general | solution.py:47
  726.3 43.8 %fusion.22 = f32[2048,4096]{1,0:T(8,128)} fusion(bf16[2048,2048]{1,0:T(8,128)(2,1)} %all-gather.7.cloned.1.call-done, bf16[2048,4096]{1,0:T(8,128)(2,1)} %all-gather.17.cloned.1.call-done), kind=kOutput, calls=%fused_computation.40 | convolution fusion | flops 34359738368 | bytes 58720256 | tf_op jit(solution)/shard_map/td,tf->df/dot_general | solution.py:62
  770.3 43.7 %fusion.23 = f32[4096,2048]{1,0:T(8,128)} fusion(bf16[2048,4096]{1,0:T(8,128)(2,1)} %all-gather.11.cloned.1.call-done, bf16[2048,2048]{1,0:T(8,128)(2,1)} %all-gather.15.cloned.1.call-done), kind=kOutput, calls=%fused_computation.41 | convolution fusion | flops 34359738368 | bytes 58720256 | tf_op jit(solution)/shard_map/tf,td->fd/dot_general | solution.py:54
  814.2 0.6 copy-done.8
  814.8 23.9 %psum.37 = f32[4096]{0:T(1024)} all-reduce(f32[4096]{0:T(1024)S(1)} %copy-done.2), channel_id=1, replica_groups=mesh['part'=1,'row'=4,'col'=4,'dep'=2] {'row','dep'}, use_global_device_ids=true, to_apply=%region_12.0 | all-reduce | flops 4096 | bytes 32768 | tf_op jit(solution)/shard_map/psum | solution.py:59
  838.7 3.6 fusion.12
  842.4 6.3 psum.36
  848.7 127.7 %reduce-scatter.9.cloned.1.call-done = f32[512,2048]{1,0:T(8,128)} async-done(((f32[2048,2048]{1,0:T(8,128)}), f32[512,2048]{1,0:T(8,128)}) %reduce-scatter.9.cloned.1.call-update) | async-done | bytes 4194320 | tf_op jit(solution)/shard_map/reduce_scatter | solution.py:48
  976.4 6.7 convert_reduce_fusion.1
  983.1 58.4 %all-reduce = (f32[2048]{0:T(1024)}, f32[2,2048]{1,0:T(2,128)S(1)}) all-reduce(f32[2048]{0:T(1024)S(1)} %get-tuple-element.19, f32[2,2048]{1,0:T(2,128)S(1)} %pad_maximum_fusion), channel_id=1, replica_groups=mesh['part'=1,'row'=4,'col'=4,'dep'=2] {'row','col'}, use_global_device_ids=true, to_apply=%region_15.0 | all-reduce | flops 6144 | bytes 49152 | tf_op jit(solution)/shard_map/psum | solution.py:53
  1041.5 0.6 fusion.17
  1042.1 218.1 %reduce-scatter.15.cloned.1.call-done = f32[512,4096]{1,0:T(8,128)} async-done(((f32[2048,4096]{1,0:T(8,128)}), f32[512,4096]{1,0:T(8,128)}) %reduce-scatter.15.cloned.1.call-update) | async-done | bytes 8388624 | tf_op jit(solution)/shard_map/reduce_scatter | solution.py:63
  1260.2 6.0 convert_element_type.42
  1266.2 275.7 %reduce-scatter.17.cloned.1.call-done = f32[1024,2048]{1,0:T(8,128)} async-done(((f32[4096,2048]{1,0:T(8,128)}), f32[1024,2048]{1,0:T(8,128)}) %reduce-scatter.17.cloned.1.call-update) | async-done | bytes 8388624 | tf_op jit(solution)/shard_map/reduce_scatter | solution.py:55
  1542.0 6.0 convert_element_type.43
  (47 shorter events, 4.0 us)
Async XLA Ops:
  7.2 93.9 %all-gather.7.cloned.1.call-start = ((), (), s32[]{:S(2)}) async-start(), calls=%async_computation.6 | async-start | bytes 10485760 | tf_op jit(solution)/shard_map/all_gather | solution.py:40
  13.8 0.6 copy-start.3
  13.8 0.6 copy-start.5
  18.2 237.8 %all-gather.9.cloned.1.call-start = ((), (), s32[]{:S(2)}) async-start(), calls=%async_computation.7 | async-start | bytes 20971520 | tf_op jit(solution)/shard_map/all_gather | solution.py:41
  19.0 320.3 %all-gather.15.cloned.1.call-start = ((), (), s32[]{:S(2)}) async-start(), calls=%async_computation.12 | async-start | bytes 10485760 | tf_op jit(solution)/shard_map/all_gather | solution.py:52
  19.8 474.2 %all-gather.13.cloned.1.call-start = ((), (), s32[]{:S(2)}) async-start(), calls=%async_computation.10 | async-start | bytes 20971520 | tf_op jit(solution)/shard_map/all_gather | solution.py:46
  20.5 519.3 %reduce-scatter.7.cloned.1.call-start = ((), (), s32[]{:S(2)}) async-start(), calls=%async_computation.8 | async-start | bytes 50331648 | tf_op jit(solution)/shard_map/reduce_scatter | solution.py:43
  299.5 285.9 %reduce-scatter.11.cloned.1.call-start = ((), (), s32[]{:S(2)}) async-start(), calls=%async_computation.13 | async-start | bytes 50331648 | tf_op jit(solution)/shard_map/reduce_scatter | solution.py:57
  537.6 0.7 copy-start.7
  537.7 101.7 %all-gather.17.cloned.1.call-start = ((), (), s32[]{:S(2)}) async-start(), calls=%async_computation.14 | async-start | bytes 25165824 | tf_op jit(solution)/shard_map/all_gather | solution.py:61
  607.2 75.5 %all-gather.11.cloned.1.call-start = ((), (), s32[]{:S(2)}) async-start(), calls=%async_computation.9 | async-start | bytes 25165824 | tf_op jit(solution)/shard_map/all_gather | solution.py:45
  608.0 230.7 %reduce-scatter.13.cloned.1.call-start = ((), (), s32[]{:S(2)}) async-start(), calls=%async_computation.15 | async-start | bytes 20971520 | tf_op jit(solution)/shard_map/reduce_scatter | solution.py:65
  682.6 293.8 %reduce-scatter.9.cloned.1.call-start = ((), (), s32[]{:S(2)}) async-start(), calls=%async_computation.11 | async-start | bytes 20971520 | tf_op jit(solution)/shard_map/reduce_scatter | solution.py:48
  725.8 534.4 %reduce-scatter.15.cloned.1.call-start = ((), (), s32[]{:S(2)}) async-start(), calls=%async_computation.16 | async-start | bytes 41943040 | tf_op jit(solution)/shard_map/reduce_scatter | solution.py:63
  770.1 771.9 %reduce-scatter.17.cloned.1.call-start = ((), (), s32[]{:S(2)}) async-start(), calls=%async_computation.17 | async-start | bytes 41943040 | tf_op jit(solution)/shard_map/reduce_scatter | solution.py:55
  814.1 0.7 copy-start.8
  814.1 0.7 copy-start.2
  814.1 24.6 %copy-start = (bf16[512,2048]{1,0:T(8,128)(2,1)S(1)}, bf16[512,2048]{1,0:T(8,128)(2,1)}, u32[]{:S(2)}) copy-start(bf16[512,2048]{1,0:T(8,128)(2,1)} %param.8) | copy-start | bytes 6291460
  814.1 24.6 %copy-start.1 = (f32[2048]{0:T(1024)S(1)}, f32[2048]{0:T(1024)}, u32[]{:S(2)}) copy-start(f32[2048]{0:T(1024)} %param.9) | copy-start | bytes 24580
  814.1 24.6 %copy-start.4 = (f32[512,1]{0,1:T(1,128)S(1)}, f32[512,1]{0,1:T(1,128)}, u32[]{:S(2)}) copy-start(f32[512,1]{0,1:T(1,128)} %copy-done.3) | copy-start | bytes 6148
  814.1 24.6 %copy-start.6 = (f32[512,1]{0,1:T(1,128)S(1)}, f32[512,1]{0,1:T(1,128)}, u32[]{:S(2)}) copy-start(f32[512,1]{0,1:T(1,128)} %copy-done.5) | copy-start | bytes 6148
Sparse Core Ops, SparseCore 0:
  18.3 82.7 all-gather.6
  102.7 153.2 all-gather.8
  257.6 81.6 all-gather.14
  340.7 153.2 all-gather.12
  496.2 43.5 reduce-scatter.6
  541.9 43.4 reduce-scatter.10
  607.3 32.0 all-gather.16
  641.0 32.0 all-gather.10
  682.7 146.2 reduce-scatter.12
  831.3 145.0 reduce-scatter.8
  978.8 281.3 reduce-scatter.14
  1262.4 279.4 reduce-scatter.16
where the time goes:
time: 1560 us
  waiting for transfers between devices  1130 us (72%)
  matrix products  261 us (17%)
  blocking collectives  92.8 us (6%)
  other arithmetic  50.3 us (3%)
    reduce_scatter x1, waiting for transfers between devices, local_step(): lax.psum_scatter(w_down_part, 'row', scatter_dimension=0, tiled=True)  276 us
    reduce_scatter x1, waiting for transfers between devices, local_step(): lax.psum_scatter(w_up_part, 'row', scatter_dimension=0, tiled=True)  218 us
    all_gather x1, waiting for transfers between devices, local_step(): w_up_full = lax.all_gather(w_up, 'row', axis=0, tiled=True)  155 us
    all_gather x1, waiting for transfers between devices, local_step(): w_down_full = lax.all_gather(w_down, 'row', axis=0, tiled=True)  155 us
    reduce_scatter x1, waiting for transfers between devices, local_step(): out_sum = lax.psum_scatter(out_part, 'col', scatter_dimension=0, tiled=True)  128 us
    all_gather x1, waiting for transfers between devices, local_step(): normed_full = lax.all_gather(normed, 'col', axis=0, tiled=True)  80.6 us
    psum x1, blocking collectives, local_step(): b_down_grad = lax.psum(jnp.sum(g_float, axis=0), ('row', 'col'))  58.4 us
    reduce_scatter x1, waiting for transfers between devices, local_step(): lax.psum_scatter(hid_part, 'dep', scatter_dimension=0, tiled=True)  45.6 us
  transfers between devices with their start and end apart: 12, of which 10 were waited for; matrix products, arithmetic and copies ran while one was open for 18% of the time, Pallas kernels for 0%

commit v1 on v0

v1 whole, which is shorter than its diff:
```python
import functools

import jax
import jax.numpy as jnp
from jax import lax
from jax.experimental import pallas as pl
from jax.experimental.pallas import tpu as pltpu
from jax.sharding import PartitionSpec as P

LN_EPS = 1e-5
GELU_K = 0.7978845608028654
GELU_C = 0.044715
F32 = jnp.float32
BF16 = jnp.bfloat16
MESH = pl.DeviceIdType.MESH

NAMES = ("A", "G", "W1", "W2", "HP", "HQ", "CP", "CQ", "DB",
         "PY", "RY", "YQ1", "YQ2", "YRF", "YRX", "PD", "RD", "DQ1", "DQ2", "DRF", "DRX",
         "S1", "R1", "S2", "R2", "K1", "K2", "OUT1", "OUT2")


def buffers(TH, DM, DS, FB):
    F2, FC = 2 * FB, 4 * FB
    shapes = {
        "A": ((2, 4, 2 * TH, DM), BF16), "G": ((2, 4, 2 * TH, DM), BF16),
        "W1": ((DM, FC), BF16), "W2": ((FC, DM), BF16),
        "HP": ((2, 2, 2, 2 * TH, F2), BF16), "CP": ((2, 2, 2, 2 * TH, F2), BF16),
        "HQ": ((2, 2, 2 * TH, F2), BF16), "CQ": ((2, 2, 2 * TH, F2), BF16),
        "DB": ((8, FC), F32),
        "S1": ((4, DS, F2), F32), "R1": ((4, DS, F2), F32), "S2": ((FB, DM), F32), "R2": ((FB, DM), F32),
        "K1": ((4, DS, F2), BF16), "K2": ((4, FB, DM // 4), BF16),
        "OUT1": ((DS, 8 * FB), BF16), "OUT2": ((2 * FB, DM // 2), BF16),
    }
    for p, rr, s in (("PY", "RY", "Y"), ("PD", "RD", "D")):
        shapes[p] = shapes[rr] = ((2, 2, TH, DM), F32)
        shapes[s + "Q1"] = shapes[s + "Q2"] = shapes[s + "RX"] = ((2, TH, DM), F32)
        shapes[s + "RF"] = ((2, TH // 2, DM), F32)
    return [jax.ShapeDtypeStruct(*shapes[n]) for n in NAMES]


def mul(x, n):
    return x * n if isinstance(x, int) else pl.multiple_of(x * n, n)


def cp(src, dst, sem):
    return pltpu.make_async_copy(src, dst, sem)


def start(*copies):
    for t in copies:
        t.start()


def wait(*copies):
    for t in copies:
        t.wait()


def kernel(cfg, a_own, g_own, w1, w2, bup, *refs):
    TH, DM, DS, FB = cfg
    o = dict(zip(NAMES, refs[:len(NAMES)]))
    ssem, rsem = refs[len(NAMES):]
    DH, F2, FC, BN, HT, T2 = DM // 2, 2 * FB, 4 * FB, DM // 4, TH // 2, 2 * TH
    A, G, W1, W2 = o["A"], o["G"], o["W1"], o["W2"]
    r, c, d = lax.axis_index("row"), lax.axis_index("col"), lax.axis_index("dep")
    hp, hi = r % 2, r // 2
    g = (r + hi) % 2
    u, v, q = r + 1 - 2 * hp, 3 - r, (r + 2) % 4
    R, L, far = (c + 1) % 4, (c + 3) % 4, (c + 2) % 4
    e = 1 - d
    pos_r, pos_v = 2 * g + hi, 2 * g + 1 - hi
    pos_u, pos_q = 2 * (1 - g) + hi, 2 * (1 - g) + 1 - hi
    half_g, half_n = pl.ds(mul(g, F2), F2), pl.ds(mul(1 - g, F2), F2)
    c_lo, c_hi = c % 2, c // 2

    ids, counts = {}, [0, 0]

    def rid(name, n=1):
        if name not in ids:
            ids[name] = counts[0]
            counts[0] += n
        return ids[name]

    for nm in ("A", "G"):
        for w in ("xr0", "xl0", "u", "xr1", "xl1", "fr0", "fl0", "fr1", "fl1"):
            rid(nm + w)
        for t in ("0", "1"):
            for w in ("c", "L", "R", "x", "y"):
                rid(nm + "d" + t + w)
    rid("w1d", 4)
    for s in ("u", "v"):
        rid("w1" + s, 8)
        rid("w2" + s, 2)
        rid("f1" + s, 2)
        rid("f2" + s)
    rid("w2d")
    for s in ("s1", "s2", "k1u"):
        rid(s, 4)
    rid("k1d", 2)
    rid("k2", 2)
    for s in ("Y", "D"):
        for w in ("p", "r", "l", "pr", "pl"):
            rid(s + w, 4)

    pending = []
    dev_e, dev_R, dev_L = {"dep": e}, {"col": R}, {"col": L}

    def dev(row, core):
        return {"row": row, "dep": core}

    class Send:
        def __init__(self, fn, n=1):
            self.fn, self.sid = fn, counts[1]
            counts[1] += n
            for j in range(n):
                pending.append((self, j))

        def desc(self, j=0):
            src, dst, rsid, device = self.fn(j)
            return pltpu.make_async_remote_copy(src_ref=src, dst_ref=dst, send_sem=ssem.at[self.sid + j], recv_sem=rsem.at[rsid],
                                                device_id=device, device_id_type=MESH)

        def start(self, j=0):
            self.desc(j).start()

    def same(ref, rsid, device):
        return Send(lambda j: (ref, ref, rsid, device))

    def arrived(dst, rsid):
        pltpu.make_async_remote_copy(src_ref=dst, dst_ref=dst, send_sem=ssem.at[0], recv_sem=rsem.at[rsid],
                                     device_id=dev_e, device_id_type=MESH).wait_recv()

    barrier = pltpu.get_barrier_semaphore()
    peers = [dev_e, dev_R, dev_L] + [dev(t, k) for t in (u, v) for k in (0, 1)]
    for p in peers:
        pl.semaphore_signal(barrier, inc=1, device_id=p, device_id_type=MESH)
    pl.semaphore_wait(barrier, len(peers))

    ARR = (("A", A, a_own), ("G", G, g_own))
    ROW = (hp, 1 - hp)

    def ch(X, t, col, core, part=None):
        if part is None:
            return X.at[ROW[t], col, pl.ds(mul(core, TH), TH)]
        return X.at[ROW[t], col, pl.ds(pl.multiple_of(core * TH + part * HT, HT), HT)]

    def w1_src(pos, core):
        gg, ii = pos // 2, pos % 2
        return w1.at[:, pl.ds(mul(((1 - gg) * 3 * ii + gg * (1 + ii)) * 2 + core, FB), FB)]

    def w1_rows(dd, row):
        return pl.ds(mul(dd * 4 + row, DS), DS)

    def w1_dst(dd, row, pos):
        return W1.at[w1_rows(dd, row), pl.ds(mul(pos, FB), FB)]

    def send_w1(tag, row, half):
        for core in (0, 1):
            for ii in (0, 1):
                pos = 2 * half + ii
                Send(lambda j, pos=pos, core=core: (w1_src(pos, core), w1_dst(d, r, pos), rid("w1" + tag) + d * 4 + pos, dev(row, core))).start()

    def wait_w1(tag, row, half):
        for dd in (0, 1):
            for ii in (0, 1):
                pos = 2 * half + ii
                arrived(w1_dst(dd, row, pos), rid("w1" + tag) + dd * 4 + pos)

    def w2_part(pos, half):
        return W2.at[pl.ds(mul(pos, FB), FB), pl.ds(mul(half, DH), DH)]

    def send_w2(tag, row):
        for core in (0, 1):
            Send(lambda j, core=core: (w2.at[pl.ds(core * FB, FB), :], w2_part(pos_r, d), rid("w2" + tag) + d, dev(row, core))).start()

    def wait_w2(tag, pos):
        for dd in (0, 1):
            arrived(w2_part(pos, dd), rid("w2" + tag) + dd)

    for nm, X, own in ARR:
        for w, dv in (("u", dev(u, d)), ("xr0", dev_R), ("xl0", dev_L)):
            Send(lambda j, X=X, own=own, nm=nm, w=w, dv=dv: (own, ch(X, 0, c, d), rid(nm + w), dv)).start()
    send_w1("v", v, g)
    send_w1("u", u, 1 - g)
    send_w2("v", v)
    send_w2("u", u)
    send_w1("u", u, g)
    for nm, X, own in ARR:
        Send(lambda j, X=X, own=own, nm=nm: (own, ch(X, 0, c, d), rid(nm + "d0c"), dev_e)).start()
    for pos in range(4):
        Send(lambda j, pos=pos: (w1_src(pos, e), w1_dst(d, r, pos), rid("w1d") + pos, dev_e)).start()
    Send(lambda j: (w2.at[pl.ds(mul(e, FB), FB), :], w2_part(pos_r, d), rid("w2d"), dev_e)).start()

    def own_copies(b0, b1, b2, b3, sems):
        ld = [cp(a_own, b0, sems.at[0]), cp(g_own, b1, sems.at[1]), cp(w2.at[pl.ds(mul(d, FB), FB), :], b3, sems.at[2])]
        ld += [cp(w1_src(pos, d), b2.at[:, pl.ds(pos * FB, FB)], sems.at[3 + pos]) for pos in range(4)]
        st = [cp(b0, ch(A, 0, c, d), sems.at[7]), cp(b1, ch(G, 0, c, d), sems.at[8]), cp(b3, w2_part(pos_r, d), sems.at[9]),
              cp(b2, W1.at[w1_rows(d, r), :], sems.at[10])]
        start(*ld)
        for i in range(3):
            wait(ld[i])
            start(st[i])
        wait(*ld[3:])
        start(st[3])
        wait(*st)

    pl.run_scoped(own_copies, pltpu.VMEM((TH, DM), BF16), pltpu.VMEM((TH, DM), BF16), pltpu.VMEM((DS, FC), BF16),
                  pltpu.VMEM((FB, DH), BF16), pltpu.SemaphoreType.DMA((11,)))

    fwd = {}
    for nm, X, _ in ARR:
        for t in (0, 1):
            k = nm + str(t)
            fwd[k] = [same(ch(X, t, L, d, 0), rid(nm + "fr" + str(t)), dev_R), same(ch(X, t, R, d, 1), rid(nm + "fl" + str(t)), dev_L),
                      same(ch(X, t, L, d), rid(nm + "d" + str(t) + "L"), dev_e), same(ch(X, t, R, d), rid(nm + "d" + str(t) + "R"), dev_e),
                      same(ch(X, t, far, d, 0), rid(nm + "d" + str(t) + "x"), dev_e), same(ch(X, t, far, d, 1), rid(nm + "d" + str(t) + "y"), dev_e)]
        fwd[nm + "p"] = [same(ch(X, 1, c, d), rid(nm + "xr1"), dev_R), same(ch(X, 1, c, d), rid(nm + "xl1"), dev_L),
                         same(ch(X, 1, c, d), rid(nm + "d1c"), dev_e)]

    def pass_on(nm, X, t):
        f, t_ = fwd[nm + str(t)], str(t)
        arrived(ch(X, t, L, d), rid(nm + "xr" + t_))
        f[0].start()
        arrived(ch(X, t, R, d), rid(nm + "xl" + t_))
        f[1].start()
        f[2].start()
        f[3].start()

    def far_in(nm, X, t):
        f, t_ = fwd[nm + str(t)], str(t)
        arrived(ch(X, t, far, d, 0), rid(nm + "fr" + t_))
        f[4].start()
        arrived(ch(X, t, far, d, 1), rid(nm + "fl" + t_))
        f[5].start()

    def other_core(t, which):
        for nm, X, _ in ARR:
            b = nm + "d" + str(t)
            if which == "far":
                arrived(ch(X, t, far, e, 0), rid(b + "x"))
                arrived(ch(X, t, far, e, 1), rid(b + "y"))
            else:
                arrived(ch(X, t, {"c": c, "L": L, "R": R}[which], e), rid(b + which))

    f1u = Send(lambda j: (W1.at[w1_rows(j, v), half_g], W1.at[w1_rows(j, v), half_g], rid("f1u") + j, dev(u, d)), 2)
    f1v = Send(lambda j: (W1.at[w1_rows(j, u), half_g], W1.at[w1_rows(j, u), half_g], rid("f1v") + j, dev(v, d)), 2)
    q0, q1 = pl.ds(0, BN), pl.ds(BN, DM - BN)

    def w2_rows(pos, cols):
        return W2.at[pl.ds(mul(pos, FB), FB), cols]

    f2u = same(w2_rows(pos_v, q0), rid("f2u"), dev(u, d))
    f2v = same(w2_rows(pos_u, q1), rid("f2v"), dev(v, d))

    pass_on("A", A, 0)
    wait_w1("v", v, g)
    for j in (0, 1):
        f1u.start(j)
    pass_on("G", G, 0)
    for nm, X, _ in ARR:
        arrived(ch(X, 1, c, d), rid(nm + "u"))
        for t in fwd[nm + "p"]:
            t.start()
    wait_w1("u", u, g)
    for j in (0, 1):
        f1v.start(j)
    send_w1("v", v, 1 - g)
    for nm, X, _ in ARR:
        far_in(nm, X, 0)
    wait_w2("v", pos_v)
    f2u.start()
    for which in ("c", "L", "R", "far"):
        other_core(0, which)
    for ii in (0, 1):
        arrived(w1_dst(e, r, 2 * g + ii), rid("w1d") + 2 * g + ii)
    arrived(w2_part(pos_r, e), rid("w2d"))
    for j in (0, 1):
        arrived(W1.at[w1_rows(j, q), half_g], rid("f1v") + j)

    RC = min(32, TH)

    def cd_block(a, gr, w1b, w2b, bias, cbuf, gbuf, put, dbs, count_db):
        cbuf[...] = jnp.dot(a, w1b, preferred_element_type=F32)
        gbuf[...] = lax.dot_general(gr, w2b, (((1,), (1,)), ((), ())), preferred_element_type=F32)

        def rows(m, acc):
            sl = pl.ds(mul(m, RC), RC)
            pre = cbuf[sl, :] + bias
            sq = pre * pre
            th = jnp.tanh(GELU_K * (pre + GELU_C * pre * sq))
            half = 0.5 * (1.0 + th)
            slope = half + 0.5 * pre * (1.0 - th * th) * GELU_K * (1.0 + 3.0 * GELU_C * sq)
            dc = gbuf[sl, :] * slope
            put(sl, (pre * half).astype(BF16), dc.astype(BF16))
            return acc + jnp.sum(dc.reshape(RC // 8, 8, FB), axis=0)

        acc = lax.fori_loop(0, T2 // RC, rows, jnp.zeros((8, FB), F32))

        @pl.when(count_db)
        def _():
            dbs[...] += acc

    def order(k):
        k = k % 4
        return (c + k + k // 2 * (5 - 2 * k)) % 4

    def phase1(ab, gb, w1b, w2b, cbuf, gbuf, hb, cb, dbs, isem, osem, wsem):
        wl = [cp(W1.at[:, half_g], w1b, wsem.at[0]), cp(W2.at[half_g, :], w2b, wsem.at[1])]
        start(*wl)
        dbs[...] = jnp.zeros_like(dbs)

        def row_of(k):
            return jnp.where(k < 4, hp, 1 - hp)

        def ins(k, s):
            return [cp(A.at[row_of(k), order(k)], ab.at[s], isem.at[s]), cp(G.at[row_of(k), order(k)], gb.at[s], isem.at[2 + s])]

        def outs(k, s):
            at = (row_of(k), order(k) // 2, order(k) % 2)
            return [cp(hb.at[s], o["HP"].at[at], osem.at[s]), cp(cb.at[s], o["CP"].at[at], osem.at[2 + s])]

        start(*ins(0, 0))
        wait(*wl)

        def fetch(k):
            @pl.when(k == 0)
            def _():
                pass_on("A", A, 1)

            @pl.when(k == 3)
            def _():
                other_core(1, "c")

            @pl.when(k == 4)
            def _():
                pass_on("G", G, 1)
                wait_w2("u", pos_u)
                f2v.start()
                other_core(1, "R")

            @pl.when(k == 5)
            def _():
                other_core(1, "L")

            @pl.when(k == 6)
            def _():
                for nm, X, _ in ARR:
                    far_in(nm, X, 1)
                other_core(1, "far")

            @pl.when(k < 7)
            def _():
                start(*ins(k + 1, 1 - k % 2))

        def it(k, _):
            s = k % 2
            wait(*ins(k, s))

            @pl.when(k >= 2)
            def _():
                wait(*outs(k - 2, s))

            for ii in (0, 1):
                cols = slice(ii * FB, (ii + 1) * FB)

                def put(sl, h, dc, cols=cols):
                    hb[s, sl, cols] = h
                    cb[s, sl, cols] = dc

                cd_block(ab[s], gb[s], w1b[:, cols], w2b[cols, :], bup[:, pl.ds(mul(2 * g + ii, FB), FB)], cbuf, gbuf, put,
                         dbs.at[:, cols], k < 4)

                @pl.when((k == 6) == (ii == 1))
                def _():
                    fetch(k)
            start(*outs(k, s))
            return 0

        lax.fori_loop(0, 8, it, 0)
        for k in (6, 7):
            wait(*outs(k, k % 2))
        t = cp(dbs, o["DB"].at[:, half_g], wsem.at[0])
        start(t)
        wait(t)

    pl.run_scoped(phase1, pltpu.VMEM((2, T2, DM), BF16), pltpu.VMEM((2, T2, DM), BF16), pltpu.VMEM((DM, F2), BF16),
                  pltpu.VMEM((F2, DM), BF16), pltpu.VMEM((T2, FB), F32), pltpu.VMEM((T2, FB), F32),
                  pltpu.VMEM((2, T2, F2), BF16), pltpu.VMEM((2, T2, F2), BF16), pltpu.VMEM((8, F2), F32),
                  pltpu.SemaphoreType.DMA((4,)), pltpu.SemaphoreType.DMA((4,)), pltpu.SemaphoreType.DMA((2,)))

    TN = (((0,), (0,)), ((), ()))
    ALLT = 8 * T2

    s1 = Send(lambda j: (o["S1"].at[j], o["R1"].at[j], rid("s1") + j, dev(v, d)), 4)
    s2 = Send(lambda j: (o["S2"].at[:, pl.ds(mul(j, BN), BN)], o["R2"].at[:, pl.ds(mul(j, BN), BN)], rid("s2") + j, dev(v, d)), 4)

    def run(n, ins, outs, work, done):
        start(*ins(0, 0))

        def it(k, _):
            s = k % 2
            wait(*ins(k, s))

            @pl.when(k < n - 1)
            def _():
                start(*ins(k + 1, 1 - s))
            work(k, s)
            start(*outs(k, s))

            @pl.when(k >= 1)
            def _():
                wait(*outs(k - 1, 1 - s))
                done(k - 1, 1 - s)
            return 0

        lax.fori_loop(0, n, it, 0)
        wait(*outs(n - 1, (n - 1) % 2))
        done(n - 1, (n - 1) % 2)

    def dw1_cols(k, pair, first):
        j = first + (1 - 2 * first) * (k // 2)
        return pl.ds(mul((k % 2) * 4 + 2 * pair + j, DS), DS)

    def dw1_send(dcb, ab, ob, isem, osem, wsem):
        t = cp(o["CP"], dcb, wsem.at[0])
        start(t)
        wait(t)

        def work(k, s):
            ob[s] = lax.dot_general(ab[s].reshape(ALLT, DS), dcb[...].reshape(ALLT, F2), TN, preferred_element_type=F32)

        run(4, lambda k, s: [cp(A.at[:, :, :, dw1_cols(k, 1 - hi, hp)], ab.at[s], isem.at[s])],
            lambda k, s: [cp(ob.at[s], o["S1"].at[k], osem.at[s])], work, lambda k, s: s1.start(k))

    pl.run_scoped(dw1_send, pltpu.VMEM((2, 2, 2, T2, F2), BF16), pltpu.VMEM((2, 2, 4, T2, DS), BF16), pltpu.VMEM((2, DS, F2), F32),
                  pltpu.SemaphoreType.DMA((2,)), pltpu.SemaphoreType.DMA((2,)), pltpu.SemaphoreType.DMA((1,)))

    def block_of(j):
        return pl.ds(mul(j, BN), BN)

    def h_cols(pair):
        return pl.ds(mul(pair, FB), FB)

    def dw2_send(hb, gb, ob, isem, osem, wsem):
        t = cp(o["HP"].at[:, :, :, :, h_cols(1 - hi)], hb, wsem.at[0])
        start(t)
        wait(t)

        def work(k, s):
            ob[s] = lax.dot_general(hb[...].reshape(ALLT, FB), gb[s].reshape(ALLT, BN), TN, preferred_element_type=F32)

        run(4, lambda k, s: [cp(G.at[:, :, :, block_of(k)], gb.at[s], isem.at[s])],
            lambda k, s: [cp(ob.at[s], o["S2"].at[:, block_of(k)], osem.at[s])], work, lambda k, s: s2.start(k))

    pl.run_scoped(dw2_send, pltpu.VMEM((2, 2, 2, T2, FB), BF16), pltpu.VMEM((2, 2, 4, T2, BN), BF16), pltpu.VMEM((2, FB, BN), F32),
                  pltpu.SemaphoreType.DMA((2,)), pltpu.SemaphoreType.DMA((2,)), pltpu.SemaphoreType.DMA((1,)))

    for ii in (0, 1):
        pos = 2 * (1 - g) + ii
        arrived(w1_dst(e, r, pos), rid("w1d") + pos)
    wait_w1("u", u, 1 - g)
    wait_w1("v", v, 1 - g)
    for j in (0, 1):
        arrived(W1.at[w1_rows(j, q), half_n], rid("f1u") + j)

    def phase2(ab, gb, w1b, w2b, cbuf, gbuf, hb, cb, dbs, isem, osem, wsem):
        def pos_of(b):
            return jnp.where(b == 0, pos_u, pos_q)

        def wl(b):
            cols = pl.ds(mul(pos_of(b), FB), FB)
            return [cp(W1.at[:, cols], w1b.at[b], wsem.at[b]), cp(W2.at[cols, :], w2b.at[b], wsem.at[2 + b])]

        start(*wl(0))
        dbs[...] = jnp.zeros_like(dbs)

        def ins(k, s):
            return [cp(A.at[hp, k % 4], ab.at[s], isem.at[s]), cp(G.at[hp, k % 4], gb.at[s], isem.at[2 + s])]

        def outs(k, s):
            at = (k % 4 // 2, k % 2, slice(None), pl.ds(mul(pos_of(k // 4) % 2, FB), FB))
            return [cp(hb.at[s], o["HQ"].at[at], osem.at[s]), cp(cb.at[s], o["CQ"].at[at], osem.at[2 + s])]

        start(*ins(0, 0))

        def it(k, _):
            s, b = k % 2, k // 4

            @pl.when(k % 4 == 0)
            def _():
                wait(*wl(b))
            wait(*ins(k, s))

            @pl.when(k < 7)
            def _():
                start(*ins(k + 1, 1 - s))

            @pl.when(k >= 2)
            def _():
                wait(*outs(k - 2, s))

            def put(sl, h, dc):
                hb[s, sl, :] = h
                cb[s, sl, :] = dc

            cd_block(ab[s], gb[s], w1b[b], w2b[b], bup[:, pl.ds(mul(pos_of(b), FB), FB)], cbuf, gbuf, put, dbs.at[b], k >= 0)
            start(*outs(k, s))

            @pl.when(k == 2)
            def _():
                arrived(w2_rows(pos_q, q1), rid("f2v"))
                arrived(w2_rows(pos_q, q0), rid("f2u"))
                start(*wl(1))
            return 0

        lax.fori_loop(0, 8, it, 0)
        for k in (6, 7):
            wait(*outs(k, k % 2))
        ts = [cp(dbs.at[b], o["DB"].at[:, pl.ds(mul(pos_of(b), FB), FB)], wsem.at[b]) for b in (0, 1)]
        start(*ts)
        wait(*ts)

    pl.run_scoped(phase2, pltpu.VMEM((2, T2, DM), BF16), pltpu.VMEM((2, T2, DM), BF16), pltpu.VMEM((2, DM, FB), BF16),
                  pltpu.VMEM((2, FB, DM), BF16), pltpu.VMEM((T2, FB), F32), pltpu.VMEM((T2, FB), F32),
                  pltpu.VMEM((2, T2, FB), BF16), pltpu.VMEM((2, T2, FB), BF16), pltpu.VMEM((2, 8, FB), F32),
                  pltpu.SemaphoreType.DMA((4,)), pltpu.SemaphoreType.DMA((4,)), pltpu.SemaphoreType.DMA((4,)))

    def wdot(lhs, wref, s, first, nt):
        sel = pl.ds(mul(g if first else 1 - g, F2), F2)
        x = lhs[...].reshape(-1, F2)
        if nt:
            return lax.dot_general(x, wref[s, :, sel], (((1,), (1,)), ((), ())), preferred_element_type=F32)
        return jnp.dot(x, wref[s, sel, :], preferred_element_type=F32)

    def region(s, nt, XP, XQ, PX, RX):
        Q1, Q2, RF, RR = o[s + "Q1"], o[s + "Q2"], o[s + "RF"], o[s + "RX"]
        ex = Send(lambda j: (PX.at[:, :, :, block_of(j)], RX.at[:, :, :, block_of(j)], rid(s + "p") + j, dev_e), 4)
        rows_r, rows_l = pl.ds(0, HT), pl.ds(HT, HT)
        far_r = Send(lambda j: (Q1.at[1 - c_hi, rows_r, block_of(j)], RF.at[1 - c_hi, :, block_of(j)], rid(s + "r") + j, dev_R), 4)
        far_l = Send(lambda j: (Q1.at[1 - c_hi, rows_l, block_of(j)], RF.at[1 - c_hi, :, block_of(j)], rid(s + "l") + j, dev_L), 4)
        pm_r = Send(lambda j: (Q2.at[R // 2, :, block_of(j)], RR.at[0, :, block_of(j)], rid(s + "pr") + j, dev_R), 4)
        pm_l = Send(lambda j: (Q2.at[L // 2, :, block_of(j)], RR.at[1, :, block_of(j)], rid(s + "pl") + j, dev_L), 4)
        wshape = (BN, FC) if nt else (FC, BN)

        def wblk(j, wb, slot, sem):
            src = W1.at[block_of(j), :] if nt else W2.at[:, block_of(j)]
            return cp(src, wb.at[slot], sem.at[slot])

        mine, other = pl.ds(mul(d, TH), TH), pl.ds(mul(e, TH), TH)

        def first(lop, loq, lfp, lfq, wb, ob, ab, qb, wsem, lsem, osem):
            lds = [cp(XP.at[hp, :, :, other], lop, lsem.at[0]), cp(XQ.at[:, :, other], loq, lsem.at[1]),
                   cp(XP.at[hp, :, c_lo, mine], lfp, lsem.at[2]), cp(XQ.at[:, c_lo, mine], lfq, lsem.at[3])]
            start(wblk(0, wb, 0, wsem), *lds)
            wait(*lds)

            def it(j, _):
                slot, prev = j % 3, (j + 2) % 3
                o1 = cp(ob, PX.at[:, :, :, block_of(j)], osem.at[0])

                @pl.when(j < 4)
                def _():
                    wait(wblk(j, wb, slot, wsem))

                    @pl.when(j < 3)
                    def _():
                        start(wblk(j + 1, wb, (j + 1) % 3, wsem))
                    ob[...] = (wdot(lop, wb, slot, True, nt) + wdot(loq, wb, slot, False, nt)).reshape(2, 2, TH, BN)
                    start(o1)

                @pl.when(j >= 1)
                def _():
                    k = j - 1
                    arrived(RX.at[:, :, :, block_of(k)], rid(s + "p") + k)
                    add = cp(RX.at[:, c_lo, :, block_of(k)], ab, osem.at[1])
                    start(add)
                    qb[...] = (wdot(lfp, wb, prev, True, nt) + wdot(lfq, wb, prev, False, nt)).reshape(2, TH, BN)
                    wait(add)
                    qb[...] += ab[...]
                    o2 = cp(qb, Q1.at[:, :, block_of(k)], osem.at[2])
                    start(o2)
                    wait(o2)
                    far_r.start(k)
                    far_l.start(k)

                @pl.when(j < 4)
                def _():
                    wait(o1)
                    ex.start(j)
                return 0

            lax.fori_loop(0, 5, it, 0)

        def second(lp, lq, wb, ab, fb, ob, wsem, lsem, isem, osem):
            lds = [cp(XP.at[hp, :, 1 - c_lo, mine], lp, lsem.at[0]), cp(XQ.at[:, 1 - c_lo, mine], lq, lsem.at[1])]
            start(*lds)

            def ins(k, sl):
                return [wblk(k, wb, sl, wsem), cp(RX.at[:, 1 - c_lo, :, block_of(k)], ab.at[sl], isem.at[sl]),
                        cp(RF.at[:, :, block_of(k)], fb.at[sl], isem.at[2 + sl])]

            def need(k):
                arrived(RF.at[R // 2, :, block_of(k)], rid(s + "r") + k)
                arrived(RF.at[L // 2, :, block_of(k)], rid(s + "l") + k)

            need(0)
            start(*ins(0, 0))
            wait(*lds)

            def outs(k, sl):
                return cp(ob.at[sl], Q2.at[:, :, block_of(k)], osem.at[sl])

            def it(k, _):
                sl = k % 2
                wait(*ins(k, sl))
                ob[sl] = (wdot(lp, wb, sl, True, nt) + wdot(lq, wb, sl, False, nt)).reshape(2, TH, BN) + ab[sl]
                ob[sl, R // 2, 0:HT, :] += fb[sl, R // 2]
                ob[sl, L // 2, HT:TH, :] += fb[sl, L // 2]
                start(outs(k, sl))

                @pl.when(k < 3)
                def _():
                    need(k + 1)
                    start(*ins(k + 1, 1 - sl))
                wait(outs(k, sl))
                pm_r.start(k)
                pm_l.start(k)
                return 0

            lax.fori_loop(0, 4, it, 0)

        def run_first():
            pl.run_scoped(first, pltpu.VMEM((2, 2, TH, F2), BF16), pltpu.VMEM((2, 2, TH, F2), BF16), pltpu.VMEM((2, TH, F2), BF16),
                          pltpu.VMEM((2, TH, F2), BF16), pltpu.VMEM((3,) + wshape, BF16), pltpu.VMEM((2, 2, TH, BN), F32),
                          pltpu.VMEM((2, TH, BN), F32), pltpu.VMEM((2, TH, BN), F32), pltpu.SemaphoreType.DMA((3,)),
                          pltpu.SemaphoreType.DMA((4,)), pltpu.SemaphoreType.DMA((3,)))

        def run_second():
            pl.run_scoped(second, pltpu.VMEM((2, TH, F2), BF16), pltpu.VMEM((2, TH, F2), BF16), pltpu.VMEM((2,) + wshape, BF16),
                          pltpu.VMEM((2, 2, TH, BN), F32), pltpu.VMEM((2, 2, HT, BN), F32), pltpu.VMEM((2, 2, TH, BN), F32),
                          pltpu.SemaphoreType.DMA((2,)), pltpu.SemaphoreType.DMA((2,)), pltpu.SemaphoreType.DMA((4,)),
                          pltpu.SemaphoreType.DMA((2,)))

        def finish():
            for j in range(4):
                arrived(RR.at[0, :, block_of(j)], rid(s + "pr") + j)
                arrived(RR.at[1, :, block_of(j)], rid(s + "pl") + j)
        return run_first, run_second, finish

    y1, y2, y3 = region("Y", False, o["HP"], o["HQ"], o["PY"], o["RY"])
    d1, d2, d3 = region("D", True, o["CP"], o["CQ"], o["PD"], o["RD"])
    y1()
    d1()
    y2()
    d2()

    def out1_cols(ii):
        return pl.ds(mul(((1 - g) * 3 * ii + g * (1 + ii)) * 2 + d, FB), FB)

    K1, K2, OUT1, OUT2 = o["K1"], o["K2"], o["OUT1"], o["OUT2"]

    def piece(ii):
        return slice(ii * FB, (ii + 1) * FB)

    k1u = [Send(lambda m, ii=ii: (K1.at[m, :, piece(ii)], OUT1.at[:, out1_cols(ii)], rid("k1u") + d * 2 + ii, dev(u, m)), 2) for ii in (0, 1)]
    k1d = [Send(lambda m, ii=ii: (K1.at[2 + e, :, piece(ii)], OUT1.at[:, out1_cols(ii)], rid("k1d") + ii, dev_e)) for ii in (0, 1)]

    def out2_at(core, jj):
        return OUT2.at[pl.ds(mul(core, FB), FB), pl.ds(mul(jj, BN), BN)]

    k2 = Send(lambda jj: (K2.at[2 * e + jj], out2_at(d, jj), rid("k2") + jj, dev_e), 2)

    def dw1_keep(dcb, ab, rb, ob, isem, osem, wsem):
        t = cp(o["CP"], dcb, wsem.at[0])
        start(t)

        def ins(k, s):
            return [cp(A.at[:, :, :, dw1_cols(k, hi, 1 - hp)], ab.at[s], isem.at[s]), cp(o["R1"].at[k], rb.at[s], isem.at[2 + s])]

        def outs(k, s):
            return cp(ob.at[s], K1.at[k], osem.at[s])

        arrived(o["R1"].at[0], rid("s1"))
        start(*ins(0, 0))
        wait(t)

        def it(k, _):
            s = k % 2
            wait(*ins(k, s))

            @pl.when(k < 3)
            def _():
                arrived(o["R1"].at[k + 1], rid("s1") + k + 1)
                start(*ins(k + 1, 1 - s))
            acc = lax.dot_general(ab[s].reshape(ALLT, DS), dcb[...].reshape(ALLT, F2), TN, preferred_element_type=F32)
            ob[s] = (acc + rb[s]).astype(BF16)
            start(outs(k, s))
            wait(outs(k, s))

            @pl.when(k < 2)
            def _():
                k1u[0].start(k)
                k1u[1].start(k)

            @pl.when(k == 2 + e)
            def _():
                k1d[0].start()
                k1d[1].start()

            @pl.when(k == 2 + d)
            def _():
                ts = [cp(ob.at[s, :, piece(ii)], OUT1.at[:, out1_cols(ii)], wsem.at[ii]) for ii in (0, 1)]
                start(*ts)
                wait(*ts)
            return 0

        lax.fori_loop(0, 4, it, 0)

    pl.run_scoped(dw1_keep, pltpu.VMEM((2, 2, 2, T2, F2), BF16), pltpu.VMEM((2, 2, 4, T2, DS), BF16), pltpu.VMEM((2, DS, F2), F32),
                  pltpu.VMEM((2, DS, F2), BF16), pltpu.SemaphoreType.DMA((4,)), pltpu.SemaphoreType.DMA((2,)), pltpu.SemaphoreType.DMA((2,)))

    def dw2_keep(hb, gb, rb, ob, isem, osem, wsem):
        t = cp(o["HP"].at[:, :, :, :, h_cols(hi)], hb, wsem.at[0])
        start(t)

        def ins(k, s):
            return cp(G.at[:, :, :, block_of(k)], gb.at[s], isem.at[s])

        start(ins(0, 0))
        wait(t)

        def it(k, _):
            s = k % 2
            wait(ins(k, s))

            @pl.when(k < 3)
            def _():
                start(ins(k + 1, 1 - s))
            acc = lax.dot_general(hb[...].reshape(ALLT, FB), gb[s].reshape(ALLT, BN), TN, preferred_element_type=F32)
            arrived(o["R2"].at[:, block_of(k)], rid("s2") + k)
            t = cp(o["R2"].at[:, block_of(k)], rb, osem.at[0])
            start(t)
            wait(t)
            ob[...] = (acc + rb[...]).astype(BF16)

            @pl.when(k // 2 == d)
            def _():
                t = cp(ob, out2_at(d, k % 2), osem.at[1])
                start(t)
                wait(t)

            @pl.when(k // 2 == e)
            def _():
                t = cp(ob, K2.at[k], osem.at[1])
                start(t)
                wait(t)
                k2.start(k % 2)
            return 0

        lax.fori_loop(0, 4, it, 0)

    pl.run_scoped(dw2_keep, pltpu.VMEM((2, 2, 2, T2, FB), BF16), pltpu.VMEM((2, 2, 4, T2, BN), BF16), pltpu.VMEM((FB, BN), F32),
                  pltpu.VMEM((FB, BN), BF16), pltpu.SemaphoreType.DMA((2,)), pltpu.SemaphoreType.DMA((2,)), pltpu.SemaphoreType.DMA((1,)))

    y3()
    d3()
    for ii in (0, 1):
        for dd in (0, 1):
            arrived(OUT1.at[:, pl.ds(mul((g * 3 * ii + (1 - g) * (1 + ii)) * 2 + dd, FB), FB)], rid("k1u") + dd * 2 + ii)
        arrived(OUT1.at[:, pl.ds(mul(((1 - g) * 3 * ii + g * (1 + ii)) * 2 + e, FB), FB)], rid("k1d") + ii)
    for jj in (0, 1):
        arrived(out2_at(e, jj), rid("k2") + jj)
    for s, j in pending:
        s.desc(j).wait_send()


SEMS = (125, 125)


def solution(mesh):
    nr, nc, nd = mesh.shape["row"], mesh.shape["col"], mesh.shape["dep"]
    assert nr == 4 and nc == 4 and nd == 2
    tok_spec = P(("part", "row", "col"), "dep")
    vec_dep = P("dep")
    part_dep = P(("part", "dep"))
    in_specs = (tok_spec, vec_dep, vec_dep, P(("dep", "row"), "col"), P("col"), P(("col", "row"), "dep"), vec_dep, tok_spec)
    out_specs = (tok_spec, tok_spec, P(("part", "dep", "row"), "col"), P(("part", "col")), P(("part", "col", "row"), "dep"), part_dep, part_dep, part_dep)

    def swap(t):
        return lax.ppermute(t, "dep", [(0, 1), (1, 0)])

    def xor(t, axis, m):
        return lax.ppermute(t, axis, [(i, i ^ m) for i in range(4)])

    def local_step(x_in, ln_scale, ln_shift, w_up, b_up, w_down, b_down, y_grad):
        d, c = lax.axis_index("dep"), lax.axis_index("col")
        th, dhalf = x_in.shape[0] // 2, x_in.shape[1]
        dm, ds_, fb = 2 * dhalf, w_up.shape[0], w_up.shape[1] // 8
        lo = d == 0

        def merge_last(mine, other):
            return jnp.where(lo, jnp.concatenate([mine, other], axis=-1), jnp.concatenate([other, mine], axis=-1))

        def tok_half(t, which):
            return lax.dynamic_slice_in_dim(t, which * th, th, 0)

        xo = merge_last(tok_half(x_in, d), swap(tok_half(x_in, 1 - d)))
        go = merge_last(tok_half(y_grad, d), swap(tok_half(y_grad, 1 - d)))
        vecs = jnp.stack([ln_scale, ln_shift, b_down.astype(F32)])
        vecs = merge_last(vecs, swap(vecs))
        gamma, beta, bdn = vecs[0], vecs[1], vecs[2]
        x_float = xo.astype(F32)
        mean_row = jnp.sum(x_float, axis=1, keepdims=True) / dm
        var_row = jnp.sum(x_float * x_float, axis=1, keepdims=True) / dm - mean_row * mean_row
        inv_std = lax.rsqrt(var_row + LN_EPS)
        x_hat = (x_float - mean_row) * inv_std
        ao = (x_hat * gamma + beta).astype(BF16)
        b3 = lax.dynamic_index_in_dim(b_up.reshape(4, 2, fb), d, 1, keepdims=False).astype(F32)
        bup = jnp.concatenate([b3[k] for k in (0, 3, 1, 2)]).reshape(1, 4 * fb)

        cfg = (th, dm, ds_, fb)
        outs = pl.pallas_call(
            functools.partial(kernel, cfg),
            name="mlp_layer",
            out_shape=buffers(*cfg),
            in_specs=[pl.BlockSpec(memory_space=pl.ANY)] * 4 + [pl.BlockSpec(memory_space=pltpu.VMEM)],
            out_specs=[pl.BlockSpec(memory_space=pl.ANY)] * len(NAMES),
            scratch_shapes=[pltpu.SemaphoreType.DMA((SEMS[0],)), pltpu.SemaphoreType.DMA((SEMS[1],))],
            compiler_params=pltpu.CompilerParams(collective_id=0, has_side_effects=True, vmem_limit_bytes=62 * 1024 * 1024),
        )(ao, go, w_up, w_down, bup)
        o = dict(zip(NAMES, outs))

        def total(s):
            own = lax.dynamic_index_in_dim(o[s + "Q1"], c // 2, 0, keepdims=False)
            return own + o[s + "RX"][0] + o[s + "RX"][1]

        def to_out(t):
            mine = lax.dynamic_slice_in_dim(t, d * dhalf, dhalf, 1)
            oth = swap(lax.dynamic_slice_in_dim(t, (1 - d) * dhalf, dhalf, 1))
            return jnp.where(lo, jnp.concatenate([mine, oth], axis=0), jnp.concatenate([oth, mine], axis=0))

        y_out = to_out((x_float + total("Y") + bdn).astype(BF16))
        norm_grad = total("D")
        g_float = go.astype(F32)
        val = norm_grad * gamma
        m1 = jnp.sum(val, axis=1, keepdims=True) / dm
        m2 = jnp.sum(val * x_hat, axis=1, keepdims=True) / dm
        x_grad = to_out((g_float + inv_std * (val - m1 - x_hat * m2)).astype(BF16))

        sums = jnp.stack([jnp.sum(norm_grad * x_hat, axis=0), jnp.sum(norm_grad, axis=0), jnp.sum(g_float, axis=0)])
        s_m = lax.dynamic_slice_in_dim(sums, d * dhalf, dhalf, 1)
        sums = s_m + swap(lax.dynamic_slice_in_dim(sums, (1 - d) * dhalf, dhalf, 1))
        for axis, m in (("row", 1), ("row", 3), ("col", 1), ("col", 3)):
            sums = sums + xor(sums, axis, m)

        db4 = jnp.sum(o["DB"], axis=0).reshape(4, fb)
        db = jnp.stack([db4[k] for k in (0, 2, 3, 1)])
        for m in (1, 3):
            db = db + xor(db, "row", m)
        db_o = swap(db)
        b_up_grad = jnp.where(lo, jnp.stack([db, db_o], axis=1), jnp.stack([db_o, db], axis=1)).reshape(8 * fb)
        return (y_out, x_grad, o["OUT1"], b_up_grad, o["OUT2"], sums[2], sums[0], sums[1])

    return jax.shard_map(local_step, mesh=mesh, in_specs=in_specs, out_specs=out_specs, check_vma=False)
```

time: 1560 us -> 783 us (0.50)
  waiting for transfers between devices: 1130 us -> 4.61 us
  Pallas kernels: 0 us -> 711 us
  matrix products: 261 us -> 0 us
  blocking collectives: 92.8 us -> 0 us
  other arithmetic: 50.3 us -> 28.5 us
    pallas_call x0 -> x1, Pallas kernels: none -> 711 us  [local_step(): pl.pallas_call(functools.partial(kernel, cfg), name='mlp_layer', out_shap...]
    reduce_scatter x6 -> x0, waiting for transfers between devices: 669 us -> none  [the longest x1 276 us: local_step(): lax.psum_scatter(w_down_part, 'row', scatter_dimension=0, tiled=True)]
    all_gather x6 -> x0, waiting for transfers between devices: 461 us -> none  [the longest x1 155 us: local_step(): w_up_full = lax.all_gather(w_up, 'row', axis=0, tiled=True)]
    dot_general x6 -> x0, matrix products: 261 us -> none  [the longest x1 43.8 us: local_step(): jnp.einsum('td,tf->df', normed_full, pre_full, preferred_element_type=jnp...]
    psum x4 -> x0, blocking collectives: 92.8 us -> none  [the longest x1 58.4 us: local_step(): b_down_grad = lax.psum(jnp.sum(g_float, axis=0), ('row', 'col'))]
    reduce_sum x3 -> x4, other arithmetic: 30.7 us -> 11 us  [the longest x1 6.06 us: local_step(): jnp.sum(norm_grad, axis=0)]
  transfers between devices with their start and end apart: 12 -> 13, of which waited for: 10 -> 5; matrix products, arithmetic and copies ran while one was open for 18% -> 3% of each run, Pallas kernels for 0% -> 0%
where the time goes in v1:
time: 783 us; the launch traced here: 773 us
  Pallas kernels  711 us (91%)
  other arithmetic  28.5 us (4%)
  starting transfers between devices  14.8 us (2%)
  local copies, waits for them, and re-layouts  13.3 us (2%)
    pallas_call x1, Pallas kernels, local_step(): pl.pallas_call(functools.partial(kernel, cfg), name='mlp_layer', out_shap...  711 us
  transfers between devices with their start and end apart: 13, of which 5 were waited for; matrix products, arithmetic and copies ran while one was open for 3% of the time, Pallas kernels for 0%

profile of v1, /device:TPU:97, one launch (start us, length us, event | category | flops | bytes accessed | tf_op | source)
XLA Modules:
  0.0 773.4 jit_solution(8777686157359582674)
XLA Ops:
  0.6 0.7 stack.58
  1.3 0.7 pad_maximum_fusion.1
  2.1 2.1 collective-permute-start.1
  4.2 2.9 constant_dynamic-slice_fusion.7
  7.2 1.1 constant_dynamic-slice_fusion.5
  8.8 0.6 pad_maximum_fusion.2
  9.8 1.0 convert_reduce_fusion
  11.2 3.1 convert_reduce_fusion.1
  14.3 2.2 fusion.7.a_own
  16.5 710.7 %mlp_layer.1 = (bf16[2,4,512,4096]{3,2,1,0:T(8,128)(2,1)}, bf16[2,4,512,4096]{3,2,1,0:T(8,128)(2,1)}, bf16[4096,2048]{1,0:T(8,128)(2,1)}, bf16[2048,4096]{1,0:T(...) custom-call(bf16[256,4096]{1,0:T(8,128)(2,1)} %fusion.7.a_own, ...), custom_call_target="tpu_custom_call" | custom-call | tf_op jit(solution)/shard_map/mlp_layer/pallas_call | solution.py:822
  727.3 0.9 reduce_sum.76
  728.3 6.1 fusion.18
  734.4 1.3 slice-done.1
  735.7 5.7 fusion.11
  743.0 2.7 fusion
  745.8 1.5 collective-permute-start.9
  747.3 0.6 collective-permute-start.6
  748.0 0.7 collective-permute-done.9
  748.7 2.0 collective-permute-start.10
  750.8 2.1 collective-permute-start.4
  753.0 0.7 collective-permute-start.11
  753.7 3.2 collective-permute-start.7
  757.0 0.8 collective-permute-done.7
  757.8 1.1 collective-permute-start.12
  758.9 0.6 copy.16
  759.5 2.4 collective-permute-done.12
  761.9 0.6 fusion.20
  762.5 2.3 maximum_select_fusion.2
  764.9 2.3 maximum_select_fusion.3
  767.2 2.1 copy.19
  769.3 1.6 copy-done.3
  770.9 2.0 copy.20
  (59 shorter events, 3.4 us)
Async XLA Ops:
  2.1 7.3 collective-permute-start.1
  4.2 3.0 copy-start.5
  4.2 4.5 copy-start.8
  4.2 5.2 copy-start.6
  4.2 5.2 copy-start.7
  7.1 2.7 collective-permute-start
  8.3 2.9 collective-permute-start.2
  9.8 6.8 copy-start.1
  728.2 19.1 %collective-permute-start.5 = (f32[4,512]{1,0:T(4,128)S(1)}, f32[4,512]{1,0:T(4,128)S(1)}, u32[]{:S(2)}, u32[]{:S(2)}) collective-permute-start(f32[4,512]{1,0:T(4,128)S(1)} %pad_maximum_fusion.3), channel_id=1, source_target_pairs={{0,8},{8,0},{16,24},{24,16},{1,9},{9,1},{17,25},{25,17},{2,10},{10... | collective-permute-start | bytes 24584 | tf_op jit(solution)/shard_map/ppermute | solution.py:793
  728.3 6.1 slice-start
  728.3 6.1 copy-start.2
  728.3 7.4 slice-start.1
  741.4 1.6 copy-start
  741.5 4.2 collective-permute-start.8
  742.1 20.4 %collective-permute-start.3 = (bf16[256,2048]{1,0:T(8,128)(2,1)S(1)}, bf16[256,2048]{1,0:T(8,128)(2,1)S(1)}, u32[]{:S(2)}, u32[]{:S(2)}) collective-permute-start(bf16[256,2048]{1,0:T(8,128)(2,1)S(1)} %get-tuple-element.35), channel_id=1, source_target_pairs={{0,1},{1,0},{2,3},{3,2},{4,5},{5,4},{6,7},{7,6},{8,9},{9,8},{10,11... | collective-permute-start | bytes 3145736 | tf_op jit(solution)/shard_map/ppermute | solution.py:790
  745.8 2.9 collective-permute-start.9
  747.3 6.4 collective-permute-start.6
  748.7 4.3 collective-permute-start.10
  750.8 14.0 %collective-permute-start.4 = (bf16[256,2048]{1,0:T(8,128)(2,1)S(1)}, bf16[256,2048]{1,0:T(8,128)(2,1)S(1)}, u32[]{:S(2)}, u32[]{:S(2)}) collective-permute-start(bf16[256,2048]{1,0:T(8,128)(2,1)S(1)} %get-tuple-element.32), channel_id=1, source_target_pairs={{0,1},{1,0},{2,3},{3,2},{4,5},{5,4},{6,7},{7,6},{8,9},{9,8},{10,11... | collective-permute-start | bytes 3145736 | tf_op jit(solution)/shard_map/ppermute | solution.py:790
  753.0 4.9 collective-permute-start.11
  753.7 4.1 collective-permute-start.7
  757.8 4.1 collective-permute-start.12
  762.5 4.6 copy-start.4
  767.2 3.7 copy-start.3

commit v2 on v0

v2 whole, which is shorter than its diff:
```python
import functools

import jax
import jax.numpy as jnp
from jax import lax
from jax.experimental import pallas as pl
from jax.experimental.pallas import tpu as pltpu
from jax.sharding import PartitionSpec as P

LN_EPS = 1e-5
GELU_K = 0.7978845608028654
GELU_C = 0.044715
F32 = jnp.float32
BF16 = jnp.bfloat16
MESH = pl.DeviceIdType.MESH

NAMES = ("A", "G", "W1", "W2", "HP", "HQ", "CP", "CQ", "DB",
         "PY", "RY", "YQ1", "YQ2", "YRF", "YRX", "PD", "RD", "DQ1", "DQ2", "DRF", "DRX",
         "S1", "R1", "S2", "R2", "K1", "K2", "OUT1", "OUT2")
TWO, RING = 2, 4
BOTH, SLOTS = (0, 1), (2,)
NT = (((1,), (1,)), ((), ()))
TN = (((0,), (0,)), ((), ()))


def flip(x):
    return 1 - x


def low(x):
    return x % 2


def high(x):
    return x // 2


def buffers(TH, DM, DS, FB):
    F2, FC, T2 = 2 * FB, 4 * FB, 2 * TH
    pair = (TWO, TWO)
    shapes = {
        "A": ((TWO, RING, T2, DM), BF16), "W1": ((DM, FC), BF16), "W2": ((FC, DM), BF16),
        "HP": (SLOTS + pair + (T2, F2), BF16), "HQ": (pair + (T2, F2), BF16), "DB": ((8, FC), F32),
        "S1": ((RING, DS, F2), F32), "S2": ((FB, DM), F32),
        "K1": ((RING, DS, F2), BF16), "K2": ((RING, FB, high(DM) // TWO), BF16),
        "OUT1": ((DS, 8 * FB), BF16), "OUT2": ((F2, high(DM)), BF16),
    }
    for new, old in (("G", "A"), ("CP", "HP"), ("CQ", "HQ"), ("R1", "S1"), ("R2", "S2")):
        shapes[new] = shapes[old]
    for p, s in (("PY", "Y"), ("PD", "D")):
        shapes[p] = shapes["R" + s] = (pair + (TH, DM), F32)
        for q in ("Q1", "Q2", "RX"):
            shapes[s + q] = (SLOTS + (TH, DM), F32)
        shapes[s + "RF"] = (SLOTS + (high(TH), DM), F32)
    return [jax.ShapeDtypeStruct(*shapes[n]) for n in NAMES]


def mul(x, n):
    return x * n if isinstance(x, int) else pl.multiple_of(x * n, n)


def cp(src, dst, sem):
    return pltpu.make_async_copy(src, dst, sem)


def batch(sem, *pairs):
    return [cp(src, dst, sem.at[i]) for i, (src, dst) in enumerate(pairs)]


def start(copies):
    for t in copies:
        t.start()


def wait(copies):
    for t in copies:
        t.wait()


def move(copies):
    start(copies)
    wait(copies)


def dma(*shape):
    return pltpu.SemaphoreType.DMA(shape)


def bf(*shape):
    return pltpu.VMEM(shape, BF16)


def fl(*shape):
    return pltpu.VMEM(shape, F32)


def when(cond):
    def deco(fn):
        pl.when(cond)(fn)
    return deco


def run(n, ins, outs, isem, osem, work, done=None, posts=None, late=()):
    posts = posts or {}

    def fetch(k, s):
        return batch(isem.at[s], *ins(k, s))

    def back(k, s):
        return batch(osem.at[s], *outs(k, s))

    start(fetch(0, 0))

    def step(k, _):
        s, nxt = low(k), k + 1
        is_late = functools.reduce(jnp.logical_or, [nxt == t for t in late], False)
        more = nxt < n
        wait(fetch(k, s))

        @when(jnp.logical_and(more, jnp.logical_not(is_late)))
        def _():
            start(fetch(nxt, flip(s)))
        if done is None:
            @when(k >= TWO)
            def _():
                wait(back(k, s))
        work(k, s)
        start(back(k, s))
        for t, fn in posts.items():
            when(k == t)(fn)
        if late:
            @when(is_late)
            def _():
                start(fetch(nxt, flip(s)))
        if done is not None:
            wait(back(k, s))
            done(k, s)
        return 0

    lax.fori_loop(0, n, step, 0)
    if done is None:
        for s in BOTH:
            wait(back(s, s))


def kernel(cfg, a_own, g_own, w1, w2, bup, *refs):
    TH, DM, DS, FB = cfg
    o = dict(zip(NAMES, refs[:len(NAMES)]))
    ssem, rsem = refs[len(NAMES):]
    DH, F2, FC, HT, T2 = high(DM), TWO * FB, RING * FB, high(TH), TWO * TH
    BN, ALLT = high(DH), TWO * RING * T2
    A, G, W1, W2 = o["A"], o["G"], o["W1"], o["W2"]
    r, c, d = lax.axis_index("row"), lax.axis_index("col"), lax.axis_index("dep")
    hp, hi = low(r), high(r)
    hn, e = flip(hi), flip(d)
    g = low(r + hi)
    gn = flip(g)
    u, v, q = r + 1 - TWO * hp, RING - 1 - r, (r + TWO) % RING
    R, L, far = (c + 1) % RING, (c + RING - 1) % RING, (c + TWO) % RING
    pos_r, pos_v, pos_u, pos_q = TWO * g + hi, TWO * g + hn, TWO * gn + hi, TWO * gn + hn
    c_lo, c_hi = low(c), high(c)

    ids, counts = {}, [0, 0]

    def name(key, n=1):
        ids[key] = counts[0]
        counts[0] += n

    def rid(key):
        return ids[key]

    for nm in "AG":
        for w in ("xr0", "xl0", "u", "xr1", "xl1", "fr0", "fl0", "fr1", "fl1"):
            name(nm + w)
        for t in "01":
            for w in "cLRxy":
                name(nm + "d" + t + w)
    for s in "uv":
        name("w1" + s, TWO * RING)
        name("w2" + s, TWO)
        name("f1" + s, RING)
        name("f2" + s)
    name("w2d")
    for s in ("w1d", "s1", "s2", "k1u"):
        name(s, RING)
    name("k1d", TWO)
    name("k2", TWO)
    for s in "YD":
        for w in ("p", "r", "l", "pr", "pl"):
            name(s + w, RING)

    pending = []
    dev_e, dev_R, dev_L = {"dep": e}, {"col": R}, {"col": L}

    def dev(row, core):
        return {"row": row, "dep": core}

    class Send:
        def __init__(self, fn, n=1):
            self.fn, self.n, self.sid = fn, n, counts[1]
            counts[1] += n
            pending.append(self)

        def desc(self, j=0):
            src, dst, rsid, device = self.fn(j)
            return pltpu.make_async_remote_copy(src_ref=src, dst_ref=dst, send_sem=ssem.at[self.sid + j], recv_sem=rsem.at[rsid],
                                                device_id=device, device_id_type=MESH)

        def start(self, j=0):
            self.desc(j).start()

        def all(self):
            for j in range(self.n):
                self.start(j)

    def same(ref, rsid, device):
        return Send(lambda j: (ref, ref, rsid, device))

    def arrived(dst, rsid):
        pltpu.make_async_remote_copy(src_ref=dst, dst_ref=dst, send_sem=ssem.at[0], recv_sem=rsem.at[rsid],
                                     device_id=dev_e, device_id_type=MESH).wait_recv()

    barrier = pltpu.get_barrier_semaphore()
    peers = [dev_e, dev_R, dev_L] + [dev(t, k) for t in (u, v) for k in BOTH]
    for p in peers:
        pl.semaphore_signal(barrier, inc=1, device_id=p, device_id_type=MESH)
    pl.semaphore_wait(barrier, len(peers))

    ARR = (("A", A, a_own), ("G", G, g_own))
    ROW = (hp, flip(hp))

    def ch(X, t, col, core, part=None):
        if part is None:
            return X.at[ROW[t], col, pl.ds(mul(core, TH), TH)]
        return X.at[ROW[t], col, pl.ds(pl.multiple_of(core * TH + part * HT, HT), HT)]

    def blk(k, n):
        return pl.ds(mul(k, n), n)

    def f_block(pos, core):
        gg, ii = high(pos), low(pos)
        return blk((flip(gg) * (RING - 1) * ii + gg * (1 + ii)) * TWO + core, FB)

    def w1_src(pos, core):
        return w1.at[:, f_block(pos, core)]

    def w1_dst(dd, row, pos):
        return W1.at[blk(dd * RING + row, DS), blk(pos, FB)]

    def send_w1(tag, row, *positions):
        for pos in positions:
            for core in BOTH:
                Send(lambda j, pos=pos, core=core: (w1_src(pos, core), w1_dst(d, r, pos), rid("w1" + tag) + d * RING + pos, dev(row, core))).start()

    def w2_part(pos, half):
        return W2.at[blk(pos, FB), blk(half, DH)]

    def send_w2(tag, row):
        for core in BOTH:
            Send(lambda j, core=core: (w2.at[blk(core, FB), :], w2_part(pos_r, d), rid("w2" + tag) + d, dev(row, core))).start()

    def wait_w2(tag, pos):
        for dd in BOTH:
            arrived(w2_part(pos, dd), rid("w2" + tag) + dd)

    send_w1("v", v, pos_v, pos_r)
    send_w1("u", u, pos_u, pos_q)
    for nm, X, own in ARR:
        for w, dv in (("u", dev(u, d)), ("xr0", dev_R), ("xl0", dev_L)):
            Send(lambda j, nm=nm, X=X, own=own, w=w, dv=dv: (own, ch(X, 0, c, d), rid(nm + w), dv)).start()
    send_w2("u", u)
    send_w1("u", u, pos_r, pos_v)
    for pos in range(RING):
        Send(lambda j, pos=pos: (w1_src(pos, e), w1_dst(d, r, pos), rid("w1d") + pos, dev_e)).start()
    Send(lambda j: (w2.at[blk(e, FB), :], w2_part(pos_r, d), rid("w2d"), dev_e)).start()
    for nm, X, own in ARR:
        Send(lambda j, nm=nm, X=X, own=own: (own, ch(X, 0, c, d), rid(nm + "d0c"), dev_e)).start()

    def own_copies(b0, b1, b2, b3, sems, sems2):
        ld = batch(sems, (a_own, b0), (g_own, b1), (w2.at[blk(d, FB), :], b3),
                   *[(w1_src(pos, d), b2.at[:, blk(pos, FB)]) for pos in range(RING)])
        st = batch(sems2, (b0, ch(A, 0, c, d)), (b1, ch(G, 0, c, d)), (b3, w2_part(pos_r, d)), (b2, W1.at[blk(d * RING + r, DS), :]))
        start(ld)
        for i, t in enumerate(st):
            wait(ld[i:] if t is st[-1] else ld[i:i + 1])
            t.start()
        wait(st)

    pl.run_scoped(own_copies, bf(TH, DM), bf(TH, DM), bf(DS, FC), bf(FB, DH), dma(RING + RING), dma(RING))

    fwd, par = {}, {}
    for nm, X, _ in ARR:
        for t in BOTH:
            b = nm + "d" + str(t)
            fwd[nm, t] = [same(ch(X, t, L, d, 0), rid(nm + "fr" + str(t)), dev_R), same(ch(X, t, R, d, 1), rid(nm + "fl" + str(t)), dev_L),
                          same(ch(X, t, L, d), rid(b + "L"), dev_e), same(ch(X, t, R, d), rid(b + "R"), dev_e),
                          same(ch(X, t, far, d, 0), rid(b + "x"), dev_e), same(ch(X, t, far, d, 1), rid(b + "y"), dev_e)]
        par[nm] = [same(ch(X, 1, c, d), rid(nm + w), dv) for w, dv in (("xr1", dev_R), ("xl1", dev_L), ("d1c", dev_e))]

    def pass_on(nm, X, t):
        to_r, to_l, d_l, d_r = fwd[nm, t][:RING]
        arrived(ch(X, t, L, d), rid(nm + "xr" + str(t)))
        to_r.start()
        arrived(ch(X, t, R, d), rid(nm + "xl" + str(t)))
        to_l.start()
        d_l.start()
        d_r.start()

    def from_u(nm, X):
        arrived(ch(X, 1, c, d), rid(nm + "u"))
        for t in par[nm]:
            t.start()

    def far_in(nm, X, t):
        for part, w in zip(BOTH, ("fr", "fl")):
            arrived(ch(X, t, far, d, part), rid(nm + w + str(t)))
            fwd[nm, t][RING + part].start()

    def other_core(t, *which):
        for nm, X, _ in ARR:
            b = nm + "d" + str(t)
            for w in which:
                if w == "far":
                    for part, z in zip(BOTH, "xy"):
                        arrived(ch(X, t, far, e, part), rid(b + z))
                else:
                    arrived(ch(X, t, {"c": c, "L": L, "R": R}[w], e), rid(b + w))

    def hop(tag, row, device, *positions):
        out = []
        for pos in positions:
            out.append(Send(lambda j, pos=pos: (w1_dst(j, row, pos), w1_dst(j, row, pos), rid(tag) + low(pos) * TWO + j, device), TWO))
        return out

    f1v = hop("f1v", u, dev(v, d), pos_v, pos_r)
    f1u = hop("f1u", v, dev(u, d), pos_r, pos_v)
    q0, q1 = pl.ds(0, BN), pl.ds(BN, DM - BN)
    f2u = same(W2.at[blk(pos_v, FB), q0], rid("f2u"), dev(u, d))
    f2v = same(W2.at[blk(pos_u, FB), q1], rid("f2v"), dev(v, d))

    def w1_in(tag, row, pos):
        for dd in BOTH:
            arrived(w1_dst(dd, row, pos), rid("w1" + tag) + dd * RING + pos)

    def w1_rest(pos, tag):
        arrived(w1_dst(e, r, pos), rid("w1d") + pos)
        for j in BOTH:
            arrived(w1_dst(j, q, pos), rid(tag) + low(pos) * TWO + j)

    for pos in (pos_r, pos_v):
        w1_in("u", u, pos)
    for t in f1v:
        t.all()
    send_w2("v", v)
    send_w1("v", v, pos_q, pos_u)
    pass_on("A", A, 0)
    for pos in (pos_r, pos_v):
        w1_in("v", v, pos)
    for t in f1u:
        t.all()
    other_core(0, "c")
    arrived(w2_part(pos_r, e), rid("w2d"))
    w1_rest(pos_r, "f1v")

    RC = min(8 * RING, TH)

    def cd_block(a, gr, w1b, w2b, bias, cbuf, gbuf, h_out, dc_out, db, count_db):
        cbuf[:] = jnp.dot(a, w1b, preferred_element_type=F32)
        gbuf[:] = lax.dot_general(gr, w2b, NT, preferred_element_type=F32)

        def rows(m, acc):
            sl = blk(m, RC)
            pre = cbuf[sl, :] + bias
            sq = pre * pre
            th = jnp.tanh(GELU_K * (pre + GELU_C * pre * sq))
            half = 0.5 * (1.0 + th)
            slope = half + 0.5 * pre * (1.0 - th * th) * GELU_K * (1.0 + 3.0 * GELU_C * sq)
            dc = gbuf[sl, :] * slope
            h_out[sl, :] = (pre * half).astype(BF16)
            dc_out[sl, :] = dc.astype(BF16)
            return acc + jnp.sum(dc.reshape(RC // 8, 8, FB), axis=0)

        acc = lax.fori_loop(0, T2 // RC, rows, jnp.zeros((8, FB), F32))

        @when(count_db)
        def _():
            db[:] += acc

    def hidden(n, place, block, need, first, posts, late):
        def body(ab, gb, w1b, w2b, cbuf, gbuf, hb, cb, dbs, isem, osem, wsem):
            def weights(b):
                pos = block(b * first)[1]
                return batch(wsem.at[b], (W1.at[:, blk(pos, FB)], w1b.at[b]), (W2.at[blk(pos, FB), :], w2b.at[b]))

            def load(b):
                need(b)
                start(weights(b))

            load(0)
            dbs[:] = jnp.zeros_like(dbs)

            def ins(k, s):
                row, col, _ = place(k)
                return (A.at[row, col], ab.at[s]), (G.at[row, col], gb.at[s])

            def outs(k, s):
                row, col, _ = place(k)
                to_p, cols = block(k)[TWO:]
                at = (high(col), low(col), slice(None), cols)
                H, C = (o["HP"].at[row], o["CP"].at[row]) if to_p else (o["HQ"], o["CQ"])
                return (hb.at[s], H.at[at]), (cb.at[s], C.at[at])

            def work(k, s):
                b, pos = block(k)[:TWO]
                for t in BOTH:
                    @when(k == t * first)
                    def _():
                        wait(weights(t))
                cd_block(ab[s], gb[s], w1b[b], w2b[b], bup[:, blk(pos, FB)], cbuf, gbuf, hb.at[s], cb.at[s], dbs.at[b], place(k)[TWO])

            run(n, ins, outs, isem, osem, work, posts={k: functools.partial(fn, load) for k, fn in posts.items()}, late=late)
            move(batch(wsem.at[0], *[(dbs.at[b], o["DB"].at[:, blk(block(b * first)[1], FB)]) for b in BOTH]))

        pl.run_scoped(body, bf(TWO, T2, DM), bf(TWO, T2, DM), bf(TWO, DM, FB), bf(TWO, FB, DM), fl(T2, FB), fl(T2, FB),
                      bf(TWO, T2, FB), bf(TWO, T2, FB), fl(TWO, 8, FB), dma(TWO, TWO), dma(TWO, TWO), dma(TWO, TWO))

    five, ten = RING + 1, TWO * RING + TWO

    def place1(k):
        early = k < ten
        k5, k2 = k % five, high(k - ten) + 1
        mine = jnp.logical_and(early, k5 < RING)
        m = jnp.where(early, k5 % RING, k2)
        return jnp.where(mine, hp, flip(hp)), (c + m + high(m) * (five - TWO * m)) % RING, mine

    def block1(k):
        b = jnp.where(k < ten, k // five % TWO, low(k))
        ii = jnp.where(b == 0, hi, hn)
        return b, TWO * g + ii, True, blk(ii, FB)

    def need1(b):
        if b:
            wait_w2("v", pos_v)
            f2u.start()
            w1_rest(pos_v, "f1v")

    def post0(load):
        pass_on("G", G, 0)
        from_u("A", A)
        other_core(0, "L", "R")

    def post2(load):
        far_in("A", A, 0)
        from_u("G", G)
        far_in("G", G, 0)
        other_core(0, "far")

    def post9(load):
        pass_on("G", G, 1)
        wait_w2("u", pos_u)
        f2v.start()
        other_core(1, "L", "R")

    def post13(load):
        for nm, X, _ in ARR:
            far_in(nm, X, 1)
        other_core(1, "far")

    posts1 = {0: post0, TWO: post2, RING - 1: lambda load: other_core(1, "c"), RING: lambda load: load(1),
              five: lambda load: pass_on("A", A, 1), ten - 1: post9, ten + RING - 1: post13}
    hidden(ten + RING + TWO, place1, block1, need1, five, posts1, (1, RING - 1, RING, ten, ten + RING))

    S1, R1, S2, R2, K1, K2, OUT1, OUT2 = [o[t] for t in ("S1", "R1", "S2", "R2", "K1", "K2", "OUT1", "OUT2")]
    s1 = Send(lambda j: (S1.at[j], R1.at[j], rid("s1") + j, dev(v, d)), RING)
    s2 = Send(lambda j: (S2.at[:, blk(j, BN)], R2.at[:, blk(j, BN)], rid("s2") + j, dev(v, d)), RING)

    def dw1_cols(k, pair, first):
        j = first + (1 - TWO * first) * high(k)
        return blk(low(k) * RING + TWO * pair + j, DS)

    def grad(left, right, left_shape, right_shape, resident, out_shape, outs, done, recv=None):
        rows, width = out_shape

        def body(lb, rb, acc, ob, nb, isem, osem, wsem):
            stay = batch(wsem, resident((lb, rb)))
            start(stay)

            def ins(k, s):
                return (left(k), lb.at[s]) if right is None else (right(k), rb.at[s]),

            def work(k, s):
                @when(k == 0)
                def _():
                    wait(stay)
                x, y = (lb[s], rb[:]) if right is None else (lb[:], rb[s])
                val = lax.dot_general(x.reshape(ALLT, rows), y.reshape(ALLT, width), TN, preferred_element_type=F32)
                if recv is None:
                    ob[s] = val
                else:
                    acc[:] = val
                    ref, rsid = recv(k)
                    arrived(ref, rsid)
                    move(batch(wsem, (ref, nb)))
                    ob[s] = (acc[:] + nb[:]).astype(BF16)

            run(RING, ins, lambda k, s: ((ob.at[s], outs(k)),), isem, osem, work, done=lambda k, s: done(k, ob.at[s], wsem))

        extra = out_shape if recv else (8, BN)
        pl.run_scoped(body, bf(*left_shape), bf(*right_shape), fl(*extra), pltpu.VMEM(SLOTS + out_shape, BF16 if recv else F32), fl(*extra),
                      dma(TWO, 1), dma(TWO, 1), dma(TWO))

    PT, PTS = (TWO, RING, T2), (TWO, TWO, TWO, T2)

    def grad1(pair, first, outs, done, recv=None):
        grad(lambda k: A.at[:, :, :, dw1_cols(k, pair, first)], None, SLOTS + PT + (DS,), PTS + (F2,), lambda b: (o["CP"], b[1]),
             (DS, F2), outs, done, recv)

    def grad2(pair, outs, done, recv=None):
        grad(None, lambda k: G.at[:, :, :, blk(k, BN)], PTS + (FB,), SLOTS + PT + (BN,), lambda b: (o["HP"].at[:, :, :, :, blk(pair, FB)], b[0]),
             (FB, BN), outs, done, recv)

    grad1(hn, hp, lambda k: S1.at[k], lambda k, ob, sem: s1.start(k))

    def block2(k):
        b = k // RING
        ii = jnp.where(b == 0, hi, hn)
        return b, TWO * gn + ii, False, blk(ii, FB)

    def need2(b):
        pos = pos_q if b else pos_u
        w1_in("u", u, pos)
        w1_in("v", v, pos)
        w1_rest(pos, "f1u")
        if b:
            arrived(W2.at[blk(pos_q, FB), q1], rid("f2v"))
            arrived(W2.at[blk(pos_q, FB), q0], rid("f2u"))

    hidden(TWO * RING, lambda k: (hp, k % RING, k >= 0), block2, need2, RING, {TWO: lambda load: load(1)}, ())

    LAG = 2

    def region(s, nt, XP, XQ, PX, RX):
        Q1, Q2, RF, RR = [o[s + t] for t in ("Q1", "Q2", "RF", "RX")]
        ex = Send(lambda j: (PX.at[:, :, :, blk(j, BN)], RX.at[:, :, :, blk(j, BN)], rid(s + "p") + j, dev_e), RING)
        away = flip(c_hi)
        far_r = Send(lambda j: (Q1.at[away, blk(0, HT), blk(j, BN)], RF.at[away, :, blk(j, BN)], rid(s + "r") + j, dev_R), RING)
        far_l = Send(lambda j: (Q1.at[away, blk(1, HT), blk(j, BN)], RF.at[away, :, blk(j, BN)], rid(s + "l") + j, dev_L), RING)
        pm_r = Send(lambda j: (Q2.at[high(R), :, blk(j, BN)], RR.at[0, :, blk(j, BN)], rid(s + "pr") + j, dev_R), RING)
        pm_l = Send(lambda j: (Q2.at[high(L), :, blk(j, BN)], RR.at[1, :, blk(j, BN)], rid(s + "pl") + j, dev_L), RING)
        wshape = (BN, FC) if nt else (FC, BN)
        mine, other = blk(d, TH), blk(e, TH)

        def wsrc(j):
            return W1.at[blk(j, BN), :] if nt else W2.at[:, blk(j, BN)]

        def wdot(p_ref, q_ref, wref, shape):
            total = 0.0
            for ref, half in ((p_ref, g), (q_ref, gn)):
                x, sel = ref[:].reshape(-1, F2), blk(half, F2)
                if nt:
                    total += lax.dot_general(x, wref[:, sel], NT, preferred_element_type=F32)
                else:
                    total += jnp.dot(x, wref[sel, :], preferred_element_type=F32)
            return total.reshape(shape)

        def first(lop, loq, lfp, lfq, wb, ob, ab, qb, wsem, lsem, osem):
            lds = batch(lsem, (XP.at[hp, :, :, other], lop), (XQ.at[:, :, other], loq), (XP.at[hp, :, c_lo, mine], lfp), (XQ.at[:, c_lo, mine], lfq))

            def wcp(j):
                return batch(wsem.at[j % RING], (wsrc(j), wb.at[j % RING]))

            start(wcp(0) + lds)
            wait(lds)

            def step(j, _):
                o1 = batch(osem, (ob, PX.at[:, :, :, blk(j, BN)]))

                @when(j < RING)
                def _():
                    wait(wcp(j))

                    @when(j < RING - 1)
                    def _():
                        start(wcp(j + 1))
                    ob[:] = wdot(lop, loq, wb.at[j % RING], (TWO, TWO, TH, BN))
                    start(o1)

                @when(j >= LAG)
                def _():
                    k = j - LAG
                    arrived(RX.at[:, :, :, blk(k, BN)], rid(s + "p") + k)
                    add = batch(lsem, (RX.at[:, c_lo, :, blk(k, BN)], ab))
                    start(add)
                    qb[:] = wdot(lfp, lfq, wb.at[k % RING], (TWO, TH, BN))
                    wait(add)
                    qb[:] += ab[:]

                @when(j < RING)
                def _():
                    wait(o1)
                    ex.start(j)

                @when(j >= LAG)
                def _():
                    k = j - LAG
                    move(batch(lsem, (qb, Q1.at[:, :, blk(k, BN)])))
                    far_r.start(k)
                    far_l.start(k)
                return 0

            lax.fori_loop(0, RING + LAG, step, 0)

        def second(lp, lq, wb, ab, fb, ob, lsem, isem, osem):
            lds = batch(lsem, (XP.at[hp, :, flip(c_lo), mine], lp), (XQ.at[:, flip(c_lo), mine], lq))
            start(lds)

            def need(k):
                arrived(RF.at[high(R), :, blk(k, BN)], rid(s + "r") + k)
                arrived(RF.at[high(L), :, blk(k, BN)], rid(s + "l") + k)

            for k in range(RING):
                need(k)
            wait(lds)

            def ins(k, sl):
                return (wsrc(k), wb.at[sl]), (RX.at[:, flip(c_lo), :, blk(k, BN)], ab.at[sl]), (RF.at[:, :, blk(k, BN)], fb.at[sl])

            def work(k, sl):
                ob[sl] = wdot(lp, lq, wb.at[sl], (TWO, TH, BN)) + ab[sl]
                for col, part in ((R, 0), (L, 1)):
                    ob[sl, high(col), part * HT:(part + 1) * HT, :] += fb[sl, high(col)]

            def done(k, sl):
                pm_r.start(k)
                pm_l.start(k)

            run(RING, ins, lambda k, sl: ((ob.at[sl], Q2.at[:, :, blk(k, BN)]),), isem, osem, work, done=done)

        def run_first():
            pl.run_scoped(first, bf(TWO, TWO, TH, F2), bf(TWO, TWO, TH, F2), bf(TWO, TH, F2), bf(TWO, TH, F2), bf(RING, *wshape),
                          fl(TWO, TWO, TH, BN), fl(TWO, TH, BN), fl(TWO, TH, BN), dma(RING, 1), dma(RING), dma(1))

        def run_second():
            pl.run_scoped(second, bf(TWO, TH, F2), bf(TWO, TH, F2), bf(TWO, *wshape), fl(TWO, TWO, TH, BN), fl(TWO, TWO, HT, BN),
                          fl(TWO, TWO, TH, BN), dma(TWO), dma(TWO, RING), dma(TWO, 1))

        def finish():
            for j in range(RING):
                arrived(RR.at[0, :, blk(j, BN)], rid(s + "pr") + j)
                arrived(RR.at[1, :, blk(j, BN)], rid(s + "pl") + j)
        return run_first, run_second, finish

    y1, y2, y3 = region("Y", False, o["HP"], o["HQ"], o["PY"], o["RY"])
    d1, d2, d3 = region("D", True, o["CP"], o["CQ"], o["PD"], o["RD"])
    y1()
    d1()
    y2()
    grad2(hn, lambda k: S2.at[:, blk(k, BN)], lambda k, ob, sem: s2.start(k))
    d2()

    def piece(ii):
        return slice(ii * FB, (ii + 1) * FB)

    k1u = [Send(lambda m, ii=ii: (K1.at[m, :, piece(ii)], OUT1.at[:, f_block(TWO * g + ii, d)], rid("k1u") + d * TWO + ii, dev(u, m)), TWO)
           for ii in BOTH]
    k1d = [Send(lambda m, ii=ii: (K1.at[TWO + e, :, piece(ii)], OUT1.at[:, f_block(TWO * g + ii, d)], rid("k1d") + ii, dev_e)) for ii in BOTH]

    def done1(k, ob, sem):
        @when(k < TWO)
        def _():
            for t in k1u:
                t.start(k)

        @when(k == TWO + e)
        def _():
            for t in k1d:
                t.start()

        @when(k == TWO + d)
        def _():
            move(batch(sem, *[(ob.at[:, piece(ii)], OUT1.at[:, f_block(TWO * g + ii, d)]) for ii in BOTH]))

    def out2_at(core, jj):
        return OUT2.at[blk(core, FB), blk(jj, BN)]

    k2 = Send(lambda jj: (K2.at[TWO * e + jj], out2_at(d, jj), rid("k2") + jj, dev_e), TWO)

    def done2(k, ob, sem):
        @when(high(k) == d)
        def _():
            move(batch(sem, (ob, out2_at(d, low(k)))))

        @when(high(k) == e)
        def _():
            k2.start(low(k))

    grad1(hi, flip(hp), lambda k: K1.at[k], done1, lambda k: (R1.at[k], rid("s1") + k))
    grad2(hi, lambda k: K2.at[k], done2, lambda k: (R2.at[:, blk(k, BN)], rid("s2") + k))

    y3()
    d3()
    for ii in BOTH:
        for dd in BOTH:
            arrived(OUT1.at[:, f_block(TWO * gn + ii, dd)], rid("k1u") + dd * TWO + ii)
        arrived(OUT1.at[:, f_block(TWO * g + ii, e)], rid("k1d") + ii)
        arrived(out2_at(e, ii), rid("k2") + ii)
    for t in pending:
        for j in range(t.n):
            t.desc(j).wait_send()
    assert tuple(counts) == SEMS, counts


SEMS = (129, 129)


def solution(mesh):
    nr, nc, nd = mesh.shape["row"], mesh.shape["col"], mesh.shape["dep"]
    assert nr == 4 and nc == 4 and nd == 2
    tok_spec = P(("part", "row", "col"), "dep")
    vec_dep = P("dep")
    part_dep = P(("part", "dep"))
    in_specs = (tok_spec, vec_dep, vec_dep, P(("dep", "row"), "col"), P("col"), P(("col", "row"), "dep"), vec_dep, tok_spec)
    out_specs = (tok_spec, tok_spec, P(("part", "dep", "row"), "col"), P(("part", "col")), P(("part", "col", "row"), "dep"), part_dep, part_dep, part_dep)

    def swap(t):
        return lax.ppermute(t, "dep", [(0, 1), (1, 0)])

    def xor(t, axis, m):
        return lax.ppermute(t, axis, [(i, i ^ m) for i in range(4)])

    def local_step(x_in, ln_scale, ln_shift, w_up, b_up, w_down, b_down, y_grad):
        d, c = lax.axis_index("dep"), lax.axis_index("col")
        th, dhalf = x_in.shape[0] // 2, x_in.shape[1]
        dm, ds_, fb = 2 * dhalf, w_up.shape[0], w_up.shape[1] // 8
        lo = d == 0

        def merge_last(mine, other):
            return jnp.where(lo, jnp.concatenate([mine, other], axis=-1), jnp.concatenate([other, mine], axis=-1))

        def tok_half(t, which):
            return lax.dynamic_slice_in_dim(t, which * th, th, 0)

        xo = merge_last(tok_half(x_in, d), swap(tok_half(x_in, 1 - d)))
        go = merge_last(tok_half(y_grad, d), swap(tok_half(y_grad, 1 - d)))
        vecs = jnp.stack([ln_scale, ln_shift, b_down.astype(F32)])
        vecs = merge_last(vecs, swap(vecs))
        gamma, beta, bdn = vecs[0], vecs[1], vecs[2]
        x_float = xo.astype(F32)
        mean_row = jnp.sum(x_float, axis=1, keepdims=True) / dm
        var_row = jnp.sum(x_float * x_float, axis=1, keepdims=True) / dm - mean_row * mean_row
        inv_std = lax.rsqrt(var_row + LN_EPS)
        x_hat = (x_float - mean_row) * inv_std
        ao = (x_hat * gamma + beta).astype(BF16)
        b3 = lax.dynamic_index_in_dim(b_up.reshape(4, 2, fb), d, 1, keepdims=False).astype(F32)
        bup = jnp.concatenate([b3[k] for k in (0, 3, 1, 2)]).reshape(1, 4 * fb)

        cfg = (th, dm, ds_, fb)
        outs = pl.pallas_call(
            functools.partial(kernel, cfg),
            name="mlp_layer",
            out_shape=buffers(*cfg),
            in_specs=[pl.BlockSpec(memory_space=pl.ANY)] * 4 + [pl.BlockSpec(memory_space=pltpu.VMEM)],
            out_specs=[pl.BlockSpec(memory_space=pl.ANY)] * len(NAMES),
            scratch_shapes=[dma(SEMS[0]), dma(SEMS[1])],
            compiler_params=pltpu.CompilerParams(collective_id=0, has_side_effects=True, vmem_limit_bytes=62 * 1024 * 1024),
        )(ao, go, w_up, w_down, bup)
        o = dict(zip(NAMES, outs))

        def total(s):
            own = lax.dynamic_index_in_dim(o[s + "Q1"], c // 2, 0, keepdims=False)
            return own + o[s + "RX"][0] + o[s + "RX"][1]

        def to_out(t):
            mine = lax.dynamic_slice_in_dim(t, d * dhalf, dhalf, 1)
            oth = swap(lax.dynamic_slice_in_dim(t, (1 - d) * dhalf, dhalf, 1))
            return jnp.where(lo, jnp.concatenate([mine, oth], axis=0), jnp.concatenate([oth, mine], axis=0))

        y_out = to_out((x_float + total("Y") + bdn).astype(BF16))
        norm_grad = total("D")
        g_float = go.astype(F32)
        val = norm_grad * gamma
        m1 = jnp.sum(val, axis=1, keepdims=True) / dm
        m2 = jnp.sum(val * x_hat, axis=1, keepdims=True) / dm
        x_grad = to_out((g_float + inv_std * (val - m1 - x_hat * m2)).astype(BF16))

        sums = jnp.stack([jnp.sum(norm_grad * x_hat, axis=0), jnp.sum(norm_grad, axis=0), jnp.sum(g_float, axis=0)])
        s_m = lax.dynamic_slice_in_dim(sums, d * dhalf, dhalf, 1)
        sums = s_m + swap(lax.dynamic_slice_in_dim(sums, (1 - d) * dhalf, dhalf, 1))
        for axis, m in (("row", 1), ("row", 3), ("col", 1), ("col", 3)):
            sums = sums + xor(sums, axis, m)

        db4 = jnp.sum(o["DB"], axis=0).reshape(4, fb)
        db = jnp.stack([db4[k] for k in (0, 2, 3, 1)])
        for m in (1, 3):
            db = db + xor(db, "row", m)
        db_o = swap(db)
        b_up_grad = jnp.where(lo, jnp.stack([db, db_o], axis=1), jnp.stack([db_o, db], axis=1)).reshape(8 * fb)
        return (y_out, x_grad, o["OUT1"], b_up_grad, o["OUT2"], sums[2], sums[0], sums[1])

    return jax.shard_map(local_step, mesh=mesh, in_specs=in_specs, out_specs=out_specs, check_vma=False)
```

time: 1560 us -> 759 us (0.49)
  waiting for transfers between devices: 1130 us -> 5.56 us
  Pallas kernels: 0 us -> 687 us
  matrix products: 261 us -> 0 us
  blocking collectives: 92.8 us -> 0 us
  other arithmetic: 50.3 us -> 28.5 us
    pallas_call x0 -> x1, Pallas kernels: none -> 687 us  [local_step(): pl.pallas_call(functools.partial(kernel, cfg), name='mlp_layer', out_shap...]
    reduce_scatter x6 -> x0, waiting for transfers between devices: 669 us -> none  [the longest x1 276 us: local_step(): lax.psum_scatter(w_down_part, 'row', scatter_dimension=0, tiled=True)]
    all_gather x6 -> x0, waiting for transfers between devices: 461 us -> none  [the longest x1 155 us: local_step(): w_up_full = lax.all_gather(w_up, 'row', axis=0, tiled=True)]
    dot_general x6 -> x0, matrix products: 261 us -> none  [the longest x1 43.8 us: local_step(): jnp.einsum('td,tf->df', normed_full, pre_full, preferred_element_type=jnp...]
    psum x4 -> x0, blocking collectives: 92.8 us -> none  [the longest x1 58.4 us: local_step(): b_down_grad = lax.psum(jnp.sum(g_float, axis=0), ('row', 'col'))]
    reduce_sum x3 -> x4, other arithmetic: 30.7 us -> 11 us  [the longest x1 6.05 us: local_step(): jnp.sum(norm_grad, axis=0)]
  transfers between devices with their start and end apart: 12 -> 13, of which waited for: 10 -> 5; matrix products, arithmetic and copies ran while one was open for 18% -> 3% of each run, Pallas kernels for 0% -> 0%
where the time goes in v2:
time: 759 us; the launch traced here: 749 us
  Pallas kernels  687 us (91%)
  other arithmetic  28.5 us (4%)
  starting transfers between devices  13.5 us (2%)
  local copies, waits for them, and re-layouts  13.4 us (2%)
    pallas_call x1, Pallas kernels, local_step(): pl.pallas_call(functools.partial(kernel, cfg), name='mlp_layer', out_shap...  687 us
  transfers between devices with their start and end apart: 13, of which 5 were waited for; matrix products, arithmetic and copies ran while one was open for 3% of the time, Pallas kernels for 0%

profile of v2, /device:TPU:97, one launch (start us, length us, event | category | flops | bytes accessed | tf_op | source)
XLA Modules:
  0.0 749.0 jit_solution(15568180021368040592)
XLA Ops:
  0.6 0.7 stack.58
  1.3 0.7 pad_maximum_fusion.1
  2.1 2.1 collective-permute-start.1
  4.2 2.9 constant_dynamic-slice_fusion.7
  7.2 1.1 constant_dynamic-slice_fusion.5
  8.8 0.6 pad_maximum_fusion.2
  9.8 1.0 convert_reduce_fusion
  11.2 3.1 convert_reduce_fusion.1
  14.3 2.2 fusion.7.a_own
  16.5 686.9 %mlp_layer.1 = (bf16[2,4,512,4096]{3,2,1,0:T(8,128)(2,1)}, bf16[2,4,512,4096]{3,2,1,0:T(8,128)(2,1)}, bf16[4096,2048]{1,0:T(8,128)(2,1)}, bf16[2048,4096]{1,0:T(...) custom-call(bf16[256,4096]{1,0:T(8,128)(2,1)} %fusion.7.a_own, ...), custom_call_target="tpu_custom_call" | custom-call | tf_op jit(solution)/shard_map/mlp_layer/pallas_call | solution.py:758
  703.4 0.9 reduce_sum.76
  704.8 6.1 fusion.18
  710.9 1.3 slice-done.1
  712.2 5.7 fusion.11
  718.9 0.6 copy-done
  719.5 2.7 fusion
  722.2 1.2 collective-permute-start.9
  723.4 2.4 collective-permute-start.6
  725.9 1.3 collective-permute-start.10
  727.3 1.5 collective-permute-start.4
  728.8 1.1 collective-permute-done.10
  730.1 2.5 collective-permute-start.7
  732.7 0.8 collective-permute-done.7
  733.5 0.5 collective-permute-start.12
  734.1 0.6 copy.16
  734.7 2.9 collective-permute-done.12
  737.6 0.6 fusion.20
  738.2 2.3 maximum_select_fusion.2
  740.6 2.3 maximum_select_fusion.3
  742.9 2.1 copy.19
  745.0 1.6 copy-done.3
  746.6 2.0 copy.20
  (59 shorter events, 3.3 us)
Async XLA Ops:
  2.1 7.3 collective-permute-start.1
  4.2 3.0 copy-start.5
  4.2 4.5 copy-start.8
  4.2 5.2 copy-start.6
  4.2 5.2 copy-start.7
  7.1 2.7 collective-permute-start
  8.3 2.9 collective-permute-start.2
  9.8 6.8 copy-start.1
  704.3 19.1 %collective-permute-start.5 = (f32[4,512]{1,0:T(4,128)S(1)}, f32[4,512]{1,0:T(4,128)S(1)}, u32[]{:S(2)}, u32[]{:S(2)}) collective-permute-start(f32[4,512]{1,0:T(4,128)S(1)} %pad_maximum_fusion.3), channel_id=1, source_target_pairs={{0,8},{8,0},{16,24},{24,16},{1,9},{9,1},{17,25},{25,17},{2,10},{10... | collective-permute-start | bytes 24584 | tf_op jit(solution)/shard_map/ppermute | solution.py:729
  704.8 6.1 slice-start
  704.8 6.1 copy-start.2
  704.8 7.4 slice-start.1
  717.9 1.6 copy-start
  718.0 4.2 collective-permute-start.8
  718.6 19.7 %collective-permute-start.3 = (bf16[256,2048]{1,0:T(8,128)(2,1)S(1)}, bf16[256,2048]{1,0:T(8,128)(2,1)S(1)}, u32[]{:S(2)}, u32[]{:S(2)}) collective-permute-start(bf16[256,2048]{1,0:T(8,128)(2,1)S(1)} %get-tuple-element.35), channel_id=1, source_target_pairs={{0,1},{1,0},{2,3},{3,2},{4,5},{5,4},{6,7},{7,6},{8,9},{9,8},{10,11... | collective-permute-start | bytes 3145736 | tf_op jit(solution)/shard_map/ppermute | solution.py:726
  722.2 3.6 collective-permute-start.9
  723.4 6.7 collective-permute-start.6
  725.9 4.1 collective-permute-start.10
  727.3 13.2 %collective-permute-start.4 = (bf16[256,2048]{1,0:T(8,128)(2,1)S(1)}, bf16[256,2048]{1,0:T(8,128)(2,1)S(1)}, u32[]{:S(2)}, u32[]{:S(2)}) collective-permute-start(bf16[256,2048]{1,0:T(8,128)(2,1)S(1)} %get-tuple-element.32), channel_id=1, source_target_pairs={{0,1},{1,0},{2,3},{3,2},{4,5},{5,4},{6,7},{7,6},{8,9},{9,8},{10,11... | collective-permute-start | bytes 3145736 | tf_op jit(solution)/shard_map/ppermute | solution.py:726
  730.0 3.5 collective-permute-start.11
  730.1 3.4 collective-permute-start.7
  733.5 4.1 collective-permute-start.12
  738.2 4.6 copy-start.4
  742.9 3.7 copy-start.3

commit v3 on v2

--- a/solution.py
+++ b/solution.py
@@ -16,8 +16,8 @@
 
 NAMES = ("A", "G", "W1", "W2", "HP", "HQ", "CP", "CQ", "DB",
          "PY", "RY", "YQ1", "YQ2", "YRF", "YRX", "PD", "RD", "DQ1", "DQ2", "DRF", "DRX",
-         "S1", "R1", "S2", "R2", "K1", "K2", "OUT1", "OUT2")
-TWO, RING = 2, 4
+         "S1", "R1", "S2", "R2", "K1", "K2", "OUT1", "OUT2", "XF", "GF", "PV", "YO", "XO", "OUTY", "OUTX", "BG", "SO")
+TWO, RING, STAGES = 2, 4, 5
 BOTH, SLOTS = (0, 1), (2,)
 NT = (((1,), (1,)), ((), ()))
 TN = (((0,), (0,)), ((), ()))
@@ -44,6 +44,9 @@
         "S1": ((RING, DS, F2), F32), "S2": ((FB, DM), F32),
         "K1": ((RING, DS, F2), BF16), "K2": ((RING, FB, high(DM) // TWO), BF16),
         "OUT1": ((DS, 8 * FB), BF16), "OUT2": ((F2, high(DM)), BF16),
+        "XF": ((TH, DM), BF16), "GF": ((TH, DM), BF16), "PV": ((8, DM), F32), "YO": ((RING, TH, high(DM) // TWO), BF16),
+        "XO": ((TH, high(DM)), BF16), "OUTY": ((T2, high(DM)), BF16), "OUTX": ((T2, high(DM)), BF16),
+        "BG": (SLOTS + (8, FC), F32), "SO": ((8, high(DM)), F32),
     }
     for new, old in (("G", "A"), ("CP", "HP"), ("CQ", "HQ"), ("R1", "S1"), ("R2", "S2")):
         shapes[new] = shapes[old]
@@ -143,10 +146,10 @@
             wait(back(s, s))
 
 
-def kernel(cfg, a_own, g_own, w1, w2, bup, *refs):
+def kernel(cfg, x_in, g_in, w1, w2, vec, bup, *refs):
     TH, DM, DS, FB = cfg
     o = dict(zip(NAMES, refs[:len(NAMES)]))
-    ssem, rsem = refs[len(NAMES):]
+    ssem, rsem, sums, sums_in, db, db_in = refs[len(NAMES):]
     DH, F2, FC, HT, T2 = high(DM), TWO * FB, RING * FB, high(TH), TWO * TH
     BN, ALLT = high(DH), TWO * RING * T2
     A, G, W1, W2 = o["A"], o["G"], o["W1"], o["W2"]
@@ -180,7 +183,11 @@
         name("w2" + s, TWO)
         name("f1" + s, RING)
         name("f2" + s)
-    name("w2d")
+    for s in ("w2d", "xf", "gf", "pv", "xo", "bg"):
+        name(s)
+    name("yo", TWO)
+    name("bf", TWO)
+    name("sum", STAGES)
     for s in ("w1d", "s1", "s2", "k1u"):
         name(s, RING)
     name("k1d", TWO)
@@ -226,7 +233,7 @@
         pl.semaphore_signal(barrier, inc=1, device_id=p, device_id_type=MESH)
     pl.semaphore_wait(barrier, len(peers))
 
-    ARR = (("A", A, a_own), ("G", G, g_own))
+    ARR = (("A", A), ("G", G))
     ROW = (hp, flip(hp))
 
     def ch(X, t, col, core, part=None):
@@ -263,33 +270,64 @@
         for dd in BOTH:
             arrived(w2_part(pos, dd), rid("w2" + tag) + dd)
 
+    XF, GF, PV = o["XF"], o["GF"], o["PV"]
+    Send(lambda j: (g_in.at[blk(e, TH), :], GF.at[:, blk(d, DH)], rid("gf"), dev_e)).start()
+    Send(lambda j: (x_in.at[blk(e, TH), :], XF.at[:, blk(d, DH)], rid("xf"), dev_e)).start()
+    Send(lambda j: (vec, PV.at[:, blk(d, DH)], rid("pv"), dev_e)).start()
     send_w1("v", v, pos_v, pos_r)
     send_w1("u", u, pos_u, pos_q)
-    for nm, X, own in ARR:
-        for w, dv in (("u", dev(u, d)), ("xr0", dev_R), ("xl0", dev_L)):
-            Send(lambda j, nm=nm, X=X, own=own, w=w, dv=dv: (own, ch(X, 0, c, d), rid(nm + w), dv)).start()
-    send_w2("u", u)
-    send_w1("u", u, pos_r, pos_v)
+
+    RL = min(8 * RING, TH)
+
+    def stats(x):
+        mean = jnp.sum(x, axis=1, keepdims=True) / DM
+        var = jnp.sum(x * x, axis=1, keepdims=True) / DM - mean * mean
+        inv_std = lax.rsqrt(var + LN_EPS)
+        return inv_std, (x - mean) * inv_std
+
+    def send_own(nm, X):
+        for w, dv in (("u", dev(u, d)), ("xr0", dev_R), ("xl0", dev_L), ("d0c", dev_e)):
+            Send(lambda j, w=w, dv=dv: (ch(X, 0, c, d), ch(X, 0, c, d), rid(nm + w), dv)).start()
+
+    def own_part(xb, gb, ab, vb, b2, b3, sems, sems2):
+        mine, other = blk(d, DH), blk(e, DH)
+        ld = batch(sems, (g_in.at[blk(d, TH), :], gb.at[:, mine]), (x_in.at[blk(d, TH), :], xb.at[:, mine]), (vec, vb.at[:, mine]))
+        wl = batch(sems2, (w2.at[blk(d, FB), :], b3), *[(w1_src(pos, d), b2.at[:, blk(pos, FB)]) for pos in range(RING)])
+        start(ld + wl)
+        wait(ld)
+        got = batch(sems, (GF.at[:, other], gb.at[:, other]), (XF.at[:, other], xb.at[:, other]), (PV.at[:, other], vb.at[:, other]))
+        for t, ref, w in zip(got, (GF, XF, PV), ("gf", "xf", "pv")):
+            arrived(ref.at[:, other], rid(w))
+            t.start()
+        wait(got[:1])
+        move(batch(sems, (gb, ch(G, 0, c, d))))
+        wait(got[1:])
+        keep = batch(sems, (xb.at[:, mine], XF.at[:, mine]), (vb.at[:, mine], PV.at[:, mine]))
+        start(keep)
+        scale, shift = vb[0:1, :], vb[1:TWO, :]
+
+        def rows(m, _):
+            sl = blk(m, RL)
+            ab[sl, :] = (stats(xb[sl, :].astype(F32))[1] * scale + shift).astype(BF16)
+            return 0
+
+        lax.fori_loop(0, TH // RL, rows, 0)
+        wait(keep)
+        send_own("G", G)
+        move(batch(sems, (ab, ch(A, 0, c, d))))
+        send_own("A", A)
+        send_w2("u", u)
+        send_w1("u", u, pos_r, pos_v)
+        wait(wl)
+        move(batch(sems2, (b3, w2_part(pos_r, d)), (b2, W1.at[blk(d * RING + r, DS), :])))
+
+    pl.run_scoped(own_part, bf(TH, DM), bf(TH, DM), bf(TH, DM), fl(8, DM), bf(DS, FC), bf(FB, DH), dma(RING), dma(RING + 1))
     for pos in range(RING):
         Send(lambda j, pos=pos: (w1_src(pos, e), w1_dst(d, r, pos), rid("w1d") + pos, dev_e)).start()
     Send(lambda j: (w2.at[blk(e, FB), :], w2_part(pos_r, d), rid("w2d"), dev_e)).start()
-    for nm, X, own in ARR:
-        Send(lambda j, nm=nm, X=X, own=own: (own, ch(X, 0, c, d), rid(nm + "d0c"), dev_e)).start()
-
-    def own_copies(b0, b1, b2, b3, sems, sems2):
-        ld = batch(sems, (a_own, b0), (g_own, b1), (w2.at[blk(d, FB), :], b3),
-                   *[(w1_src(pos, d), b2.at[:, blk(pos, FB)]) for pos in range(RING)])
-        st = batch(sems2, (b0, ch(A, 0, c, d)), (b1, ch(G, 0, c, d)), (b3, w2_part(pos_r, d)), (b2, W1.at[blk(d * RING + r, DS), :]))
-        start(ld)
-        for i, t in enumerate(st):
-            wait(ld[i:] if t is st[-1] else ld[i:i + 1])
-            t.start()
-        wait(st)
-
-    pl.run_scoped(own_copies, bf(TH, DM), bf(TH, DM), bf(DS, FC), bf(FB, DH), dma(RING + RING), dma(RING))
 
     fwd, par = {}, {}
-    for nm, X, _ in ARR:
+    for nm, X in ARR:
         for t in BOTH:
             b = nm + "d" + str(t)
             fwd[nm, t] = [same(ch(X, t, L, d, 0), rid(nm + "fr" + str(t)), dev_R), same(ch(X, t, R, d, 1), rid(nm + "fl" + str(t)), dev_L),
@@ -317,7 +355,7 @@
             fwd[nm, t][RING + part].start()
 
     def other_core(t, *which):
-        for nm, X, _ in ARR:
+        for nm, X in ARR:
             b = nm + "d" + str(t)
             for w in which:
                 if w == "far":
@@ -353,7 +391,7 @@
         t.all()
     send_w2("v", v)
     send_w1("v", v, pos_q, pos_u)
-    pass_on("A", A, 0)
+    pass_on("G", G, 0)
     for pos in (pos_r, pos_v):
         w1_in("v", v, pos)
     for t in f1u:
@@ -445,29 +483,29 @@
             w1_rest(pos_v, "f1v")
 
     def post0(load):
-        pass_on("G", G, 0)
+        pass_on("A", A, 0)
+        from_u("G", G)
+        other_core(0, "L", "R")
+
+    def post2(load):
+        far_in("G", G, 0)
         from_u("A", A)
-        other_core(0, "L", "R")
-
-    def post2(load):
         far_in("A", A, 0)
-        from_u("G", G)
-        far_in("G", G, 0)
         other_core(0, "far")
 
     def post9(load):
-        pass_on("G", G, 1)
+        pass_on("A", A, 1)
         wait_w2("u", pos_u)
         f2v.start()
         other_core(1, "L", "R")
 
     def post13(load):
-        for nm, X, _ in ARR:
-            far_in(nm, X, 1)
+        far_in("G", G, 1)
+        far_in("A", A, 1)
         other_core(1, "far")
 
     posts1 = {0: post0, TWO: post2, RING - 1: lambda load: other_core(1, "c"), RING: lambda load: load(1),
-              five: lambda load: pass_on("A", A, 1), ten - 1: post9, ten + RING - 1: post13}
+              five: lambda load: pass_on("G", G, 1), ten - 1: post9, ten + RING - 1: post13}
     hidden(ten + RING + TWO, place1, block1, need1, five, posts1, (1, RING - 1, RING, ten, ten + RING))
 
     S1, R1, S2, R2, K1, K2, OUT1, OUT2 = [o[t] for t in ("S1", "R1", "S2", "R2", "K1", "K2", "OUT1", "OUT2")]
@@ -644,19 +682,18 @@
             pl.run_scoped(second, bf(TWO, TH, F2), bf(TWO, TH, F2), bf(TWO, *wshape), fl(TWO, TWO, TH, BN), fl(TWO, TWO, HT, BN),
                           fl(TWO, TWO, TH, BN), dma(TWO), dma(TWO, RING), dma(TWO, 1))
 
-        def finish():
-            for j in range(RING):
-                arrived(RR.at[0, :, blk(j, BN)], rid(s + "pr") + j)
-                arrived(RR.at[1, :, blk(j, BN)], rid(s + "pl") + j)
-        return run_first, run_second, finish
-
-    y1, y2, y3 = region("Y", False, o["HP"], o["HQ"], o["PY"], o["RY"])
-    d1, d2, d3 = region("D", True, o["CP"], o["CQ"], o["PD"], o["RD"])
+        def come(j):
+            arrived(RR.at[0, :, blk(j, BN)], rid(s + "pr") + j)
+            arrived(RR.at[1, :, blk(j, BN)], rid(s + "pl") + j)
+        return run_first, run_second, come
+
+    y1, y2, y_come = region("Y", False, o["HP"], o["HQ"], o["PY"], o["RY"])
+    d1, d2, d_come = region("D", True, o["CP"], o["CQ"], o["PD"], o["RD"])
+    d1()
     y1()
-    d1()
+    d2()
+    grad2(hn, lambda k: S2.at[:, blk(k, BN)], lambda k, ob, sem: s2.start(k))
     y2()
-    grad2(hn, lambda k: S2.at[:, blk(k, BN)], lambda k, ob, sem: s2.start(k))
-    d2()
 
     def piece(ii):
         return slice(ii * FB, (ii + 1) * FB)
@@ -695,11 +732,122 @@
             k2.start(low(k))
 
     grad1(hi, flip(hp), lambda k: K1.at[k], done1, lambda k: (R1.at[k], rid("s1") + k))
+
+    RX_, OUTX, XO, OUTY, YO, BG, SO = [o[t] for t in ("DRX", "OUTX", "XO", "OUTY", "YO", "BG", "SO")]
+    xo = Send(lambda j: (XO, OUTX.at[blk(d, TH), :], rid("xo"), dev_e))
+    stages = [dev_e, dev(u, d), dev(v, d), {"col": c + 1 - TWO * c_lo}, {"col": RING - 1 - c}]
+    assert len(stages) == STAGES
+    sum_send = [Send(lambda j, k=k, dv=dv: (sums.at[k], sums_in.at[k], rid("sum") + k, dv))
+                for k, dv in enumerate(stages)]
+    bsend = [Send(lambda j, k=k, dv=dv: (db.at[k], db_in.at[k], rid("bf") + k, dv)) for k, dv in enumerate((dev(u, d), dev(v, d)))]
+    bg = Send(lambda j: (BG.at[d], BG.at[d], rid("bg"), dev_e))
+
+    def finish_dx(q1b, rlb, rrb, xb, gb, vb, xob, acc, dbb, isem, osem, wsem):
+        RB = min(8 * RING, high(TH))
+        par_ = batch(wsem, (PV, vb), (o["DB"], dbb))
+        start(par_)
+        for j in range(RING):
+            d_come(j)
+        acc[:] = jnp.zeros_like(acc)
+
+        def ins(k, s):
+            rows = blk(k, RB)
+            return ((o["DQ1"].at[c_hi, rows], q1b.at[s]), (RX_.at[0, rows], rlb.at[s]), (RX_.at[1, rows], rrb.at[s]), (XF.at[rows, :], xb.at[s]),
+                    (G.at[hp, c, pl.ds(pl.multiple_of(d * TH + k * RB, RB), RB), :], gb.at[s]))
+
+        def outs(k, s):
+            return ((xob.at[s, :, blk(d, DH)], OUTX.at[pl.ds(pl.multiple_of(d * TH + k * RB, RB), RB), :]),
+                    (xob.at[s, :, blk(e, DH)], XO.at[blk(k, RB), :]))
+
+        def fold(x):
+            return jnp.sum(x.reshape(RB // 8, 8, DM), axis=0)
+
+        def work(k, s):
+            @when(k == 0)
+            def _():
+                wait(par_)
+            da = q1b[s] + rlb[s] + rrb[s]
+            inv_std, xhat = stats(xb[s].astype(F32))
+            gr = gb[s].astype(F32)
+            val = da * vb[0:1, :]
+            m1 = jnp.sum(val, axis=1, keepdims=True) / DM
+            m2 = jnp.sum(val * xhat, axis=1, keepdims=True) / DM
+            xob[s] = (gr + inv_std * (val - m1 - xhat * m2)).astype(BF16)
+            for i, t in enumerate((da * xhat, da, gr)):
+                acc[i] += fold(t)
+
+        run(TH // RB, ins, outs, isem, osem, work)
+        xo.start()
+        for i in range(RING - 1):
+            row = jnp.sum(acc[i], axis=0, keepdims=True)
+            acc[i, 0:1, :] = row
+        for i in range(RING - 1):
+            sums[STAGES, i:i + 1, :] = acc[i, 0:1, blk(d, DH)]
+            sums[0, i:i + 1, :] = acc[i, 0:1, blk(e, DH)]
+        db[0, 0:1, :] = jnp.sum(dbb[:], axis=0, keepdims=True)
+        cur = sums[STAGES]
+        cur_b = db[0]
+        for k in range(STAGES):
+            if k:
+                sums[k] = cur
+            sum_send[k].start()
+            if k in (1, TWO):
+                db[k - 1] = cur_b
+                bsend[k - 1].start()
+            arrived(sums_in.at[k], rid("sum") + k)
+            cur = cur + sums_in[k]
+            if k in (1, TWO):
+                arrived(db_in.at[k - 1], rid("bf") + k - 1)
+                cur_b = cur_b + db_in[k - 1]
+        sums[STAGES] = cur
+        db[TWO] = cur_b
+        move(batch(wsem, (sums.at[STAGES], SO), (db.at[TWO], BG.at[d])))
+        bg.start()
+
+    def dx_all():
+        RB = min(8 * RING, high(TH))
+        pl.run_scoped(finish_dx, fl(TWO, RB, DM), fl(TWO, RB, DM), fl(TWO, RB, DM), bf(TWO, RB, DM), bf(TWO, RB, DM), fl(8, DM),
+                      bf(TWO, RB, DM), fl(RING - 1, 8, DM), fl(8, FC), dma(TWO, RING + 1), dma(TWO, TWO), dma(TWO))
+
+    dx_all()
     grad2(hi, lambda k: K2.at[k], done2, lambda k: (R2.at[:, blk(k, BN)], rid("s2") + k))
 
-    y3()
-    d3()
+    def outy_at(core, jj):
+        return OUTY.at[blk(core, TH), blk(jj, BN)]
+
+    yo = Send(lambda jj: (YO.at[TWO * e + jj], outy_at(d, jj), rid("yo") + jj, dev_e), TWO)
+
+    def finish_y(q1b, xb, vb, rxb, yb, isem, osem, wsem):
+        def ins(k, s):
+            cols = blk(k, BN)
+            return (o["YQ1"].at[c_hi, :, cols], q1b.at[s]), (XF.at[:, cols], xb.at[s]), (PV.at[:, cols], vb.at[s])
+
+        def work(k, s):
+            arr = batch(wsem, (o["YRX"].at[:, :, blk(k, BN)], rxb))
+            for j in range(RING):
+                @when(k == j)
+                def _():
+                    y_come(j)
+            move(arr)
+            yb[s] = (xb[s].astype(F32) + (q1b[s] + rxb[0] + rxb[1]) + vb[s, TWO:TWO + 1, :]).astype(BF16)
+
+        def done(k, s):
+            @when(high(k) == d)
+            def _():
+                move(batch(wsem, (yb.at[s], outy_at(d, low(k)))))
+
+            @when(high(k) == e)
+            def _():
+                yo.start(low(k))
+
+        run(RING, ins, lambda k, s: ((yb.at[s], YO.at[k]),), isem, osem, work, done=done)
+
+    pl.run_scoped(finish_y, fl(TWO, TH, BN), bf(TWO, TH, BN), fl(TWO, 8, BN), fl(TWO, TH, BN), bf(TWO, TH, BN), dma(TWO, RING), dma(TWO, 1), dma(1))
+
+    arrived(OUTX.at[blk(e, TH), :], rid("xo"))
+    arrived(BG.at[e], rid("bg"))
     for ii in BOTH:
+        arrived(outy_at(e, ii), rid("yo") + ii)
         for dd in BOTH:
             arrived(OUT1.at[:, f_block(TWO * gn + ii, dd)], rid("k1u") + dd * TWO + ii)
         arrived(OUT1.at[:, f_block(TWO * g + ii, e)], rid("k1d") + ii)
@@ -710,7 +858,7 @@
     assert tuple(counts) == SEMS, counts
 
 
-SEMS = (129, 129)
+SEMS = (143, 143)
 
 
 def solution(mesh):
@@ -722,79 +870,27 @@
     in_specs = (tok_spec, vec_dep, vec_dep, P(("dep", "row"), "col"), P("col"), P(("col", "row"), "dep"), vec_dep, tok_spec)
     out_specs = (tok_spec, tok_spec, P(("part", "dep", "row"), "col"), P(("part", "col")), P(("part", "col", "row"), "dep"), part_dep, part_dep, part_dep)
 
-    def swap(t):
-        return lax.ppermute(t, "dep", [(0, 1), (1, 0)])
-
-    def xor(t, axis, m):
-        return lax.ppermute(t, axis, [(i, i ^ m) for i in range(4)])
-
     def local_step(x_in, ln_scale, ln_shift, w_up, b_up, w_down, b_down, y_grad):
-        d, c = lax.axis_index("dep"), lax.axis_index("col")
+        d = lax.axis_index("dep")
         th, dhalf = x_in.shape[0] // 2, x_in.shape[1]
-        dm, ds_, fb = 2 * dhalf, w_up.shape[0], w_up.shape[1] // 8
-        lo = d == 0
-
-        def merge_last(mine, other):
-            return jnp.where(lo, jnp.concatenate([mine, other], axis=-1), jnp.concatenate([other, mine], axis=-1))
-
-        def tok_half(t, which):
-            return lax.dynamic_slice_in_dim(t, which * th, th, 0)
-
-        xo = merge_last(tok_half(x_in, d), swap(tok_half(x_in, 1 - d)))
-        go = merge_last(tok_half(y_grad, d), swap(tok_half(y_grad, 1 - d)))
-        vecs = jnp.stack([ln_scale, ln_shift, b_down.astype(F32)])
-        vecs = merge_last(vecs, swap(vecs))
-        gamma, beta, bdn = vecs[0], vecs[1], vecs[2]
-        x_float = xo.astype(F32)
-        mean_row = jnp.sum(x_float, axis=1, keepdims=True) / dm
-        var_row = jnp.sum(x_float * x_float, axis=1, keepdims=True) / dm - mean_row * mean_row
-        inv_std = lax.rsqrt(var_row + LN_EPS)
-        x_hat = (x_float - mean_row) * inv_std
-        ao = (x_hat * gamma + beta).astype(BF16)
+        ds_, fb = w_up.shape[0], w_up.shape[1] // 8
+        vec = jnp.stack([ln_scale, ln_shift, b_down.astype(F32)] + [jnp.zeros_like(ln_scale)] * 5)
         b3 = lax.dynamic_index_in_dim(b_up.reshape(4, 2, fb), d, 1, keepdims=False).astype(F32)
         bup = jnp.concatenate([b3[k] for k in (0, 3, 1, 2)]).reshape(1, 4 * fb)
 
-        cfg = (th, dm, ds_, fb)
+        cfg = (th, 2 * dhalf, ds_, fb)
         outs = pl.pallas_call(
             functools.partial(kernel, cfg),
             name="mlp_layer",
             out_shape=buffers(*cfg),
-            in_specs=[pl.BlockSpec(memory_space=pl.ANY)] * 4 + [pl.BlockSpec(memory_space=pltpu.VMEM)],
+            in_specs=[pl.BlockSpec(memory_space=pl.ANY)] * 5 + [pl.BlockSpec(memory_space=pltpu.VMEM)],
             out_specs=[pl.BlockSpec(memory_space=pl.ANY)] * len(NAMES),
-            scratch_shapes=[dma(SEMS[0]), dma(SEMS[1])],
+            scratch_shapes=[dma(SEMS[0]), dma(SEMS[1]), fl(STAGES + 1, 8, dhalf), fl(STAGES, 8, dhalf), fl(3, 8, 4 * fb), fl(2, 8, 4 * fb)],
             compiler_params=pltpu.CompilerParams(collective_id=0, has_side_effects=True, vmem_limit_bytes=62 * 1024 * 1024),
-        )(ao, go, w_up, w_down, bup)
+        )(x_in, y_grad, w_up, w_down, vec, bup)
         o = dict(zip(NAMES, outs))
-
-        def total(s):
-            own = lax.dynamic_index_in_dim(o[s + "Q1"], c // 2, 0, keepdims=False)
-            return own + o[s + "RX"][0] + o[s + "RX"][1]
-
-        def to_out(t):
-            mine = lax.dynamic_slice_in_dim(t, d * dhalf, dhalf, 1)
-            oth = swap(lax.dynamic_slice_in_dim(t, (1 - d) * dhalf, dhalf, 1))
-            return jnp.where(lo, jnp.concatenate([mine, oth], axis=0), jnp.concatenate([oth, mine], axis=0))
-
-        y_out = to_out((x_float + total("Y") + bdn).astype(BF16))
-        norm_grad = total("D")
-        g_float = go.astype(F32)
-        val = norm_grad * gamma
-        m1 = jnp.sum(val, axis=1, keepdims=True) / dm
-        m2 = jnp.sum(val * x_hat, axis=1, keepdims=True) / dm
-        x_grad = to_out((g_float + inv_std * (val - m1 - x_hat * m2)).astype(BF16))
-
-        sums = jnp.stack([jnp.sum(norm_grad * x_hat, axis=0), jnp.sum(norm_grad, axis=0), jnp.sum(g_float, axis=0)])
-        s_m = lax.dynamic_slice_in_dim(sums, d * dhalf, dhalf, 1)
-        sums = s_m + swap(lax.dynamic_slice_in_dim(sums, (1 - d) * dhalf, dhalf, 1))
-        for axis, m in (("row", 1), ("row", 3), ("col", 1), ("col", 3)):
-            sums = sums + xor(sums, axis, m)
-
-        db4 = jnp.sum(o["DB"], axis=0).reshape(4, fb)
-        db = jnp.stack([db4[k] for k in (0, 2, 3, 1)])
-        for m in (1, 3):
-            db = db + xor(db, "row", m)
-        db_o = swap(db)
-        b_up_grad = jnp.where(lo, jnp.stack([db, db_o], axis=1), jnp.stack([db_o, db], axis=1)).reshape(8 * fb)
-        return (y_out, x_grad, o["OUT1"], b_up_grad, o["OUT2"], sums[2], sums[0], sums[1])
+        db = o["BG"][:, 0].reshape(2, 4, fb)
+        b_up_grad = jnp.stack([db[:, k] for k in (0, 2, 3, 1)]).reshape(8 * fb)
+        return (o["OUTY"], o["OUTX"], o["OUT1"], b_up_grad, o["OUT2"], o["SO"][2], o["SO"][0], o["SO"][1])
 
     return jax.shard_map(local_step, mesh=mesh, in_specs=in_specs, out_specs=out_specs, check_vma=False)

time: 759 us -> 773 us (1.018); the launches traced: 749 us -> 772 us
  Pallas kernels: 687 us -> 754 us
  other arithmetic: 28.5 us -> 1.32 us
  starting transfers between devices: 13.5 us -> 0 us
    pallas_call x1, Pallas kernels: 687 us -> 754 us  [local_step(): pl.pallas_call(functools.partial(kernel, cfg), name='mlp_layer', out_shap...]
    reduce_sum x5 -> x0, other arithmetic: 16.7 us -> none  [the longest x1 6.05 us: local_step(): jnp.sum(norm_grad, axis=0)]
    ppermute x13 -> x0, starting transfers between devices: 13.5 us -> none  [the longest x7 7.39 us: swap(): return lax.ppermute(t, 'dep', [(0, 1), (1, 0)])]
  transfers between devices with their start and end apart: 13 -> 0, of which waited for: 5 -> 0; matrix products, arithmetic and copies ran while one was open for 3% -> 0% of each run, Pallas kernels for 0% -> 0%
where the time goes in v3:
time: 773 us; the launch traced here: 772 us
  Pallas kernels  754 us (98%)
  local copies, waits for them, and re-layouts  15.8 us (2%)
    pallas_call x1, Pallas kernels, local_step(): pl.pallas_call(functools.partial(kernel, cfg), name='mlp_layer', out_shap...  754 us

profile of v3, /device:TPU:97, one launch (start us, length us, event | category | flops | bytes accessed | tf_op | source)
XLA Modules:
  0.0 772.1 jit_solution(32136502266436246)
XLA Ops:
  0.6 0.7 reshape.34
  1.4 0.6 pad_maximum_fusion
  2.0 0.7 stack.28
  2.7 1.4 stack.26.vec
  4.1 754.3 %mlp_layer.1 = (bf16[2,4,512,4096]{3,2,1,0:T(8,128)(2,1)}, bf16[2,4,512,4096]{3,2,1,0:T(8,128)(2,1)}, bf16[4096,2048]{1,0:T(8,128)(2,1)}, bf16[2048,4096]{1,0:T(...) custom-call(bf16[512,2048]{1,0:T(8,128)(2,1)} %x_in.1, ...), custom_call_target="tpu_custom_call" | custom-call | tf_op jit(solution)/shard_map/mlp_layer/pallas_call | solution.py:882
  758.4 0.0 copy-start.2
  758.4 1.1 slice_reduce_fusion
  759.6 0.6 copy.24
  760.2 1.6 fusion
  761.7 0.0 copy-start.1
  761.7 3.3 copy.33
  765.1 0.0 copy-done.2
  765.1 1.3 copy.34
  766.4 0.0 copy-done.1
  766.4 0.0 copy-start
  766.4 2.1 copy.35
  768.5 1.6 copy-done
  770.1 2.0 copy.36
  (9 shorter events, 0.1 us)
Async XLA Ops:
  758.4 6.7 copy-start.2
  761.7 4.6 copy-start.1
  766.4 3.7 copy-start

commit v4 on v3

--- a/solution.py
+++ b/solution.py
@@ -17,7 +17,7 @@
 NAMES = ("A", "G", "W1", "W2", "HP", "HQ", "CP", "CQ", "DB",
          "PY", "RY", "YQ1", "YQ2", "YRF", "YRX", "PD", "RD", "DQ1", "DQ2", "DRF", "DRX",
          "S1", "R1", "S2", "R2", "K1", "K2", "OUT1", "OUT2", "XF", "GF", "PV", "YO", "XO", "OUTY", "OUTX", "BG", "SO")
-TWO, RING, STAGES = 2, 4, 5
+TWO, RING, STAGES, MANY = 2, 4, 5, 16
 BOTH, SLOTS = (0, 1), (2,)
 NT = (((1,), (1,)), ((), ()))
 TN = (((0,), (0,)), ((), ()))
@@ -66,8 +66,15 @@
     return pltpu.make_async_copy(src, dst, sem)
 
 
+def parts(src, dst):
+    rows = dst.shape[0]
+    n = rows if rows == TWO and len(dst.shape) > RING - 1 else RING if rows % (8 * RING) == 0 else 1
+    m = rows // n
+    return [(src.at[pl.ds(i * m, m)], dst.at[pl.ds(i * m, m)]) for i in range(n)] if n > 1 else [(src, dst)]
+
+
 def batch(sem, *pairs):
-    return [cp(src, dst, sem.at[i]) for i, (src, dst) in enumerate(pairs)]
+    return [cp(src, dst, sem.at[i]) for i, (src, dst) in enumerate(t for pair in pairs for t in parts(*pair))]
 
 
 def start(copies):
@@ -136,14 +143,24 @@
             def _():
                 start(fetch(nxt, flip(s)))
         if done is not None:
-            wait(back(k, s))
-            done(k, s)
+            @when(k == 0)
+            def _():
+                wait(back(k, s))
+                done(k, s)
+
+            @when(k >= TWO)
+            def _():
+                wait(back(k - 1, flip(s)))
+                done(k - 1, flip(s))
         return 0
 
     lax.fori_loop(0, n, step, 0)
+    last = n - 1
     if done is None:
-        for s in BOTH:
-            wait(back(s, s))
+        wait(back(last - 1, flip(low(last))))
+    wait(back(last, low(last)))
+    if done is not None:
+        done(last, low(last))
 
 
 def kernel(cfg, x_in, g_in, w1, w2, vec, bup, *refs):
@@ -173,11 +190,13 @@
         return ids[key]
 
     for nm in "AG":
-        for w in ("xr0", "xl0", "u", "xr1", "xl1", "fr0", "fl0", "fr1", "fl1"):
+        for w in ("xr1", "xl1", "fr0", "fl0", "fr1", "fl1"):
             name(nm + w)
+        for w in ("xr0", "xl0", "u"):
+            name(nm + w, TWO)
         for t in "01":
             for w in "cLRxy":
-                name(nm + "d" + t + w)
+                name(nm + "d" + t + w, TWO)
     for s in "uv":
         name("w1" + s, TWO * RING)
         name("w2" + s, TWO)
@@ -274,8 +293,11 @@
     Send(lambda j: (g_in.at[blk(e, TH), :], GF.at[:, blk(d, DH)], rid("gf"), dev_e)).start()
     Send(lambda j: (x_in.at[blk(e, TH), :], XF.at[:, blk(d, DH)], rid("xf"), dev_e)).start()
     Send(lambda j: (vec, PV.at[:, blk(d, DH)], rid("pv"), dev_e)).start()
+    OWN_TO = (("xr0", dev_R), ("xl0", dev_L), ("u", dev(u, d)), ("d0c", dev_e))
     send_w1("v", v, pos_v, pos_r)
     send_w1("u", u, pos_u, pos_q)
+    for w, dv in OWN_TO:
+        Send(lambda j, w=w, dv=dv: (g_in.at[blk(d, TH), :], G.at[hp, c, blk(d, TH), blk(d, DH)], rid("G" + w), dv)).start()
 
     RL = min(8 * RING, TH)
 
@@ -285,23 +307,20 @@
         inv_std = lax.rsqrt(var + LN_EPS)
         return inv_std, (x - mean) * inv_std
 
-    def send_own(nm, X):
-        for w, dv in (("u", dev(u, d)), ("xr0", dev_R), ("xl0", dev_L), ("d0c", dev_e)):
-            Send(lambda j, w=w, dv=dv: (ch(X, 0, c, d), ch(X, 0, c, d), rid(nm + w), dv)).start()
 
     def own_part(xb, gb, ab, vb, b2, b3, sems, sems2):
         mine, other = blk(d, DH), blk(e, DH)
         ld = batch(sems, (g_in.at[blk(d, TH), :], gb.at[:, mine]), (x_in.at[blk(d, TH), :], xb.at[:, mine]), (vec, vb.at[:, mine]))
-        wl = batch(sems2, (w2.at[blk(d, FB), :], b3), *[(w1_src(pos, d), b2.at[:, blk(pos, FB)]) for pos in range(RING)])
-        start(ld + wl)
+        start(ld)
         wait(ld)
         got = batch(sems, (GF.at[:, other], gb.at[:, other]), (XF.at[:, other], xb.at[:, other]), (PV.at[:, other], vb.at[:, other]))
-        for t, ref, w in zip(got, (GF, XF, PV), ("gf", "xf", "pv")):
+        for ref, w in ((GF, "gf"), (XF, "xf"), (PV, "pv")):
             arrived(ref.at[:, other], rid(w))
-            t.start()
-        wait(got[:1])
-        move(batch(sems, (gb, ch(G, 0, c, d))))
-        wait(got[1:])
+            if ref is GF:
+                for w, dv in OWN_TO:
+                    Send(lambda j, w=w, dv=dv: (GF.at[:, blk(e, DH)], G.at[hp, c, blk(d, TH), blk(e, DH)], rid("G" + w) + 1, dv)).start()
+        move(got)
+        start(batch(sems2, (gb, ch(G, 0, c, d))))
         keep = batch(sems, (xb.at[:, mine], XF.at[:, mine]), (vb.at[:, mine], PV.at[:, mine]))
         start(keep)
         scale, shift = vb[0:1, :], vb[1:TWO, :]
@@ -313,15 +332,18 @@
 
         lax.fori_loop(0, TH // RL, rows, 0)
         wait(keep)
-        send_own("G", G)
         move(batch(sems, (ab, ch(A, 0, c, d))))
-        send_own("A", A)
+        for w, dv in OWN_TO:
+            Send(lambda j, w=w, dv=dv: (ch(A, 0, c, d), ch(A, 0, c, d), rid("A" + w), dv)).start()
         send_w2("u", u)
         send_w1("u", u, pos_r, pos_v)
-        wait(wl)
-        move(batch(sems2, (b3, w2_part(pos_r, d)), (b2, W1.at[blk(d * RING + r, DS), :])))
-
-    pl.run_scoped(own_part, bf(TH, DM), bf(TH, DM), bf(TH, DM), fl(8, DM), bf(DS, FC), bf(FB, DH), dma(RING), dma(RING + 1))
+        wait(batch(sems2, (gb, ch(G, 0, c, d))))
+        wl = batch(sems, (w2.at[blk(d, FB), :], b3), (w1_src(0, d), b2.at[:, blk(0, FB)]))
+        move(wl)
+        move(batch(sems, *[(w1_src(pos, d), b2.at[:, blk(pos, FB)]) for pos in range(1, RING)]))
+        move(batch(sems, (b3, w2_part(pos_r, d)), (b2, W1.at[blk(d * RING + r, DS), :])))
+
+    pl.run_scoped(own_part, bf(TH, DM), bf(TH, DM), bf(TH, DM), fl(8, DM), bf(DS, FC), bf(FB, DH), dma(MANY), dma(MANY))
     for pos in range(RING):
         Send(lambda j, pos=pos: (w1_src(pos, e), w1_dst(d, r, pos), rid("w1d") + pos, dev_e)).start()
     Send(lambda j: (w2.at[blk(e, FB), :], w2_part(pos_r, d), rid("w2d"), dev_e)).start()
@@ -335,17 +357,24 @@
                           same(ch(X, t, far, d, 0), rid(b + "x"), dev_e), same(ch(X, t, far, d, 1), rid(b + "y"), dev_e)]
         par[nm] = [same(ch(X, 1, c, d), rid(nm + w), dv) for w, dv in (("xr1", dev_R), ("xl1", dev_L), ("d1c", dev_e))]
 
+    def own_in(nm, X, t, col, w, core=d):
+        if nm + w in ("Gxr0", "Gxl0", "Gu", "Gd0c"):
+            for half, i in ((core, 0), (flip(core), 1)):
+                arrived(X.at[ROW[t], col, blk(core, TH), blk(half, DH)], rid(nm + w) + i)
+        else:
+            arrived(ch(X, t, col, core), rid(nm + w))
+
     def pass_on(nm, X, t):
         to_r, to_l, d_l, d_r = fwd[nm, t][:RING]
-        arrived(ch(X, t, L, d), rid(nm + "xr" + str(t)))
+        own_in(nm, X, t, L, "xr" + str(t))
         to_r.start()
-        arrived(ch(X, t, R, d), rid(nm + "xl" + str(t)))
+        own_in(nm, X, t, R, "xl" + str(t))
         to_l.start()
         d_l.start()
         d_r.start()
 
     def from_u(nm, X):
-        arrived(ch(X, 1, c, d), rid(nm + "u"))
+        own_in(nm, X, 1, c, "u")
         for t in par[nm]:
             t.start()
 
@@ -362,7 +391,7 @@
                     for part, z in zip(BOTH, "xy"):
                         arrived(ch(X, t, far, e, part), rid(b + z))
                 else:
-                    arrived(ch(X, t, {"c": c, "L": L, "R": R}[w], e), rid(b + w))
+                    own_in(nm, X, t, {"c": c, "L": L, "R": R}[w], b[1:] + w, e)
 
     def hop(tag, row, device, *positions):
         out = []
@@ -460,7 +489,7 @@
             move(batch(wsem.at[0], *[(dbs.at[b], o["DB"].at[:, blk(block(b * first)[1], FB)]) for b in BOTH]))
 
         pl.run_scoped(body, bf(TWO, T2, DM), bf(TWO, T2, DM), bf(TWO, DM, FB), bf(TWO, FB, DM), fl(T2, FB), fl(T2, FB),
-                      bf(TWO, T2, FB), bf(TWO, T2, FB), fl(TWO, 8, FB), dma(TWO, TWO), dma(TWO, TWO), dma(TWO, TWO))
+                      bf(TWO, T2, FB), bf(TWO, T2, FB), fl(TWO, 8, FB), dma(TWO, MANY), dma(TWO, MANY), dma(TWO, MANY))
 
     five, ten = RING + 1, TWO * RING + TWO
 
@@ -516,7 +545,7 @@
         j = first + (1 - TWO * first) * high(k)
         return blk(low(k) * RING + TWO * pair + j, DS)
 
-    def grad(left, right, left_shape, right_shape, resident, out_shape, outs, done, recv=None):
+    def grad(left, right, left_shape, right_shape, resident, out_shape, outs, done, recv=None, posts=None):
         rows, width = out_shape
 
         def body(lb, rb, acc, ob, nb, isem, osem, wsem):
@@ -541,11 +570,11 @@
                     move(batch(wsem, (ref, nb)))
                     ob[s] = (acc[:] + nb[:]).astype(BF16)
 
-            run(RING, ins, lambda k, s: ((ob.at[s], outs(k)),), isem, osem, work, done=lambda k, s: done(k, ob.at[s], wsem))
+            run(RING, ins, lambda k, s: ((ob.at[s], outs(k)),), isem, osem, work, done=lambda k, s: done(k, ob.at[s], wsem), posts=posts)
 
         extra = out_shape if recv else (8, BN)
         pl.run_scoped(body, bf(*left_shape), bf(*right_shape), fl(*extra), pltpu.VMEM(SLOTS + out_shape, BF16 if recv else F32), fl(*extra),
-                      dma(TWO, 1), dma(TWO, 1), dma(TWO))
+                      dma(TWO, MANY), dma(TWO, MANY), dma(MANY))
 
     PT, PTS = (TWO, RING, T2), (TWO, TWO, TWO, T2)
 
@@ -553,9 +582,9 @@
         grad(lambda k: A.at[:, :, :, dw1_cols(k, pair, first)], None, SLOTS + PT + (DS,), PTS + (F2,), lambda b: (o["CP"], b[1]),
              (DS, F2), outs, done, recv)
 
-    def grad2(pair, outs, done, recv=None):
+    def grad2(pair, outs, done, recv=None, posts=None):
         grad(None, lambda k: G.at[:, :, :, blk(k, BN)], PTS + (FB,), SLOTS + PT + (BN,), lambda b: (o["HP"].at[:, :, :, :, blk(pair, FB)], b[0]),
-             (FB, BN), outs, done, recv)
+             (FB, BN), outs, done, recv, posts)
 
     grad1(hn, hp, lambda k: S1.at[k], lambda k, ob, sem: s1.start(k))
 
@@ -676,11 +705,11 @@
 
         def run_first():
             pl.run_scoped(first, bf(TWO, TWO, TH, F2), bf(TWO, TWO, TH, F2), bf(TWO, TH, F2), bf(TWO, TH, F2), bf(RING, *wshape),
-                          fl(TWO, TWO, TH, BN), fl(TWO, TH, BN), fl(TWO, TH, BN), dma(RING, 1), dma(RING), dma(1))
+                          fl(TWO, TWO, TH, BN), fl(TWO, TH, BN), fl(TWO, TH, BN), dma(RING, RING), dma(MANY), dma(MANY))
 
         def run_second():
             pl.run_scoped(second, bf(TWO, TH, F2), bf(TWO, TH, F2), bf(TWO, *wshape), fl(TWO, TWO, TH, BN), fl(TWO, TWO, HT, BN),
-                          fl(TWO, TWO, TH, BN), dma(TWO), dma(TWO, RING), dma(TWO, 1))
+                          fl(TWO, TWO, TH, BN), dma(MANY), dma(TWO, MANY), dma(TWO, MANY))
 
         def come(j):
             arrived(RR.at[0, :, blk(j, BN)], rid(s + "pr") + j)
@@ -785,32 +814,32 @@
             sums[STAGES, i:i + 1, :] = acc[i, 0:1, blk(d, DH)]
             sums[0, i:i + 1, :] = acc[i, 0:1, blk(e, DH)]
         db[0, 0:1, :] = jnp.sum(dbb[:], axis=0, keepdims=True)
-        cur = sums[STAGES]
-        cur_b = db[0]
-        for k in range(STAGES):
-            if k:
-                sums[k] = cur
-            sum_send[k].start()
-            if k in (1, TWO):
-                db[k - 1] = cur_b
-                bsend[k - 1].start()
-            arrived(sums_in.at[k], rid("sum") + k)
-            cur = cur + sums_in[k]
-            if k in (1, TWO):
-                arrived(db_in.at[k - 1], rid("bf") + k - 1)
-                cur_b = cur_b + db_in[k - 1]
-        sums[STAGES] = cur
-        db[TWO] = cur_b
+        sum_send[0].start()
+
+    def stage(k):
+        arrived(sums_in.at[k], rid("sum") + k)
+        sums[STAGES] += sums_in[k]
+        if k in (1, TWO):
+            arrived(db_in.at[k - 1], rid("bf") + k - 1)
+            db[k] = db[k - 1] + db_in[k - 1]
+        if k < STAGES - 1:
+            sums[k + 1] = sums[STAGES]
+            sum_send[k + 1].start()
+        if k < TWO:
+            bsend[k].start()
+
+    def sums_out(wsem):
+        stage(STAGES - 1)
         move(batch(wsem, (sums.at[STAGES], SO), (db.at[TWO], BG.at[d])))
         bg.start()
 
     def dx_all():
         RB = min(8 * RING, high(TH))
         pl.run_scoped(finish_dx, fl(TWO, RB, DM), fl(TWO, RB, DM), fl(TWO, RB, DM), bf(TWO, RB, DM), bf(TWO, RB, DM), fl(8, DM),
-                      bf(TWO, RB, DM), fl(RING - 1, 8, DM), fl(8, FC), dma(TWO, RING + 1), dma(TWO, TWO), dma(TWO))
+                      bf(TWO, RB, DM), fl(RING - 1, 8, DM), fl(8, FC), dma(TWO, MANY + RING), dma(TWO, MANY), dma(MANY))
 
     dx_all()
-    grad2(hi, lambda k: K2.at[k], done2, lambda k: (R2.at[:, blk(k, BN)], rid("s2") + k))
+    grad2(hi, lambda k: K2.at[k], done2, lambda k: (R2.at[:, blk(k, BN)], rid("s2") + k), {k: functools.partial(stage, k) for k in range(RING)})
 
     def outy_at(core, jj):
         return OUTY.at[blk(core, TH), blk(jj, BN)]
@@ -840,9 +869,10 @@
             def _():
                 yo.start(low(k))
 
+        sums_out(wsem)
         run(RING, ins, lambda k, s: ((yb.at[s], YO.at[k]),), isem, osem, work, done=done)
 
-    pl.run_scoped(finish_y, fl(TWO, TH, BN), bf(TWO, TH, BN), fl(TWO, 8, BN), fl(TWO, TH, BN), bf(TWO, TH, BN), dma(TWO, RING), dma(TWO, 1), dma(1))
+    pl.run_scoped(finish_y, fl(TWO, TH, BN), bf(TWO, TH, BN), fl(TWO, 8, BN), fl(TWO, TH, BN), bf(TWO, TH, BN), dma(TWO, MANY), dma(TWO, MANY), dma(MANY))
 
     arrived(OUTX.at[blk(e, TH), :], rid("xo"))
     arrived(BG.at[e], rid("bg"))
@@ -858,7 +888,7 @@
     assert tuple(counts) == SEMS, counts
 
 
-SEMS = (143, 143)
+SEMS = (169, 147)
 
 
 def solution(mesh):
@@ -885,7 +915,7 @@
             out_shape=buffers(*cfg),
             in_specs=[pl.BlockSpec(memory_space=pl.ANY)] * 5 + [pl.BlockSpec(memory_space=pltpu.VMEM)],
             out_specs=[pl.BlockSpec(memory_space=pl.ANY)] * len(NAMES),
-            scratch_shapes=[dma(SEMS[0]), dma(SEMS[1]), fl(STAGES + 1, 8, dhalf), fl(STAGES, 8, dhalf), fl(3, 8, 4 * fb), fl(2, 8, 4 * fb)],
+            scratch_shapes=[dma(SEMS[1]), dma(SEMS[0]), fl(STAGES + 1, 8, dhalf), fl(STAGES, 8, dhalf), fl(3, 8, 4 * fb), fl(2, 8, 4 * fb)],
             compiler_params=pltpu.CompilerParams(collective_id=0, has_side_effects=True, vmem_limit_bytes=62 * 1024 * 1024),
         )(x_in, y_grad, w_up, w_down, vec, bup)
         o = dict(zip(NAMES, outs))

time: 773 us -> 730 us (0.944)
  Pallas kernels: 754 us -> 711 us
    pallas_call x1, Pallas kernels: 754 us -> 711 us  [local_step(): pl.pallas_call(functools.partial(kernel, cfg), name='mlp_layer', out_shap...]
where the time goes in v4:
time: 730 us; the launch traced here: 729 us
  Pallas kernels  711 us (97%)
  local copies, waits for them, and re-layouts  15.8 us (2%)
    pallas_call x1, Pallas kernels, local_step(): pl.pallas_call(functools.partial(kernel, cfg), name='mlp_layer', out_shap...  711 us

profile of v4, /device:TPU:97, one launch (start us, length us, event | category | flops | bytes accessed | tf_op | source)
XLA Modules:
  0.0 728.8 jit_solution(2870519050982085683)
XLA Ops:
  0.6 0.7 reshape.34
  1.4 0.6 pad_maximum_fusion
  2.0 0.7 stack.28
  2.7 1.4 stack.26.vec
  4.1 711.0 %mlp_layer.1 = (bf16[2,4,512,4096]{3,2,1,0:T(8,128)(2,1)}, bf16[2,4,512,4096]{3,2,1,0:T(8,128)(2,1)}, bf16[4096,2048]{1,0:T(8,128)(2,1)}, bf16[2048,4096]{1,0:T(...) custom-call(bf16[512,2048]{1,0:T(8,128)(2,1)} %x_in.1, ...), custom_call_target="tpu_custom_call" | custom-call | tf_op jit(solution)/shard_map/mlp_layer/pallas_call | solution.py:912
  715.1 0.0 copy-start.2
  715.1 1.1 slice_reduce_fusion
  716.3 0.6 copy.24
  716.9 1.6 fusion
  718.5 0.0 copy-start.1
  718.5 3.3 copy.33
  721.8 0.0 copy-done.2
  721.8 1.3 copy.34
  723.1 0.0 copy-done.1
  723.1 0.0 copy-start
  723.1 2.1 copy.35
  725.2 1.6 copy-done
  726.8 2.0 copy.36
  (9 shorter events, 0.1 us)
Async XLA Ops:
  715.1 6.7 copy-start.2
  718.5 4.6 copy-start.1
  723.1 3.7 copy-start

commit v5 on v4

--- a/solution.py
+++ b/solution.py
@@ -483,7 +483,7 @@
                     @when(k == t * first)
                     def _():
                         wait(weights(t))
-                cd_block(ab[s], gb[s], w1b[b], w2b[b], bup[:, blk(pos, FB)], cbuf, gbuf, hb.at[s], cb.at[s], dbs.at[b], place(k)[TWO])
+                cd_block(ab[s], gb[s], w1b[b], w2b[b], bup[:, f_block(pos, d)].astype(F32), cbuf, gbuf, hb.at[s], cb.at[s], dbs.at[b], place(k)[TWO])
 
             run(n, ins, outs, isem, osem, work, posts={k: functools.partial(fn, load) for k, fn in posts.items()}, late=late)
             move(batch(wsem.at[0], *[(dbs.at[b], o["DB"].at[:, blk(block(b * first)[1], FB)]) for b in BOTH]))
@@ -529,13 +529,24 @@
         other_core(1, "L", "R")
 
     def post13(load):
+        start(early())
         far_in("G", G, 1)
         far_in("A", A, 1)
         other_core(1, "far")
 
+    ahead = []
+
+    def early():
+        rb, sem = ahead
+        return batch(sem, (o["CP"].at[hp], rb.at[hp]),
+                     *[(o["CP"].at[flip(hp), high(t), low(t)], rb.at[flip(hp), high(t), low(t)]) for t in (c, R)])
+
+    def rest():
+        rb, sem = ahead
+        return batch(sem.at[pl.ds(MANY, MANY)], *[(o["CP"].at[flip(hp), high(t), low(t)], rb.at[flip(hp), high(t), low(t)]) for t in (L, far)])
+
     posts1 = {0: post0, TWO: post2, RING - 1: lambda load: other_core(1, "c"), RING: lambda load: load(1),
               five: lambda load: pass_on("G", G, 1), ten - 1: post9, ten + RING - 1: post13}
-    hidden(ten + RING + TWO, place1, block1, need1, five, posts1, (1, RING - 1, RING, ten, ten + RING))
 
     S1, R1, S2, R2, K1, K2, OUT1, OUT2 = [o[t] for t in ("S1", "R1", "S2", "R2", "K1", "K2", "OUT1", "OUT2")]
     s1 = Send(lambda j: (S1.at[j], R1.at[j], rid("s1") + j, dev(v, d)), RING)
@@ -545,12 +556,15 @@
         j = first + (1 - TWO * first) * high(k)
         return blk(low(k) * RING + TWO * pair + j, DS)
 
-    def grad(left, right, left_shape, right_shape, resident, out_shape, outs, done, recv=None, posts=None):
+    def grad(left, right, left_shape, right_shape, resident, out_shape, outs, done, recv=None, posts=None, mid=None, pre=None):
         rows, width = out_shape
 
-        def body(lb, rb, acc, ob, nb, isem, osem, wsem):
-            stay = batch(wsem, resident((lb, rb)))
-            start(stay)
+        def body(acc, ob, nb, isem, osem, wsem, lb, rb):
+            if pre is not None:
+                stay = early() + rest()
+            else:
+                stay = batch(wsem, resident((lb, rb)))
+                start(stay)
 
             def ins(k, s):
                 return (left(k), lb.at[s]) if right is None else (right(k), rb.at[s]),
@@ -565,6 +579,8 @@
                     ob[s] = val
                 else:
                     acc[:] = val
+                    if mid:
+                        when(k == RING - 1)(mid)
                     ref, rsid = recv(k)
                     arrived(ref, rsid)
                     move(batch(wsem, (ref, nb)))
@@ -573,20 +589,29 @@
             run(RING, ins, lambda k, s: ((ob.at[s], outs(k)),), isem, osem, work, done=lambda k, s: done(k, ob.at[s], wsem), posts=posts)
 
         extra = out_shape if recv else (8, BN)
-        pl.run_scoped(body, bf(*left_shape), bf(*right_shape), fl(*extra), pltpu.VMEM(SLOTS + out_shape, BF16 if recv else F32), fl(*extra),
-                      dma(TWO, MANY), dma(TWO, MANY), dma(MANY))
+        kinds = [fl(*extra), pltpu.VMEM(SLOTS + out_shape, BF16 if recv else F32), fl(*extra), dma(TWO, MANY), dma(TWO, MANY), dma(MANY)]
+        if pre is not None:
+            pl.run_scoped(lambda *bufs: body(*bufs, pre), *kinds, bf(*left_shape))
+        else:
+            pl.run_scoped(body, *kinds, bf(*left_shape), bf(*right_shape))
 
     PT, PTS = (TWO, RING, T2), (TWO, TWO, TWO, T2)
 
-    def grad1(pair, first, outs, done, recv=None):
+    def grad1(pair, first, outs, done, recv=None, pre=None):
         grad(lambda k: A.at[:, :, :, dw1_cols(k, pair, first)], None, SLOTS + PT + (DS,), PTS + (F2,), lambda b: (o["CP"], b[1]),
-             (DS, F2), outs, done, recv)
-
-    def grad2(pair, outs, done, recv=None, posts=None):
+             (DS, F2), outs, done, recv, pre=pre)
+
+    def grad2(pair, outs, done, recv=None, posts=None, mid=None):
         grad(None, lambda k: G.at[:, :, :, blk(k, BN)], PTS + (FB,), SLOTS + PT + (BN,), lambda b: (o["HP"].at[:, :, :, :, blk(pair, FB)], b[0]),
-             (FB, BN), outs, done, recv, posts)
-
-    grad1(hn, hp, lambda k: S1.at[k], lambda k, ob, sem: s1.start(k))
+             (FB, BN), outs, done, recv, posts, mid)
+
+    def phase1(rb, sem):
+        ahead.extend((rb, sem))
+        hidden(ten + RING + TWO, place1, block1, need1, five, posts1, (1, RING - 1, RING, ten, ten + RING))
+        start(rest())
+        grad1(hn, hp, lambda k: S1.at[k], lambda k, ob, sem: s1.start(k), pre=rb)
+
+    pl.run_scoped(phase1, bf(*PTS, F2), dma(TWO * MANY))
 
     def block2(k):
         b = k // RING
@@ -603,8 +628,6 @@
             arrived(W2.at[blk(pos_q, FB), q0], rid("f2u"))
 
     hidden(TWO * RING, lambda k: (hp, k % RING, k >= 0), block2, need2, RING, {TWO: lambda load: load(1)}, ())
-
-    LAG = 2
 
     def region(s, nt, XP, XQ, PX, RX):
         Q1, Q2, RF, RR = [o[s + t] for t in ("Q1", "Q2", "RF", "RX")]
@@ -620,22 +643,21 @@
         def wsrc(j):
             return W1.at[blk(j, BN), :] if nt else W2.at[:, blk(j, BN)]
 
-        def wdot(p_ref, q_ref, wref, shape):
-            total = 0.0
+        def wdot(out, p_ref, q_ref, wref):
             for ref, half in ((p_ref, g), (q_ref, gn)):
                 x, sel = ref[:].reshape(-1, F2), blk(half, F2)
                 if nt:
-                    total += lax.dot_general(x, wref[:, sel], NT, preferred_element_type=F32)
+                    val = lax.dot_general(x, wref[:, sel], NT, preferred_element_type=F32)
                 else:
-                    total += jnp.dot(x, wref[sel, :], preferred_element_type=F32)
-            return total.reshape(shape)
-
-        def first(lop, loq, lfp, lfq, wb, ob, ab, qb, wsem, lsem, osem):
+                    val = jnp.dot(x, wref[sel, :], preferred_element_type=F32)
+                val = val.reshape(out.shape)
+                out[:] = val if ref is p_ref else out[:] + val
+
+        def first(lop, loq, lfp, lfq, wb, ob, ab, qb, wsem, lsem, osem, asem):
+            def wcp(j):
+                return batch(wsem.at[low(j)], (wsrc(j), wb.at[low(j)]))
+
             lds = batch(lsem, (XP.at[hp, :, :, other], lop), (XQ.at[:, :, other], loq), (XP.at[hp, :, c_lo, mine], lfp), (XQ.at[:, c_lo, mine], lfq))
-
-            def wcp(j):
-                return batch(wsem.at[j % RING], (wsrc(j), wb.at[j % RING]))
-
             start(wcp(0) + lds)
             wait(lds)
 
@@ -649,33 +671,35 @@
                     @when(j < RING - 1)
                     def _():
                         start(wcp(j + 1))
-                    ob[:] = wdot(lop, loq, wb.at[j % RING], (TWO, TWO, TH, BN))
+                    wdot(ob, lop, loq, wb.at[low(j)])
                     start(o1)
 
-                @when(j >= LAG)
+                @when(j >= 1)
                 def _():
-                    k = j - LAG
+                    k = j - 1
                     arrived(RX.at[:, :, :, blk(k, BN)], rid(s + "p") + k)
-                    add = batch(lsem, (RX.at[:, c_lo, :, blk(k, BN)], ab))
-                    start(add)
-                    qb[:] = wdot(lfp, lfq, wb.at[k % RING], (TWO, TH, BN))
-                    wait(add)
-                    qb[:] += ab[:]
+                    start(batch(asem, (RX.at[:, c_lo, :, blk(k, BN)], ab)))
 
                 @when(j < RING)
                 def _():
                     wait(o1)
                     ex.start(j)
 
-                @when(j >= LAG)
+                @when(j >= 1)
                 def _():
-                    k = j - LAG
+                    k = j - 1
+                    wait(batch(asem, (RX.at[:, c_lo, :, blk(k, BN)], ab)))
+                    qb[:] += ab[:]
                     move(batch(lsem, (qb, Q1.at[:, :, blk(k, BN)])))
                     far_r.start(k)
                     far_l.start(k)
+
+                @when(j < RING)
+                def _():
+                    wdot(qb, lfp, lfq, wb.at[low(j)])
                 return 0
 
-            lax.fori_loop(0, RING + LAG, step, 0)
+            lax.fori_loop(0, RING + 1, step, 0)
 
         def second(lp, lq, wb, ab, fb, ob, lsem, isem, osem):
             lds = batch(lsem, (XP.at[hp, :, flip(c_lo), mine], lp), (XQ.at[:, flip(c_lo), mine], lq))
@@ -693,7 +717,8 @@
                 return (wsrc(k), wb.at[sl]), (RX.at[:, flip(c_lo), :, blk(k, BN)], ab.at[sl]), (RF.at[:, :, blk(k, BN)], fb.at[sl])
 
             def work(k, sl):
-                ob[sl] = wdot(lp, lq, wb.at[sl], (TWO, TH, BN)) + ab[sl]
+                wdot(ob.at[sl], lp, lq, wb.at[sl])
+                ob[sl] += ab[sl]
                 for col, part in ((R, 0), (L, 1)):
                     ob[sl, high(col), part * HT:(part + 1) * HT, :] += fb[sl, high(col)]
 
@@ -704,8 +729,8 @@
             run(RING, ins, lambda k, sl: ((ob.at[sl], Q2.at[:, :, blk(k, BN)]),), isem, osem, work, done=done)
 
         def run_first():
-            pl.run_scoped(first, bf(TWO, TWO, TH, F2), bf(TWO, TWO, TH, F2), bf(TWO, TH, F2), bf(TWO, TH, F2), bf(RING, *wshape),
-                          fl(TWO, TWO, TH, BN), fl(TWO, TH, BN), fl(TWO, TH, BN), dma(RING, RING), dma(MANY), dma(MANY))
+            pl.run_scoped(first, bf(TWO, TWO, TH, F2), bf(TWO, TWO, TH, F2), bf(TWO, TH, F2), bf(TWO, TH, F2), bf(TWO, *wshape),
+                          fl(TWO, TWO, TH, BN), fl(TWO, TH, BN), fl(TWO, TH, BN), dma(TWO, RING), dma(MANY), dma(MANY), dma(MANY))
 
         def run_second():
             pl.run_scoped(second, bf(TWO, TH, F2), bf(TWO, TH, F2), bf(TWO, *wshape), fl(TWO, TWO, TH, BN), fl(TWO, TWO, HT, BN),
@@ -839,40 +864,47 @@
                       bf(TWO, RB, DM), fl(RING - 1, 8, DM), fl(8, FC), dma(TWO, MANY + RING), dma(TWO, MANY), dma(MANY))
 
     dx_all()
-    grad2(hi, lambda k: K2.at[k], done2, lambda k: (R2.at[:, blk(k, BN)], rid("s2") + k), {k: functools.partial(stage, k) for k in range(RING)})
 
     def outy_at(core, jj):
         return OUTY.at[blk(core, TH), blk(jj, BN)]
 
     yo = Send(lambda jj: (YO.at[TWO * e + jj], outy_at(d, jj), rid("yo") + jj, dev_e), TWO)
 
-    def finish_y(q1b, xb, vb, rxb, yb, isem, osem, wsem):
-        def ins(k, s):
+    def last_part(q1b, xb, vb, rxb, yb, sem, sem2):
+        def finish_y(k):
             cols = blk(k, BN)
-            return (o["YQ1"].at[c_hi, :, cols], q1b.at[s]), (XF.at[:, cols], xb.at[s]), (PV.at[:, cols], vb.at[s])
-
-        def work(k, s):
-            arr = batch(wsem, (o["YRX"].at[:, :, blk(k, BN)], rxb))
-            for j in range(RING):
-                @when(k == j)
-                def _():
-                    y_come(j)
-            move(arr)
-            yb[s] = (xb[s].astype(F32) + (q1b[s] + rxb[0] + rxb[1]) + vb[s, TWO:TWO + 1, :]).astype(BF16)
-
-        def done(k, s):
-            @when(high(k) == d)
+            here = batch(sem, (o["YQ1"].at[c_hi, :, cols], q1b), (XF.at[:, cols], xb), (PV.at[:, cols], vb))
+            start(here)
+            y_come(k)
+            move(batch(sem2, (o["YRX"].at[:, :, cols], rxb)))
+            wait(here)
+            yb[:] = (xb[:].astype(F32) + (q1b[:] + rxb[0] + rxb[1]) + vb[TWO:TWO + 1, :]).astype(BF16)
+
+            @when(d == high(k))
             def _():
-                move(batch(wsem, (yb.at[s], outy_at(d, low(k)))))
-
-            @when(high(k) == e)
+                move(batch(sem, (yb, outy_at(high(k), low(k)))))
+
+            @when(e == high(k))
             def _():
+                move(batch(sem, (yb, YO.at[k])))
                 yo.start(low(k))
 
-        sums_out(wsem)
-        run(RING, ins, lambda k, s: ((yb.at[s], YO.at[k]),), isem, osem, work, done=done)
-
-    pl.run_scoped(finish_y, fl(TWO, TH, BN), bf(TWO, TH, BN), fl(TWO, 8, BN), fl(TWO, TH, BN), bf(TWO, TH, BN), dma(TWO, MANY), dma(TWO, MANY), dma(MANY))
+        def third():
+            stage(TWO)
+            finish_y(0)
+            stage(RING - 1)
+            finish_y(1)
+            finish_y(TWO)
+
+        def mid():
+            sums_out(sem)
+            finish_y(RING - 1)
+
+        posts = {k: functools.partial(stage, k) for k in BOTH}
+        posts[TWO] = third
+        grad2(hi, lambda k: K2.at[k], done2, lambda k: (R2.at[:, blk(k, BN)], rid("s2") + k), posts, mid)
+
+    pl.run_scoped(last_part, fl(TH, BN), bf(TH, BN), fl(8, BN), fl(TWO, TH, BN), bf(TH, BN), dma(MANY), dma(MANY))
 
     arrived(OUTX.at[blk(e, TH), :], rid("xo"))
     arrived(BG.at[e], rid("bg"))
@@ -901,12 +933,9 @@
     out_specs = (tok_spec, tok_spec, P(("part", "dep", "row"), "col"), P(("part", "col")), P(("part", "col", "row"), "dep"), part_dep, part_dep, part_dep)
 
     def local_step(x_in, ln_scale, ln_shift, w_up, b_up, w_down, b_down, y_grad):
-        d = lax.axis_index("dep")
         th, dhalf = x_in.shape[0] // 2, x_in.shape[1]
         ds_, fb = w_up.shape[0], w_up.shape[1] // 8
         vec = jnp.stack([ln_scale, ln_shift, b_down.astype(F32)] + [jnp.zeros_like(ln_scale)] * 5)
-        b3 = lax.dynamic_index_in_dim(b_up.reshape(4, 2, fb), d, 1, keepdims=False).astype(F32)
-        bup = jnp.concatenate([b3[k] for k in (0, 3, 1, 2)]).reshape(1, 4 * fb)
 
         cfg = (th, 2 * dhalf, ds_, fb)
         outs = pl.pallas_call(
@@ -917,7 +946,7 @@
             out_specs=[pl.BlockSpec(memory_space=pl.ANY)] * len(NAMES),
             scratch_shapes=[dma(SEMS[1]), dma(SEMS[0]), fl(STAGES + 1, 8, dhalf), fl(STAGES, 8, dhalf), fl(3, 8, 4 * fb), fl(2, 8, 4 * fb)],
             compiler_params=pltpu.CompilerParams(collective_id=0, has_side_effects=True, vmem_limit_bytes=62 * 1024 * 1024),
-        )(x_in, y_grad, w_up, w_down, vec, bup)
+        )(x_in, y_grad, w_up, w_down, vec, b_up.reshape(1, 8 * fb))
         o = dict(zip(NAMES, outs))
         db = o["BG"][:, 0].reshape(2, 4, fb)
         b_up_grad = jnp.stack([db[:, k] for k in (0, 2, 3, 1)]).reshape(8 * fb)

time: 730 us -> 742 us (1.016)
  Pallas kernels: 711 us -> 722 us
    pallas_call x1, Pallas kernels: 711 us -> 722 us  [local_step(): pl.pallas_call(functools.partial(kernel, cfg), name='mlp_layer', out_shap...]
where the time goes in v5:
time: 742 us; the launch traced here: 740 us
  Pallas kernels  722 us (97%)
  local copies, waits for them, and re-layouts  16.4 us (2%)
    pallas_call x1, Pallas kernels, local_step(): pl.pallas_call(functools.partial(kernel, cfg), name='mlp_layer', out_shap...  722 us

profile of v5, /device:TPU:97, one launch (start us, length us, event | category | flops | bytes accessed | tf_op | source)
XLA Modules:
  0.0 740.2 jit_solution(17118723242948307640)
XLA Ops:
  0.6 0.7 stack.28
  1.3 1.3 reshape.22.bup
  2.6 1.4 stack.26.vec
  4.1 722.4 %mlp_layer.1 = (bf16[2,4,512,4096]{3,2,1,0:T(8,128)(2,1)}, bf16[2,4,512,4096]{3,2,1,0:T(8,128)(2,1)}, bf16[4096,2048]{1,0:T(8,128)(2,1)}, bf16[2048,4096]{1,0:T(...) custom-call(bf16[512,2048]{1,0:T(8,128)(2,1)} %x_in.1, ...), custom_call_target="tpu_custom_call" | custom-call | tf_op jit(solution)/shard_map/mlp_layer/pallas_call | solution.py:941
  726.5 0.0 copy-start.2
  726.5 1.1 slice_reduce_fusion
  727.7 0.6 copy.24
  728.3 1.6 fusion
  729.9 0.0 copy-start.1
  729.9 3.3 copy.33
  733.2 0.0 copy-done.2
  733.2 1.3 copy.34
  734.5 0.0 copy-done.1
  734.5 0.0 copy-start
  734.5 2.1 copy.35
  736.6 1.6 copy-done
  738.2 2.0 copy.36
  (7 shorter events, 0.1 us)
Async XLA Ops:
  726.5 6.7 copy-start.2
  729.9 4.6 copy-start.1
  734.5 3.7 copy-start

commit v6 on v5

--- a/solution.py
+++ b/solution.py
@@ -18,6 +18,7 @@
          "PY", "RY", "YQ1", "YQ2", "YRF", "YRX", "PD", "RD", "DQ1", "DQ2", "DRF", "DRX",
          "S1", "R1", "S2", "R2", "K1", "K2", "OUT1", "OUT2", "XF", "GF", "PV", "YO", "XO", "OUTY", "OUTX", "BG", "SO")
 TWO, RING, STAGES, MANY = 2, 4, 5, 16
+LAG = 2
 BOTH, SLOTS = (0, 1), (2,)
 NT = (((1,), (1,)), ((), ()))
 TN = (((0,), (0,)), ((), ()))
@@ -655,7 +656,7 @@
 
         def first(lop, loq, lfp, lfq, wb, ob, ab, qb, wsem, lsem, osem, asem):
             def wcp(j):
-                return batch(wsem.at[low(j)], (wsrc(j), wb.at[low(j)]))
+                return batch(wsem.at[j % RING], (wsrc(j), wb.at[j % RING]))
 
             lds = batch(lsem, (XP.at[hp, :, :, other], lop), (XQ.at[:, :, other], loq), (XP.at[hp, :, c_lo, mine], lfp), (XQ.at[:, c_lo, mine], lfq))
             start(wcp(0) + lds)
@@ -671,35 +672,34 @@
                     @when(j < RING - 1)
                     def _():
                         start(wcp(j + 1))
-                    wdot(ob, lop, loq, wb.at[low(j)])
+                    wdot(ob, lop, loq, wb.at[j % RING])
                     start(o1)
 
-                @when(j >= 1)
+                @when(j >= LAG)
                 def _():
-                    k = j - 1
+                    k = j - LAG
                     arrived(RX.at[:, :, :, blk(k, BN)], rid(s + "p") + k)
-                    start(batch(asem, (RX.at[:, c_lo, :, blk(k, BN)], ab)))
+                    add = batch(asem, (RX.at[:, c_lo, :, blk(k, BN)], ab))
+                    start(add)
+                    wdot(qb, lfp, lfq, wb.at[k % RING])
+                    wait(add)
+                    qb[:] += ab[:]
+                    start(batch(lsem, (qb, Q1.at[:, :, blk(k, BN)])))
 
                 @when(j < RING)
                 def _():
                     wait(o1)
                     ex.start(j)
 
-                @when(j >= 1)
+                @when(j >= LAG)
                 def _():
-                    k = j - 1
-                    wait(batch(asem, (RX.at[:, c_lo, :, blk(k, BN)], ab)))
-                    qb[:] += ab[:]
-                    move(batch(lsem, (qb, Q1.at[:, :, blk(k, BN)])))
+                    k = j - LAG
+                    wait(batch(lsem, (qb, Q1.at[:, :, blk(k, BN)])))
                     far_r.start(k)
                     far_l.start(k)
-
-                @when(j < RING)
-                def _():
-                    wdot(qb, lfp, lfq, wb.at[low(j)])
                 return 0
 
-            lax.fori_loop(0, RING + 1, step, 0)
+            lax.fori_loop(0, RING + LAG, step, 0)
 
         def second(lp, lq, wb, ab, fb, ob, lsem, isem, osem):
             lds = batch(lsem, (XP.at[hp, :, flip(c_lo), mine], lp), (XQ.at[:, flip(c_lo), mine], lq))
@@ -729,8 +729,8 @@
             run(RING, ins, lambda k, sl: ((ob.at[sl], Q2.at[:, :, blk(k, BN)]),), isem, osem, work, done=done)
 
         def run_first():
-            pl.run_scoped(first, bf(TWO, TWO, TH, F2), bf(TWO, TWO, TH, F2), bf(TWO, TH, F2), bf(TWO, TH, F2), bf(TWO, *wshape),
-                          fl(TWO, TWO, TH, BN), fl(TWO, TH, BN), fl(TWO, TH, BN), dma(TWO, RING), dma(MANY), dma(MANY), dma(MANY))
+            pl.run_scoped(first, bf(TWO, TWO, TH, F2), bf(TWO, TWO, TH, F2), bf(TWO, TH, F2), bf(TWO, TH, F2), bf(RING, *wshape),
+                          fl(TWO, TWO, TH, BN), fl(TWO, TH, BN), fl(TWO, TH, BN), dma(RING, RING), dma(MANY), dma(MANY), dma(MANY))
 
         def run_second():
             pl.run_scoped(second, bf(TWO, TH, F2), bf(TWO, TH, F2), bf(TWO, *wshape), fl(TWO, TWO, TH, BN), fl(TWO, TWO, HT, BN),

time: 742 us -> 726 us (0.978)
  Pallas kernels: 722 us -> 707 us
    pallas_call x1, Pallas kernels: 722 us -> 707 us  [local_step(): pl.pallas_call(functools.partial(kernel, cfg), name='mlp_layer', out_shap...]
where the time goes in v6:
time: 726 us; the launch traced here: 724 us
  Pallas kernels  707 us (97%)
  local copies, waits for them, and re-layouts  16.4 us (2%)
    pallas_call x1, Pallas kernels, local_step(): pl.pallas_call(functools.partial(kernel, cfg), name='mlp_layer', out_shap...  707 us

profile of v6, /device:TPU:97, one launch (start us, length us, event | category | flops | bytes accessed | tf_op | source)
XLA Modules:
  0.0 724.4 jit_solution(13484040606776075756)
XLA Ops:
  0.6 0.7 stack.28
  1.3 1.3 reshape.22.bup
  2.6 1.4 stack.26.vec
  4.1 706.6 %mlp_layer.1 = (bf16[2,4,512,4096]{3,2,1,0:T(8,128)(2,1)}, bf16[2,4,512,4096]{3,2,1,0:T(8,128)(2,1)}, bf16[4096,2048]{1,0:T(8,128)(2,1)}, bf16[2048,4096]{1,0:T(...) custom-call(bf16[512,2048]{1,0:T(8,128)(2,1)} %x_in.1, ...), custom_call_target="tpu_custom_call" | custom-call | tf_op jit(solution)/shard_map/mlp_layer/pallas_call | solution.py:941
  710.7 0.0 copy-start.2
  710.7 1.1 slice_reduce_fusion
  711.9 0.6 copy.24
  712.5 1.6 fusion
  714.1 0.0 copy-start.1
  714.1 3.3 copy.33
  717.4 0.0 copy-done.2
  717.4 1.3 copy.34
  718.7 0.0 copy-done.1
  718.7 0.0 copy-start
  718.7 2.1 copy.35
  720.9 1.6 copy-done
  722.4 2.0 copy.36
  (7 shorter events, 0.1 us)
Async XLA Ops:
  710.7 6.7 copy-start.2
  714.1 4.6 copy-start.1
  718.7 3.7 copy-start

commit v7 on v6

--- a/solution.py
+++ b/solution.py
@@ -45,9 +45,9 @@
         "S1": ((RING, DS, F2), F32), "S2": ((FB, DM), F32),
         "K1": ((RING, DS, F2), BF16), "K2": ((RING, FB, high(DM) // TWO), BF16),
         "OUT1": ((DS, 8 * FB), BF16), "OUT2": ((F2, high(DM)), BF16),
-        "XF": ((TH, DM), BF16), "GF": ((TH, DM), BF16), "PV": ((8, DM), F32), "YO": ((RING, TH, high(DM) // TWO), BF16),
+        "XF": ((TH, DM), BF16), "GF": ((TH, DM), BF16), "PV": ((RING - 1, 1, DM), F32), "YO": ((RING, TH, high(DM) // TWO), BF16),
         "XO": ((TH, high(DM)), BF16), "OUTY": ((T2, high(DM)), BF16), "OUTX": ((T2, high(DM)), BF16),
-        "BG": (SLOTS + (8, FC), F32), "SO": ((8, high(DM)), F32),
+        "BG": (SLOTS + (RING, 8, FB), F32), "SO": ((8, high(DM)), F32),
     }
     for new, old in (("G", "A"), ("CP", "HP"), ("CQ", "HQ"), ("R1", "S1"), ("R2", "S2")):
         shapes[new] = shapes[old]
@@ -164,7 +164,7 @@
         done(last, low(last))
 
 
-def kernel(cfg, x_in, g_in, w1, w2, vec, bup, *refs):
+def kernel(cfg, x_in, g_in, w1, w2, gam, bet, bdn, bup, *refs):
     TH, DM, DS, FB = cfg
     o = dict(zip(NAMES, refs[:len(NAMES)]))
     ssem, rsem, sums, sums_in, db, db_in = refs[len(NAMES):]
@@ -203,7 +203,8 @@
         name("w2" + s, TWO)
         name("f1" + s, RING)
         name("f2" + s)
-    for s in ("w2d", "xf", "gf", "pv", "xo", "bg"):
+    name("pv", RING - 1)
+    for s in ("w2d", "xf", "gf", "xo", "bg"):
         name(s)
     name("yo", TWO)
     name("bf", TWO)
@@ -293,7 +294,9 @@
     XF, GF, PV = o["XF"], o["GF"], o["PV"]
     Send(lambda j: (g_in.at[blk(e, TH), :], GF.at[:, blk(d, DH)], rid("gf"), dev_e)).start()
     Send(lambda j: (x_in.at[blk(e, TH), :], XF.at[:, blk(d, DH)], rid("xf"), dev_e)).start()
-    Send(lambda j: (vec, PV.at[:, blk(d, DH)], rid("pv"), dev_e)).start()
+    VEC = (gam, bet, bdn)
+    for i, ref in enumerate(VEC):
+        Send(lambda j, i=i, ref=ref: (ref, PV.at[i, :, blk(d, DH)], rid("pv") + i, dev_e)).start()
     OWN_TO = (("xr0", dev_R), ("xl0", dev_L), ("u", dev(u, d)), ("d0c", dev_e))
     send_w1("v", v, pos_v, pos_r)
     send_w1("u", u, pos_u, pos_q)
@@ -311,20 +314,24 @@
 
     def own_part(xb, gb, ab, vb, b2, b3, sems, sems2):
         mine, other = blk(d, DH), blk(e, DH)
-        ld = batch(sems, (g_in.at[blk(d, TH), :], gb.at[:, mine]), (x_in.at[blk(d, TH), :], xb.at[:, mine]), (vec, vb.at[:, mine]))
+        ld = batch(sems, (g_in.at[blk(d, TH), :], gb.at[:, mine]), (x_in.at[blk(d, TH), :], xb.at[:, mine]),
+                   *[(ref, vb.at[i, :, mine]) for i, ref in enumerate(VEC)])
         start(ld)
         wait(ld)
-        got = batch(sems, (GF.at[:, other], gb.at[:, other]), (XF.at[:, other], xb.at[:, other]), (PV.at[:, other], vb.at[:, other]))
-        for ref, w in ((GF, "gf"), (XF, "xf"), (PV, "pv")):
+        got = batch(sems, (GF.at[:, other], gb.at[:, other]), (XF.at[:, other], xb.at[:, other]),
+                    *[(PV.at[i, :, other], vb.at[i, :, other]) for i in range(len(VEC))])
+        for i in range(len(VEC)):
+            arrived(PV.at[i, :, other], rid("pv") + i)
+        for ref, w in ((GF, "gf"), (XF, "xf")):
             arrived(ref.at[:, other], rid(w))
             if ref is GF:
                 for w, dv in OWN_TO:
                     Send(lambda j, w=w, dv=dv: (GF.at[:, blk(e, DH)], G.at[hp, c, blk(d, TH), blk(e, DH)], rid("G" + w) + 1, dv)).start()
         move(got)
         start(batch(sems2, (gb, ch(G, 0, c, d))))
-        keep = batch(sems, (xb.at[:, mine], XF.at[:, mine]), (vb.at[:, mine], PV.at[:, mine]))
+        keep = batch(sems, (xb.at[:, mine], XF.at[:, mine]), *[(vb.at[i, :, mine], PV.at[i, :, mine]) for i in range(len(VEC))])
         start(keep)
-        scale, shift = vb[0:1, :], vb[1:TWO, :]
+        scale, shift = vb[0], vb[1]
 
         def rows(m, _):
             sl = blk(m, RL)
@@ -344,7 +351,7 @@
         move(batch(sems, *[(w1_src(pos, d), b2.at[:, blk(pos, FB)]) for pos in range(1, RING)]))
         move(batch(sems, (b3, w2_part(pos_r, d)), (b2, W1.at[blk(d * RING + r, DS), :])))
 
-    pl.run_scoped(own_part, bf(TH, DM), bf(TH, DM), bf(TH, DM), fl(8, DM), bf(DS, FC), bf(FB, DH), dma(MANY), dma(MANY))
+    pl.run_scoped(own_part, bf(TH, DM), bf(TH, DM), bf(TH, DM), fl(RING - 1, 1, DM), bf(DS, FC), bf(FB, DH), dma(MANY), dma(MANY))
     for pos in range(RING):
         Send(lambda j, pos=pos: (w1_src(pos, e), w1_dst(d, r, pos), rid("w1d") + pos, dev_e)).start()
     Send(lambda j: (w2.at[blk(e, FB), :], w2_part(pos_r, d), rid("w2d"), dev_e)).start()
@@ -484,7 +491,7 @@
                     @when(k == t * first)
                     def _():
                         wait(weights(t))
-                cd_block(ab[s], gb[s], w1b[b], w2b[b], bup[:, f_block(pos, d)].astype(F32), cbuf, gbuf, hb.at[s], cb.at[s], dbs.at[b], place(k)[TWO])
+                cd_block(ab[s], gb[s], w1b[b], w2b[b], bup[:, f_block(pos, d)], cbuf, gbuf, hb.at[s], cb.at[s], dbs.at[b], place(k)[TWO])
 
             run(n, ins, outs, isem, osem, work, posts={k: functools.partial(fn, load) for k, fn in posts.items()}, late=late)
             move(batch(wsem.at[0], *[(dbs.at[b], o["DB"].at[:, blk(block(b * first)[1], FB)]) for b in BOTH]))
@@ -580,11 +587,17 @@
                     ob[s] = val
                 else:
                     acc[:] = val
+                    ref, rsid = recv(k)
                     if mid:
-                        when(k == RING - 1)(mid)
-                    ref, rsid = recv(k)
-                    arrived(ref, rsid)
-                    move(batch(wsem, (ref, nb)))
+                        for t, fn in enumerate(mid):
+                            if t:
+                                arrived(ref, rsid)
+                                start(batch(wsem, (ref, nb)))
+                            when(k == RING - 1)(fn)
+                        wait(batch(wsem, (ref, nb)))
+                    else:
+                        arrived(ref, rsid)
+                        move(batch(wsem, (ref, nb)))
                     ob[s] = (acc[:] + nb[:]).astype(BF16)
 
             run(RING, ins, lambda k, s: ((ob.at[s], outs(k)),), isem, osem, work, done=lambda k, s: done(k, ob.at[s], wsem), posts=posts)
@@ -823,7 +836,7 @@
             da = q1b[s] + rlb[s] + rrb[s]
             inv_std, xhat = stats(xb[s].astype(F32))
             gr = gb[s].astype(F32)
-            val = da * vb[0:1, :]
+            val = da * vb[0]
             m1 = jnp.sum(val, axis=1, keepdims=True) / DM
             m2 = jnp.sum(val * xhat, axis=1, keepdims=True) / DM
             xob[s] = (gr + inv_std * (val - m1 - xhat * m2)).astype(BF16)
@@ -855,12 +868,12 @@
 
     def sums_out(wsem):
         stage(STAGES - 1)
-        move(batch(wsem, (sums.at[STAGES], SO), (db.at[TWO], BG.at[d])))
+        move(batch(wsem, (sums.at[STAGES], SO), *[(db.at[TWO, :, blk(pos, FB)], BG.at[d, row]) for pos, row in enumerate((0, RING - 1, 1, TWO))]))
         bg.start()
 
     def dx_all():
         RB = min(8 * RING, high(TH))
-        pl.run_scoped(finish_dx, fl(TWO, RB, DM), fl(TWO, RB, DM), fl(TWO, RB, DM), bf(TWO, RB, DM), bf(TWO, RB, DM), fl(8, DM),
+        pl.run_scoped(finish_dx, fl(TWO, RB, DM), fl(TWO, RB, DM), fl(TWO, RB, DM), bf(TWO, RB, DM), bf(TWO, RB, DM), fl(RING - 1, 1, DM),
                       bf(TWO, RB, DM), fl(RING - 1, 8, DM), fl(8, FC), dma(TWO, MANY + RING), dma(TWO, MANY), dma(MANY))
 
     dx_all()
@@ -871,14 +884,18 @@
     yo = Send(lambda jj: (YO.at[TWO * e + jj], outy_at(d, jj), rid("yo") + jj, dev_e), TWO)
 
     def last_part(q1b, xb, vb, rxb, yb, sem, sem2):
+        def fetch_y(k):
+            cols = blk(k, BN)
+            start(batch(sem, (o["YQ1"].at[c_hi, :, cols], q1b), (XF.at[:, cols], xb), (PV.at[TWO, :, cols], vb)))
+            y_come(k)
+            start(batch(sem2, (o["YRX"].at[:, :, cols], rxb)))
+
         def finish_y(k):
             cols = blk(k, BN)
-            here = batch(sem, (o["YQ1"].at[c_hi, :, cols], q1b), (XF.at[:, cols], xb), (PV.at[:, cols], vb))
-            start(here)
-            y_come(k)
-            move(batch(sem2, (o["YRX"].at[:, :, cols], rxb)))
+            here = batch(sem, (o["YQ1"].at[c_hi, :, cols], q1b), (XF.at[:, cols], xb), (PV.at[TWO, :, cols], vb))
             wait(here)
-            yb[:] = (xb[:].astype(F32) + (q1b[:] + rxb[0] + rxb[1]) + vb[TWO:TWO + 1, :]).astype(BF16)
+            wait(batch(sem2, (o["YRX"].at[:, :, cols], rxb)))
+            yb[:] = (xb[:].astype(F32) + (q1b[:] + rxb[0] + rxb[1]) + vb[:]).astype(BF16)
 
             @when(d == high(k))
             def _():
@@ -891,20 +908,23 @@
 
         def third():
             stage(TWO)
-            finish_y(0)
-            stage(RING - 1)
-            finish_y(1)
-            finish_y(TWO)
-
-        def mid():
+            for k in range(RING - 1):
+                fetch_y(k)
+                finish_y(k)
+                if k == 0:
+                    stage(RING - 1)
+
+        def before():
             sums_out(sem)
-            finish_y(RING - 1)
+            fetch_y(RING - 1)
+
+        mid = (before, lambda: finish_y(RING - 1))
 
         posts = {k: functools.partial(stage, k) for k in BOTH}
         posts[TWO] = third
         grad2(hi, lambda k: K2.at[k], done2, lambda k: (R2.at[:, blk(k, BN)], rid("s2") + k), posts, mid)
 
-    pl.run_scoped(last_part, fl(TH, BN), bf(TH, BN), fl(8, BN), fl(TWO, TH, BN), bf(TH, BN), dma(MANY), dma(MANY))
+    pl.run_scoped(last_part, fl(TH, BN), bf(TH, BN), fl(1, BN), fl(TWO, TH, BN), bf(TH, BN), dma(MANY), dma(MANY))
 
     arrived(OUTX.at[blk(e, TH), :], rid("xo"))
     arrived(BG.at[e], rid("bg"))
@@ -920,7 +940,7 @@
     assert tuple(counts) == SEMS, counts
 
 
-SEMS = (169, 147)
+SEMS = (171, 149)
 
 
 def solution(mesh):
@@ -935,21 +955,20 @@
     def local_step(x_in, ln_scale, ln_shift, w_up, b_up, w_down, b_down, y_grad):
         th, dhalf = x_in.shape[0] // 2, x_in.shape[1]
         ds_, fb = w_up.shape[0], w_up.shape[1] // 8
-        vec = jnp.stack([ln_scale, ln_shift, b_down.astype(F32)] + [jnp.zeros_like(ln_scale)] * 5)
+        rows = [t.astype(F32).reshape(1, -1) for t in (ln_scale, ln_shift, b_down, b_up)]
 
         cfg = (th, 2 * dhalf, ds_, fb)
         outs = pl.pallas_call(
             functools.partial(kernel, cfg),
             name="mlp_layer",
             out_shape=buffers(*cfg),
-            in_specs=[pl.BlockSpec(memory_space=pl.ANY)] * 5 + [pl.BlockSpec(memory_space=pltpu.VMEM)],
+            in_specs=[pl.BlockSpec(memory_space=pl.ANY)] * 7 + [pl.BlockSpec(memory_space=pltpu.VMEM)],
             out_specs=[pl.BlockSpec(memory_space=pl.ANY)] * len(NAMES),
             scratch_shapes=[dma(SEMS[1]), dma(SEMS[0]), fl(STAGES + 1, 8, dhalf), fl(STAGES, 8, dhalf), fl(3, 8, 4 * fb), fl(2, 8, 4 * fb)],
             compiler_params=pltpu.CompilerParams(collective_id=0, has_side_effects=True, vmem_limit_bytes=62 * 1024 * 1024),
-        )(x_in, y_grad, w_up, w_down, vec, b_up.reshape(1, 8 * fb))
+        )(x_in, y_grad, w_up, w_down, *rows)
         o = dict(zip(NAMES, outs))
-        db = o["BG"][:, 0].reshape(2, 4, fb)
-        b_up_grad = jnp.stack([db[:, k] for k in (0, 2, 3, 1)]).reshape(8 * fb)
+        b_up_grad = o["BG"][:, :, 0].transpose(1, 0, 2).reshape(8 * fb)
         return (o["OUTY"], o["OUTX"], o["OUT1"], b_up_grad, o["OUT2"], o["SO"][2], o["SO"][0], o["SO"][1])
 
     return jax.shard_map(local_step, mesh=mesh, in_specs=in_specs, out_specs=out_specs, check_vma=False)

time: 726 us -> 724 us (level)
  no operation moved by 1% of the time
where the time goes in v7:
time: 724 us; the launch traced here: 723 us
  Pallas kernels  706 us (98%)
  local copies, waits for them, and re-layouts  13.6 us (2%)
    pallas_call x1, Pallas kernels, local_step(): pl.pallas_call(functools.partial(kernel, cfg), name='mlp_layer', out_shap...  706 us

profile of v7, /device:TPU:97, one launch (start us, length us, event | category | flops | bytes accessed | tf_op | source)
XLA Modules:
  0.0 723.2 jit_solution(16346456671991929294)
XLA Ops:
  0.6 1.3 reshape.42
  1.9 1.3 reshape.44
  3.2 706.3 %mlp_layer.1 = (bf16[2,4,512,4096]{3,2,1,0:T(8,128)(2,1)}, bf16[2,4,512,4096]{3,2,1,0:T(8,128)(2,1)}, bf16[4096,2048]{1,0:T(8,128)(2,1)}, bf16[2048,4096]{1,0:T(...) custom-call(bf16[512,2048]{1,0:T(8,128)(2,1)} %x_in.1, ...), custom_call_target="tpu_custom_call" | custom-call | tf_op jit(solution)/shard_map/mlp_layer/pallas_call | solution.py:961
  709.6 0.0 copy-start.2
  709.6 1.1 slice.12
  710.7 0.6 copy.18
  711.3 1.6 fusion
  712.8 0.0 copy-start.1
  712.8 3.3 copy.27
  716.1 0.0 copy-done.2
  716.2 1.3 copy.28
  717.5 0.0 copy-done.1
  717.5 0.0 copy-start
  717.5 2.1 copy.29
  719.6 1.6 copy-done
  721.2 2.0 copy.30
  (2 shorter events, 0.0 us)
Async XLA Ops:
  709.6 6.6 copy-start.2
  712.8 4.6 copy-start.1
  717.5 3.7 copy-start

commit v8 on v7

--- a/solution.py
+++ b/solution.py
@@ -344,7 +344,7 @@
         for w, dv in OWN_TO:
             Send(lambda j, w=w, dv=dv: (ch(A, 0, c, d), ch(A, 0, c, d), rid("A" + w), dv)).start()
         send_w2("u", u)
-        send_w1("u", u, pos_r, pos_v)
+        send_w1("u", u, pos_r)
         wait(batch(sems2, (gb, ch(G, 0, c, d))))
         wl = batch(sems, (w2.at[blk(d, FB), :], b3), (w1_src(0, d), b2.at[:, blk(0, FB)]))
         move(wl)
@@ -409,7 +409,8 @@
 
     f1v = hop("f1v", u, dev(v, d), pos_v, pos_r)
     f1u = hop("f1u", v, dev(u, d), pos_r, pos_v)
-    q0, q1 = pl.ds(0, BN), pl.ds(BN, DM - BN)
+    cut = BN - high(FB)
+    q0, q1 = pl.ds(0, cut), pl.ds(cut, DM - cut)
     f2u = same(W2.at[blk(pos_v, FB), q0], rid("f2u"), dev(u, d))
     f2v = same(W2.at[blk(pos_u, FB), q1], rid("f2v"), dev(v, d))
 
@@ -431,8 +432,9 @@
     pass_on("G", G, 0)
     for pos in (pos_r, pos_v):
         w1_in("v", v, pos)
-    for t in f1u:
-        t.all()
+    f1u[0].all()
+    send_w1("u", u, pos_v)
+    f1u[1].all()
     other_core(0, "c")
     arrived(w2_part(pos_r, e), rid("w2d"))
     w1_rest(pos_r, "f1v")

time: 724 us -> 724 us (level)
  no operation moved by 1% of the time
where the time goes in v8:
time: 724 us; the launch traced here: 722 us
  Pallas kernels  705 us (97%)
  local copies, waits for them, and re-layouts  13.6 us (2%)
    pallas_call x1, Pallas kernels, local_step(): pl.pallas_call(functools.partial(kernel, cfg), name='mlp_layer', out_shap...  705 us

profile of v8, /device:TPU:97, one launch (start us, length us, event | category | flops | bytes accessed | tf_op | source)
XLA Modules:
  0.0 722.4 jit_solution(15672831040712954797)
XLA Ops:
  0.6 1.3 reshape.42
  1.9 1.3 reshape.44
  3.2 705.5 %mlp_layer.1 = (bf16[2,4,512,4096]{3,2,1,0:T(8,128)(2,1)}, bf16[2,4,512,4096]{3,2,1,0:T(8,128)(2,1)}, bf16[4096,2048]{1,0:T(8,128)(2,1)}, bf16[2048,4096]{1,0:T(...) custom-call(bf16[512,2048]{1,0:T(8,128)(2,1)} %x_in.1, ...), custom_call_target="tpu_custom_call" | custom-call | tf_op jit(solution)/shard_map/mlp_layer/pallas_call | solution.py:963
  708.7 0.0 copy-start.2
  708.7 1.1 slice.12
  709.8 0.6 copy.18
  710.4 1.6 fusion
  712.0 0.0 copy-start.1
  712.0 3.3 copy.27
  715.3 0.0 copy-done.2
  715.3 1.3 copy.28
  716.6 0.0 copy-done.1
  716.6 0.0 copy-start
  716.6 2.1 copy.29
  718.8 1.6 copy-done
  720.3 2.0 copy.30
  (2 shorter events, 0.0 us)
Async XLA Ops:
  708.7 6.6 copy-start.2
  712.0 4.6 copy-start.1
  716.6 3.7 copy-start
